TPU v7x, 128 devices: a whole 4x4x4 slice. The times are simulated.
128 devices in a mesh: dep: 8 (over x_lo, z), res: 16 (over y, x_hi, core).
Axes of the slice: x: 4 (x_hi: 2, x_lo: 2; x = x_hi * 2 + x_lo), y: 4, z: 4, core: 2. Of those that a mesh axis runs over, the one named last changes fastest.
Arguments:
- homolog_representation: bfloat16 [512, 512, 256], P('dep', 'res'), may hold values from -6 to 6
- presence_indicator: int32 [512, 512], P('dep', 'res'), may hold values from 0 to 1, as said below
- pairwise_delta_sensitivity: bfloat16 [512, 512, 128], P('res', 'dep'), may hold values from -192 to 192
- upstream_sensitivity: bfloat16 [512, 512, 256], P('dep', 'res'), may hold values from -6 to 6
- asking_matrix: bfloat16 [256, 256], replicated, may hold values from -8.25 to 8.25
- lookup_matrix: bfloat16 [256, 256], replicated, may hold values from -0.25 to 0.25
- content_matrix: bfloat16 [256, 256], replicated, may hold values from -0.375 to 0.375
- sigmoid_matrix: bfloat16 [256, 256], replicated, may hold values from -0.375 to 0.375
- emission_matrix: bfloat16 [256, 256], replicated, may hold values from -0.375 to 0.375
- lhs_projection_matrix: bfloat16 [256, 32], replicated, may hold values from -0.375 to 0.375
- rhs_projection_matrix: bfloat16 [256, 32], replicated, may hold values from -0.375 to 0.375
- pairwise_projection_matrix: bfloat16 [1024, 128], replicated, may hold values from -0.1875 to 0.1875
Outputs:
- alignment_gradient: bfloat16 [512, 512, 256], P('dep', 'res')
- intermediate_sensitivity: bfloat16 [512, 512, 256], P('dep', 'res')
Inputs may be any that keep to these rules, and one draw needn't show every extreme that they name: `presence_indicator`: every residue of sequence 0 is present.
All inputs are finite; a program needn't handle non-finite values.
Results may differ from a plain program's by a relative error of at most 0.018.
The roundings to bfloat16 on the way count: a program that leaves them out, or rounds other values in their place, can miss the bound.
Values may be sent and summed in bfloat16 or wider, within the bound.
A program may use at most 320 MiB of HBM per device.

v0:
```python
import math

import jax
import jax.numpy as jnp
from jax import lax
from jax.sharding import Mesh
from jax.sharding import PartitionSpec as P

FEATURE_DEPTH = 256
H = 8
DH = 32
PROJ_WIDTH = 32
CZ = 128
DEP = ("dep_0", "dep_1")


epsilon = 1e-05
big_penalty = 1000000000.0


def sent_to_all(array, axis):
    length = lax.axis_size(axis)
    return lax.all_to_all(
        jnp.broadcast_to(array[None], (length, *array.shape)), axis, 0, 0, tiled=True
    )


def taken_together(array, axis):
    return sent_to_all(array, axis).astype(jnp.float32).sum(axis=0)


def joined_along(pieces, dim):
    pieces = jnp.moveaxis(pieces, 0, dim)
    lengths = pieces.shape
    return pieces.reshape(*lengths[:dim], lengths[dim] * lengths[dim + 1], *lengths[dim + 2 :])


def all_blocks(array, axes, turns):
    pieces = array
    for k in turns:
        pieces = lax.all_gather(pieces, axes[k])
    done = turns[::-1]
    back = [done.index(k) for k in range(len(axes))]
    pieces = pieces.transpose(*back, *range(len(axes), pieces.ndim))
    return pieces.reshape(-1, *array.shape)


def gathered_by_axis(array, axes, turns, dim):
    return joined_along(all_blocks(array, axes, turns), dim)


def normalize(values):
    center = values - jnp.mean(values, -1, keepdims=True)
    inverse_scale = lax.rsqrt(jnp.mean(center * center, -1, keepdims=True) + epsilon)
    return (center * inverse_scale, inverse_scale)


def attend_column(column, livecol, parameter_collection):
    asking_matrix, lookup_matrix, content_matrix, sigmoid_matrix, emission_matrix = (
        parameter_collection
    )
    standardized_tensor, unused_inv = normalize(column.astype(jnp.float32))
    normed_b = standardized_tensor.astype(jnp.bfloat16)
    extent_along = column.shape[0]
    query = (
        (jnp.dot(normed_b, asking_matrix, preferred_element_type=jnp.float32) * DH ** (-0.5))
        .astype(jnp.bfloat16)
        .reshape(extent_along, H, DH)
    )
    keyed = (
        jnp.dot(normed_b, lookup_matrix, preferred_element_type=jnp.float32)
        .astype(jnp.bfloat16)
        .reshape(extent_along, H, DH)
    )
    content_projected = (
        jnp.dot(normed_b, content_matrix, preferred_element_type=jnp.float32)
        .astype(jnp.bfloat16)
        .reshape(extent_along, H, DH)
    )
    gating = jax.nn.sigmoid(jnp.dot(normed_b, sigmoid_matrix, preferred_element_type=jnp.float32))
    scores = jnp.einsum("shd,thd->hst", query, keyed, preferred_element_type=jnp.float32)
    scores = scores + ((livecol - 1.0) * big_penalty)[None, None, :]
    peak_score = jnp.max(scores, -1, keepdims=True)
    powers = jnp.exp(scores - peak_score)
    attention_probabilities = (powers / jnp.sum(powers, -1, keepdims=True)).astype(jnp.bfloat16)
    blended_tensor = jnp.einsum(
        "wvx,xwj->vwj",
        attention_probabilities,
        content_projected,
        preferred_element_type=jnp.float32,
    ).reshape(extent_along, FEATURE_DEPTH)
    gated = (gating * blended_tensor).astype(jnp.bfloat16)
    update = jnp.dot(gated, emission_matrix, preferred_element_type=jnp.float32)
    return (column.astype(jnp.float32) + update).astype(jnp.bfloat16)


def vertical_attention_whole(block_cols, live_cols, parameter_collection):

    def per_column(column_pair):
        return attend_column(column_pair[0], column_pair[1], parameter_collection)

    results = lax.map(per_column, (jnp.swapaxes(block_cols, 0, 1), jnp.swapaxes(live_cols, 0, 1)))
    return jnp.swapaxes(results, 0, 1)


def project_pair(rows, recip_rows, pairwise_projection_matrix, count_i, count_j):
    projected = lax.dot_general(
        rows.reshape(-1, CZ),
        pairwise_projection_matrix,
        (((1,), (1,)), ((), ())),
        preferred_element_type=jnp.float32,
    )
    return (
        projected.reshape(count_i, count_j, PROJ_WIDTH, PROJ_WIDTH) * recip_rows[:, :, None, None]
    ).astype(jnp.bfloat16)


def on_device(
    homolog_representation,
    presence_indicator,
    pairwise_delta_sensitivity,
    upstream_sensitivity,
    asking_matrix,
    lookup_matrix,
    content_matrix,
    sigmoid_matrix,
    emission_matrix,
    lhs_projection_matrix,
    rhs_projection_matrix,
    pairwise_projection_matrix,
):
    parameter_collection = (
        asking_matrix,
        lookup_matrix,
        content_matrix,
        sigmoid_matrix,
        emission_matrix,
    )
    homologs_each_shard, positions_each_shard, feature_depth = homolog_representation.shape
    total_res = positions_each_shard * lax.axis_size("res")
    live_homologs = presence_indicator.astype(jnp.float32)
    live_b = live_homologs.astype(jnp.bfloat16)
    columns, live_cols_b = (
        lax.all_to_all(homolog_representation, DEP, split_axis=1, concat_axis=0, tiled=True),
        lax.all_to_all(live_b, DEP, split_axis=1, concat_axis=0, tiled=True),
    )
    live_cols = live_cols_b.astype(jnp.float32)
    after_cols, pullback_function = jax.vjp(
        lambda entry: vertical_attention_whole(entry, live_cols, parameter_collection), columns
    )
    refreshed_result = lax.all_to_all(after_cols, DEP, split_axis=0, concat_axis=1, tiled=True)
    standardized_tensor, inverse_scale = normalize(refreshed_result.astype(jnp.float32))
    flattened_tensor = standardized_tensor.astype(jnp.bfloat16).reshape(-1, feature_depth)
    left = (
        jnp.dot(
            flattened_tensor, lhs_projection_matrix, preferred_element_type=jnp.float32
        ).reshape(homologs_each_shard, positions_each_shard, PROJ_WIDTH)
        * live_homologs[..., None]
    ).astype(jnp.bfloat16)
    right = (
        jnp.dot(
            flattened_tensor, rhs_projection_matrix, preferred_element_type=jnp.float32
        ).reshape(homologs_each_shard, positions_each_shard, PROJ_WIDTH)
        * live_homologs[..., None]
    ).astype(jnp.bfloat16)
    right_flat, live_all_b = (
        lax.all_gather(
            right.reshape(homologs_each_shard, positions_each_shard * PROJ_WIDTH),
            "res",
            axis=1,
            tiled=True,
        ),
        lax.all_gather(live_b, "res", axis=1, tiled=True),
    )
    right_all = right_flat.reshape(homologs_each_shard, total_res, PROJ_WIDTH)
    partial_counts = jnp.dot(
        live_homologs.T, live_all_b.astype(jnp.float32), precision=lax.Precision.HIGHEST
    )
    counts = taken_together(partial_counts.astype(jnp.bfloat16), DEP).astype(jnp.float32)
    recip = 1.0 / (0.001 + counts)
    pair_whole = gathered_by_axis(pairwise_delta_sensitivity, DEP, (0, 1), 1)
    stride = math.gcd(total_res, 64)

    def left_block(block_index, state):
        position = block_index * stride
        cot_rows = lax.dynamic_slice_in_dim(pair_whole, position, stride, 1)
        recip_rows = lax.dynamic_slice_in_dim(recip, position, stride, 1)
        outer_cot = project_pair(
            cot_rows, recip_rows, pairwise_projection_matrix, positions_each_shard, stride
        )
        right_rows_now = lax.dynamic_slice_in_dim(right_all, position, stride, 1)
        return state + jnp.einsum(
            "ijce,sje->sic", outer_cot, right_rows_now, preferred_element_type=jnp.float32
        )

    left_grad = lax.fori_loop(
        0,
        total_res // stride,
        left_block,
        jnp.zeros((homologs_each_shard, positions_each_shard, PROJ_WIDTH), jnp.float32),
    )
    left_all = lax.all_gather(
        left.reshape(homologs_each_shard, positions_each_shard * PROJ_WIDTH),
        "res",
        axis=1,
        tiled=True,
    ).reshape(homologs_each_shard, total_res, PROJ_WIDTH)
    pair_cols = lax.all_to_all(pair_whole, "res", split_axis=1, concat_axis=0, tiled=True)
    recip_cols = recip.T

    def right_block(block_index, state):
        position = block_index * stride
        cot_rows = lax.dynamic_slice_in_dim(pair_cols, position, stride, 0)
        recip_rows = lax.dynamic_slice_in_dim(recip_cols, position, stride, 0)
        outer_cot = project_pair(
            cot_rows, recip_rows, pairwise_projection_matrix, stride, positions_each_shard
        )
        left_rows_now = lax.dynamic_slice_in_dim(left_all, position, stride, 1)
        return state + jnp.einsum(
            "ijce,sic->sje", outer_cot, left_rows_now, preferred_element_type=jnp.float32
        )

    right_grad = lax.fori_loop(
        0,
        total_res // stride,
        right_block,
        jnp.zeros((homologs_each_shard, positions_each_shard, PROJ_WIDTH), jnp.float32),
    )
    left_b = (left_grad * live_homologs[..., None]).astype(jnp.bfloat16).reshape(-1, PROJ_WIDTH)
    rhs_projected_tensor = (
        (right_grad * live_homologs[..., None]).astype(jnp.bfloat16).reshape(-1, PROJ_WIDTH)
    )
    tensor_contraction = (((1,), (1,)), ((), ()))
    layernorm_sensitivity = lax.dot_general(
        left_b, lhs_projection_matrix, tensor_contraction, preferred_element_type=jnp.float32
    )
    layernorm_sensitivity = (
        layernorm_sensitivity
        + lax.dot_general(
            rhs_projected_tensor,
            rhs_projection_matrix,
            tensor_contraction,
            preferred_element_type=jnp.float32,
        )
    ).reshape(homologs_each_shard, positions_each_shard, feature_depth)
    first_mean = jnp.mean(layernorm_sensitivity, -1, keepdims=True)
    second_mean = jnp.mean(layernorm_sensitivity * standardized_tensor, -1, keepdims=True)
    intermediate_sensitivity = (
        inverse_scale * (layernorm_sensitivity - first_mean - standardized_tensor * second_mean)
        + upstream_sensitivity.astype(jnp.float32)
    ).astype(jnp.bfloat16)
    gradient_columns = lax.all_to_all(
        intermediate_sensitivity, DEP, split_axis=1, concat_axis=0, tiled=True
    )
    alignment_columns = pullback_function(gradient_columns)[0]
    alignment_gradient = lax.all_to_all(
        alignment_columns, DEP, split_axis=0, concat_axis=1, tiled=True
    )
    return (alignment_gradient, intermediate_sensitivity)


def solution(mesh):
    finer = Mesh(mesh.devices.reshape(2, 4, mesh.shape["res"]), ("dep_0", "dep_1", "res"))
    in_specs = (
        P(DEP, "res", None),
        P(DEP, "res"),
        P("res", DEP, None),
        P(DEP, "res", None),
        P(),
        P(),
        P(),
        P(),
        P(),
        P(),
        P(),
        P(),
    )
    out_specs = (P(DEP, "res", None), P(DEP, "res", None))
    return jax.shard_map(
        on_device, mesh=finer, in_specs=in_specs, out_specs=out_specs, check_vma=False
    )
```

profile of v0, /device:TPU:0, one launch (start us, length us, event | category | flops | bytes accessed | tf_op | source)
XLA Modules:
  0.0 650.4 jit_solution(17822961926403856372)
XLA Ops:
  25.8 21.6 %all-to-all-done = bf16[64,32,256]{2,0,1:T(8,128)(2,1)S(1)} async-done(((bf16[64,32,256]{2,0,1:T(8,128)(2,1)}), bf16[64,32,256]{2,0,1:T(8,128)(2,1)S(1)}, u32[]{:S(2)}, u32[]{:S(2)}) %all-to-all-start) | async-done | bytes 1048608 | tf_op jit(solution)/shard_map/all_to_all | solution.py:144
  47.6 113.7 %while.84 = (s32[]{:T(128)}, bf16[4,512,256]{2,1,0:T(8,128)(2,1)}, f32[4,512,256]{2,1,0:T(8,128)}, f32[4,512,1]{1,2,0:T(1,128)}, f32[4,512,1]{1,2,0:T(1,128)}, /...) while((s32[]{:T(128)}, bf16[4,512,256]{2,1,0:T(8,128)(2,1)}, ...), condition=%wide.region_6.7_spmd, body=%wide.region_0.6_spmd.sunk | while | flops 640416256 | bytes 79293168 | solution.py:102
  169.2 13.4 %all-to-all-done.2 = bf16[512,4,256]{2,1,0:T(4,128)(2,1)S(1)} async-done(((bf16[512,4,256]{2,1,0:T(4,128)(2,1)}), bf16[512,4,256]{2,1,0:T(4,128)(2,1)S(1)}, u32[]{:S(2)}, u32[]{:S(2)}) %all-to-all-start.2) | async-done | bytes 1048608 | tf_op jit(solution)/shard_map/all_to_all | solution.py:151
  193.6 25.0 %all_gather.26 = bf16[64,512]{0,1:T(8,128)(2,1)S(1)} all-gather(bf16[64,32]{0,1:T(8,128)(2,1)} %copy-done.21), channel_id=1, replica_groups=mesh['dep_0'=2,'dep_1'=4,'res'=16] {'res'}, dimensions={1}, use_global_device_ids=true | all-gather | bytes 69632 | tf_op jit(solution)/shard_map/all_gather | solution.py:173
  224.4 9.7 %all-to-all-done.3 = bf16[8,32,512]{2,1,0:T(8,128)(2,1)} async-done(((bf16[8,32,512]{2,1,0:T(8,128)(2,1)}), bf16[8,32,512]{2,1,0:T(8,128)(2,1)}, u32[]{:S(2)}, u32[]{:S(2)}) %all-to-all-start.3) | async-done | bytes 262176 | tf_op jit(solution)/shard_map/all_to_all | solution.py:23
  264.7 72.5 %while.86 = (s32[]{:T(128)}, f32[64,32,32]{0,2,1:T(8,128)}, bf16[64,512,32]{0,2,1:T(8,128)(2,1)}, bf16[32,512,128]{2,1,0:T(8,128)(2,1)}, bf16[1024,128]{1,0:T(8,...) while((s32[]{:T(128)}, f32[64,32,32]{0,2,1:T(8,128)}, ...), condition=%wide.region_11.12_spmd.clone, body=%wide.region_10.11_spmd.clone.sunk | while | flops 809631744 | bytes 2908329 | solution.py:196
  312.2 6.9 %fusion.249 = f32[64,32,32]{0,2,1:T(8,128)} fusion(f32[32,64]{1,0:T(8,128)S(1)} %constant_dynamic-slice_fusion.23, bf16[64,64,32]{1,0,2:T(8,128)(2,1)S(1)} %copy.327, f32[64,32,32]{0,2,1:T(8,128)} %get-tuple-element.2138, bf16[32,512,128]{2,1,0:T(8,128)(2,1)} %get-tuple-element.2150, s32[]{:T(128)S(6)} %select_n.22, ...), kind=kOutput, calls=%fused_computation.124.clone.1 | convolution fusion | flops 809631744 | bytes 1843205 | tf_op jit(solution)/shard_map/while/body/eval_jaxpr/ijce,sje->sic/dot_general | solution.py:192
  345.5 73.1 %while.87 = (s32[]{:T(128)}, f32[64,32,32]{0,2,1:T(8,128)}, bf16[64,512,32]{0,2,1:T(8,128)(2,1)}, bf16[512,32,128]{2,0,1:T(8,128)(2,1)}, bf16[1024,128]{1,0:T(8,...) while((s32[]{:T(128)}, f32[64,32,32]{0,2,1:T(8,128)}, ...), condition=%wide.region_13.14_spmd.clone, body=%wide.region_12.13_spmd.clone.sunk | while | flops 809631744 | bytes 2908329 | solution.py:223
  356.9 6.6 %fusion.253 = f32[64,32,32]{0,2,1:T(8,128)} fusion(bf16[32,32,128,1]{2,1,0,3:T(8,128)(2,1)} %bitcast.499, f32[64,32]{0,1:T(8,128)S(1)} %constant_dynamic-slice_fusion.25, bf16[64,64,32]{1,0,2:T(8,128)(2,1)S(1)} %copy.328, f32[64,32,32]{0,2,1:T(8,128)} %get-tuple-element.2108, bf16[512,32,128]{2,0,1:T(8,128)(2,1)} %get-tuple-element.2120, ...), kind=kOutput, calls=%fused_computation.136.clone.1 | convolution fusion | flops 809631744 | bytes 1843205 | tf_op jit(solution)/shard_map/while/body/eval_jaxpr/ijce,sic->sje/dot_general | solution.py:219
  375.2 6.6 %fusion.253 = f32[64,32,32]{0,2,1:T(8,128)} fusion(bf16[32,32,128,1]{2,1,0,3:T(8,128)(2,1)} %bitcast.499, f32[64,32]{0,1:T(8,128)S(1)} %constant_dynamic-slice_fusion.25, bf16[64,64,32]{1,0,2:T(8,128)(2,1)S(1)} %copy.328, f32[64,32,32]{0,2,1:T(8,128)} %get-tuple-element.2108, bf16[512,32,128]{2,0,1:T(8,128)(2,1)} %get-tuple-element.2120, ...), kind=kOutput, calls=%fused_computation.136.clone.1 | convolution fusion | flops 809631744 | bytes 1843205 | tf_op jit(solution)/shard_map/while/body/eval_jaxpr/ijce,sic->sje/dot_general | solution.py:219
  384.3 6.6 %fusion.253 = f32[64,32,32]{0,2,1:T(8,128)} fusion(bf16[32,32,128,1]{2,1,0,3:T(8,128)(2,1)} %bitcast.499, f32[64,32]{0,1:T(8,128)S(1)} %constant_dynamic-slice_fusion.25, bf16[64,64,32]{1,0,2:T(8,128)(2,1)S(1)} %copy.328, f32[64,32,32]{0,2,1:T(8,128)} %get-tuple-element.2108, bf16[512,32,128]{2,0,1:T(8,128)(2,1)} %get-tuple-element.2120, ...), kind=kOutput, calls=%fused_computation.136.clone.1 | convolution fusion | flops 809631744 | bytes 1843205 | tf_op jit(solution)/shard_map/while/body/eval_jaxpr/ijce,sic->sje/dot_general | solution.py:219
  393.5 6.6 %fusion.253 = f32[64,32,32]{0,2,1:T(8,128)} fusion(bf16[32,32,128,1]{2,1,0,3:T(8,128)(2,1)} %bitcast.499, f32[64,32]{0,1:T(8,128)S(1)} %constant_dynamic-slice_fusion.25, bf16[64,64,32]{1,0,2:T(8,128)(2,1)S(1)} %copy.328, f32[64,32,32]{0,2,1:T(8,128)} %get-tuple-element.2108, bf16[512,32,128]{2,0,1:T(8,128)(2,1)} %get-tuple-element.2120, ...), kind=kOutput, calls=%fused_computation.136.clone.1 | convolution fusion | flops 809631744 | bytes 1843205 | tf_op jit(solution)/shard_map/while/body/eval_jaxpr/ijce,sic->sje/dot_general | solution.py:219
  411.8 6.6 %fusion.253 = f32[64,32,32]{0,2,1:T(8,128)} fusion(bf16[32,32,128,1]{2,1,0,3:T(8,128)(2,1)} %bitcast.499, f32[64,32]{0,1:T(8,128)S(1)} %constant_dynamic-slice_fusion.25, bf16[64,64,32]{1,0,2:T(8,128)(2,1)S(1)} %copy.328, f32[64,32,32]{0,2,1:T(8,128)} %get-tuple-element.2108, bf16[512,32,128]{2,0,1:T(8,128)(2,1)} %get-tuple-element.2120, ...), kind=kOutput, calls=%fused_computation.136.clone.1 | convolution fusion | flops 809631744 | bytes 1843205 | tf_op jit(solution)/shard_map/while/body/eval_jaxpr/ijce,sic->sje/dot_general | solution.py:219
  430.7 18.9 %all_to_all.99 = bf16[64,32,256]{2,0,1:T(8,128)(2,1)S(1)} all-to-all(bf16[64,32,256]{2,0,1:T(8,128)(2,1)S(1)} %fusion.108), channel_id=1, replica_groups=mesh['dep_0'=2,'dep_1'=4,'res'=16] {'dep_0','dep_1'}, dimensions={1} | all-to-all | bytes 2097152 | tf_op jit(solution)/shard_map/all_to_all | solution.py:252
  451.7 170.0 %while.85 = (s32[]{:T(128)}, bf16[4,512,256]{1,2,0:T(8,128)(2,1)}, bf16[4,512,256]{2,1,0:T(8,128)(2,1)}, bf16[256,256]{1,0:T(8,128)(2,1)S(1)}, f32[4,512,256]{1,...) while((s32[]{:T(128)}, bf16[4,512,256]{1,2,0:T(8,128)(2,1)}, ...), condition=%wide.region_21.22_spmd, body=%wide.region_16.21_spmd.sunk | while | flops 921048064 | bytes 107711776 | solution.py:102
  466.5 8.9 %fusion.242 = bf16[8,512,32]{1,2,0:T(8,128)(2,1)S(1)} fusion(f32[4,8,512,512]{2,3,1,0:T(8,128)} %get-tuple-element.2222, s32[]{:T(128)S(6)} %sub.204, f32[8,512]{1,0:T(8,128)S(1)} %bitcast_divide_fusion.2, bf16[4,512,8,32]{1,3,2,0:T(8,128)(2,1)} %get-tuple-element.2225, bf16[8,512,512]{1,2,0:T(8,128)(2,1)} %copy-done.2, ...), kind=kOutput, calls=%fused_computation.72.clone.1 | convolution fusion | flops 147324928 | bytes 21545984 | tf_op jit(solution)/shard_map/transpose(jvp())/while/body/eval_jaxpr/shd,thd->hst/dot_general | solution.py:81
  475.4 8.9 %fusion.240 = bf16[8,512,32]{1,2,0:T(8,128)(2,1)S(1)} fusion(f32[4,8,512,512]{2,3,1,0:T(8,128)} %get-tuple-element.2222, s32[]{:T(128)S(6)} %sub.204, f32[8,512]{1,0:T(8,128)S(1)} %bitcast_divide_fusion.2, bf16[4,512,8,32]{1,3,2,0:T(8,128)(2,1)} %get-tuple-element.2223, bf16[8,512,512]{1,2,0:T(8,128)(2,1)} %copy-done.2, ...), kind=kOutput, calls=%fused_computation.69.clone.1 | convolution fusion | flops 146931712 | bytes 21545984 | tf_op jit(solution)/shard_map/transpose(jvp())/while/body/eval_jaxpr/shd,thd->hst/dot_general | solution.py:81
  509.0 8.9 %fusion.242 = bf16[8,512,32]{1,2,0:T(8,128)(2,1)S(1)} fusion(f32[4,8,512,512]{2,3,1,0:T(8,128)} %get-tuple-element.2222, s32[]{:T(128)S(6)} %sub.204, f32[8,512]{1,0:T(8,128)S(1)} %bitcast_divide_fusion.2, bf16[4,512,8,32]{1,3,2,0:T(8,128)(2,1)} %get-tuple-element.2225, bf16[8,512,512]{1,2,0:T(8,128)(2,1)} %copy-done.2, ...), kind=kOutput, calls=%fused_computation.72.clone.1 | convolution fusion | flops 147324928 | bytes 21545984 | tf_op jit(solution)/shard_map/transpose(jvp())/while/body/eval_jaxpr/shd,thd->hst/dot_general | solution.py:81
  517.9 8.9 %fusion.240 = bf16[8,512,32]{1,2,0:T(8,128)(2,1)S(1)} fusion(f32[4,8,512,512]{2,3,1,0:T(8,128)} %get-tuple-element.2222, s32[]{:T(128)S(6)} %sub.204, f32[8,512]{1,0:T(8,128)S(1)} %bitcast_divide_fusion.2, bf16[4,512,8,32]{1,3,2,0:T(8,128)(2,1)} %get-tuple-element.2223, bf16[8,512,512]{1,2,0:T(8,128)(2,1)} %copy-done.2, ...), kind=kOutput, calls=%fused_computation.69.clone.1 | convolution fusion | flops 146931712 | bytes 21545984 | tf_op jit(solution)/shard_map/transpose(jvp())/while/body/eval_jaxpr/shd,thd->hst/dot_general | solution.py:81
  551.5 8.9 %fusion.242 = bf16[8,512,32]{1,2,0:T(8,128)(2,1)S(1)} fusion(f32[4,8,512,512]{2,3,1,0:T(8,128)} %get-tuple-element.2222, s32[]{:T(128)S(6)} %sub.204, f32[8,512]{1,0:T(8,128)S(1)} %bitcast_divide_fusion.2, bf16[4,512,8,32]{1,3,2,0:T(8,128)(2,1)} %get-tuple-element.2225, bf16[8,512,512]{1,2,0:T(8,128)(2,1)} %copy-done.2, ...), kind=kOutput, calls=%fused_computation.72.clone.1 | convolution fusion | flops 147324928 | bytes 21545984 | tf_op jit(solution)/shard_map/transpose(jvp())/while/body/eval_jaxpr/shd,thd->hst/dot_general | solution.py:81
  560.4 8.9 %fusion.240 = bf16[8,512,32]{1,2,0:T(8,128)(2,1)S(1)} fusion(f32[4,8,512,512]{2,3,1,0:T(8,128)} %get-tuple-element.2222, s32[]{:T(128)S(6)} %sub.204, f32[8,512]{1,0:T(8,128)S(1)} %bitcast_divide_fusion.2, bf16[4,512,8,32]{1,3,2,0:T(8,128)(2,1)} %get-tuple-element.2223, bf16[8,512,512]{1,2,0:T(8,128)(2,1)} %copy-done.2, ...), kind=kOutput, calls=%fused_computation.69.clone.1 | convolution fusion | flops 146931712 | bytes 21545984 | tf_op jit(solution)/shard_map/transpose(jvp())/while/body/eval_jaxpr/shd,thd->hst/dot_general | solution.py:81
  594.0 8.9 %fusion.242 = bf16[8,512,32]{1,2,0:T(8,128)(2,1)S(1)} fusion(f32[4,8,512,512]{2,3,1,0:T(8,128)} %get-tuple-element.2222, s32[]{:T(128)S(6)} %sub.204, f32[8,512]{1,0:T(8,128)S(1)} %bitcast_divide_fusion.2, bf16[4,512,8,32]{1,3,2,0:T(8,128)(2,1)} %get-tuple-element.2225, bf16[8,512,512]{1,2,0:T(8,128)(2,1)} %copy-done.2, ...), kind=kOutput, calls=%fused_computation.72.clone.1 | convolution fusion | flops 147324928 | bytes 21545984 | tf_op jit(solution)/shard_map/transpose(jvp())/while/body/eval_jaxpr/shd,thd->hst/dot_general | solution.py:81
  602.9 8.9 %fusion.240 = bf16[8,512,32]{1,2,0:T(8,128)(2,1)S(1)} fusion(f32[4,8,512,512]{2,3,1,0:T(8,128)} %get-tuple-element.2222, s32[]{:T(128)S(6)} %sub.204, f32[8,512]{1,0:T(8,128)S(1)} %bitcast_divide_fusion.2, bf16[4,512,8,32]{1,3,2,0:T(8,128)(2,1)} %get-tuple-element.2223, bf16[8,512,512]{1,2,0:T(8,128)(2,1)} %copy-done.2, ...), kind=kOutput, calls=%fused_computation.69.clone.1 | convolution fusion | flops 146931712 | bytes 21545984 | tf_op jit(solution)/shard_map/transpose(jvp())/while/body/eval_jaxpr/shd,thd->hst/dot_general | solution.py:81
  629.3 12.6 %all-to-all-done.6 = bf16[512,4,256]{2,1,0:T(4,128)(2,1)S(1)} async-done(((bf16[512,4,256]{2,1,0:T(4,128)(2,1)}), bf16[512,4,256]{2,1,0:T(4,128)(2,1)S(1)}, u32[]{:S(2)}, u32[]{:S(2)}) %all-to-all-start.6) | async-done | bytes 1048608 | tf_op jit(solution)/shard_map/all_to_all | solution.py:256
  (396 shorter events, 422.3 us)
Async XLA Ops:
  7.2 182.4 %copy-start = (bf16[256,32]{0,1:T(8,128)(2,1)S(1)}, bf16[256,32]{0,1:T(8,128)(2,1)}, u32[]{:S(2)}) copy-start(bf16[256,32]{0,1:T(8,128)(2,1)} %param.30) | copy-start | bytes 49156
  7.2 40.4 %copy-start.6 = (bf16[256,256]{1,0:T(8,128)(2,1)S(1)}, bf16[256,256]{1,0:T(8,128)(2,1)}, u32[]{:S(2)}) copy-start(bf16[256,256]{1,0:T(8,128)(2,1)} %param.25) | copy-start | bytes 393220
  7.2 40.4 %copy-start.4 = (bf16[256,256]{1,0:T(8,128)(2,1)S(1)}, bf16[256,256]{1,0:T(8,128)(2,1)}, u32[]{:S(2)}) copy-start(bf16[256,256]{1,0:T(8,128)(2,1)} %param.26) | copy-start | bytes 393220
  7.2 40.4 %copy-start.12 = (bf16[256,256]{1,0:T(8,128)(2,1)S(1)}, bf16[256,256]{1,0:T(8,128)(2,1)}, u32[]{:S(2)}) copy-start(bf16[256,256]{1,0:T(8,128)(2,1)} %param.27) | copy-start | bytes 393220
  7.2 40.4 %copy-start.8 = (bf16[256,256]{1,0:T(8,128)(2,1)S(1)}, bf16[256,256]{1,0:T(8,128)(2,1)}, u32[]{:S(2)}) copy-start(bf16[256,256]{1,0:T(8,128)(2,1)} %param.28) | copy-start | bytes 393220
  7.2 40.3 %all-gather.11.cloned.1.call-start = ((), (), s32[]{:S(2)}) async-start(), calls=%async_computation.9 | async-start | bytes 1572864 | tf_op jit(solution)/shard_map/all_gather | solution.py:41
  8.7 38.9 %copy-start.21 = (bf16[64,32]{0,1:T(8,128)(2,1)}, bf16[64,32]{0,1:T(8,128)(2,1)S(1)}, u32[]{:S(2)}) copy-start(bf16[64,32]{0,1:T(8,128)(2,1)S(1)} %get-tuple-element.1600) | copy-start | bytes 12292
  9.4 12.5 %all-to-all-start.1 = ((bf16[8,2,128]{2,1,0:T(2,128)(2,1)}), bf16[8,2,128]{2,1,0:T(2,128)(2,1)S(1)}, u32[]{:S(2)}, u32[]{:S(2)}) async-start(bf16[8,2,128]{2,1,0:T(2,128)(2,1)} %reshape.379), calls=%async_computation.1 | async-start | bytes 8192 | tf_op jit(solution)/shard_map/all_to_all | solution.py:145
  21.8 25.6 %all-to-all-start = ((bf16[64,32,256]{2,0,1:T(8,128)(2,1)}), bf16[64,32,256]{2,0,1:T(8,128)(2,1)S(1)}, u32[]{:S(2)}, u32[]{:S(2)}) async-start(bf16[64,32,256]{2,0,1:T(8,128)(2,1)} %copy.229), calls=%async_computation | async-start | bytes 2097152 | tf_op jit(solution)/shard_map/all_to_all | solution.py:144
  25.4 223.0 %all-gather.13.cloned.1.call-start = ((), (), s32[]{:S(2)}) async-start(), calls=%async_computation.10 | async-start | bytes 5242880 | tf_op jit(solution)/shard_map/all_gather | solution.py:41
  164.3 18.3 %all-to-all-start.2 = ((bf16[512,4,256]{2,1,0:T(4,128)(2,1)}), bf16[512,4,256]{2,1,0:T(4,128)(2,1)S(1)}, u32[]{:S(2)}, u32[]{:S(2)}) async-start(bf16[512,4,256]{2,1,0:T(4,128)(2,1)} %bitcast.293), calls=%async_computation.2 | async-start | bytes 2097152 | tf_op jit(solution)/shard_map/all_to_all | solution.py:151
  168.3 96.3 %all-gather.7.cloned.1.call-start = ((), (), s32[]{:S(2)}) async-start(), calls=%async_computation.7 | async-start | bytes 4456448 | tf_op jit(solution)/shard_map/all_gather | solution.py:167
  220.3 13.8 %all-to-all-start.3 = ((bf16[8,32,512]{2,1,0:T(8,128)(2,1)}), bf16[8,32,512]{2,1,0:T(8,128)(2,1)}, u32[]{:S(2)}, u32[]{:S(2)}) async-start(bf16[8,32,512]{2,1,0:T(8,128)(2,1)} %broadcast_in_dim.162), calls=%async_computation.3 | async-start | bytes 524288 | tf_op jit(solution)/shard_map/all_to_all | solution.py:23
  224.3 121.2 %all-gather.9.cloned.1.call-start = ((), (), s32[]{:S(2)}) async-start(), calls=%async_computation.8 | async-start | bytes 4456448 | tf_op jit(solution)/shard_map/all_gather | solution.py:202
  259.6 80.4 %all-to-all-start.4 = ((bf16[32,512,128]{2,0,1:T(8,128)(2,1)}), bf16[32,512,128]{2,0,1:T(8,128)(2,1)}, u32[]{:S(2)}, u32[]{:S(2)}) async-start(bf16[32,512,128]{2,0,1:T(8,128)(2,1)} %copy.248), calls=%async_computation.4 | async-start | bytes 8388608 | tf_op jit(solution)/shard_map/all_to_all | solution.py:208
  345.5 75.1 %copy-start.20 = (f32[64,32]{1,0:T(8,128)S(1)}, f32[64,32]{1,0:T(8,128)}, u32[]{:S(2)}) copy-start(f32[64,32]{1,0:T(8,128)} %copy.240) | copy-start | bytes 24580
  430.7 21.0 %copy-start.5 = (bf16[256,256]{1,0:T(8,128)(2,1)S(1)}, bf16[256,256]{1,0:T(8,128)(2,1)}, u32[]{:S(2)}) copy-start(bf16[256,256]{1,0:T(8,128)(2,1)} %param.26) | copy-start | bytes 393220
  430.7 21.0 %copy-start.7 = (bf16[256,256]{1,0:T(8,128)(2,1)S(1)}, bf16[256,256]{1,0:T(8,128)(2,1)}, u32[]{:S(2)}) copy-start(bf16[256,256]{1,0:T(8,128)(2,1)} %param.25) | copy-start | bytes 393220
  460.0 5.8 copy-start.2
  502.5 5.8 copy-start.2
  545.0 5.8 copy-start.2
  621.6 6.0 copy-start.10
  624.1 17.7 %all-to-all-start.6 = ((bf16[512,4,256]{2,1,0:T(4,128)(2,1)}), bf16[512,4,256]{2,1,0:T(4,128)(2,1)S(1)}, u32[]{:S(2)}, u32[]{:S(2)}) async-start(bf16[512,4,256]{2,1,0:T(4,128)(2,1)} %bitcast.83), calls=%async_computation.6 | async-start | bytes 2097152 | tf_op jit(solution)/shard_map/all_to_all | solution.py:256
  627.7 15.9 %copy-start.1 = (bf16[256,32]{0,1:T(8,128)(2,1)S(1)}, bf16[256,32]{0,1:T(8,128)(2,1)}, u32[]{:S(2)}) copy-start(bf16[256,32]{0,1:T(8,128)(2,1)} %param.30) | copy-start | bytes 49156
  (15 other events, 41.7 us)
Sparse Core Ops, SparseCore 0:
  9.7 34.8 all-gather.10
  47.7 48.9 all-gather.12
  193.7 54.7 all-gather.6
  250.9 84.7 all-gather.8
where the time goes:
time: 664 us; the launch traced here: 650 us
  matrix products  260 us (39%)
  local copies, waits for them, and re-layouts  126 us (19%)
  other arithmetic  117 us (18%)
  waiting for transfers between devices  61.3 us (9%)
  blocking collectives  43.8 us (7%)
  starting transfers between devices  27 us (4%)
  between operations  14.6 us (2%)
    dot_general x12, matrix products, attend_column(): jnp.einsum('shd,thd->hst', query, keyed, preferred_element_type=jnp.float32)  78.5 us
    dynamic_update_slice x28, other arithmetic, vertical_attention_whole(): lax.map(per_column, (jnp.swapaxes(block_cols, 0, 1), jnp.swapaxes(live_co...  60.9 us
    dot_general x8, matrix products, right_block(): jnp.einsum('ijce,sic->sje', outer_cot, left_rows_now, preferred_element_t...  53 us
    dot_general x8, matrix products, left_block(): jnp.einsum('ijce,sje->sic', outer_cot, right_rows_now, preferred_element_...  52.5 us
    dot_general x12, matrix products, attend_column(): jnp.einsum('wvx,xwj->vwj', attention_probabilities, content_projected, pr...  36.5 us
    all_gather x1, blocking collectives, on_device(): lax.all_gather(live_b, 'res', axis=1, tiled=True)  25 us
    reduce_sum x4, other arithmetic, attend_column(): powers = jnp.exp(scores - peak_score)  23.1 us
    all_to_all x1, waiting for transfers between devices, on_device(): lax.all_to_all(homolog_representation, DEP, split_axis=1, concat_axis=0,...  21.6 us
  transfers between devices with their start and end apart: 10, of which 5 were waited for; matrix products, arithmetic and copies ran while one was open for 37% of the time, Pallas kernels for 0%

commit v1 on v0

v1 whole, which is shorter than its diff:
```python
import jax
import jax.numpy as jnp
from jax import lax
from jax.experimental import pallas as pl
from jax.experimental.pallas import tpu as pltpu
from jax.sharding import PartitionSpec as P

F = 256
H = 8
DH = 32
N = 512
CW = 32
CZ = 128
EPS = 1e-05
BIG = 1e9
f32 = jnp.float32
bf16 = jnp.bfloat16
SCALE = DH ** (-0.5)
NT = (((1,), (1,)), ((), ()))


def mm(a, b):
    return jnp.dot(a, b, preferred_element_type=f32)


def mmt(a, b):
    return lax.dot_general(a, b, NT, preferred_element_type=f32)


def norm(v, axis):
    c = v - jnp.mean(v, axis, keepdims=True)
    inv = lax.rsqrt(jnp.mean(c * c, axis, keepdims=True) + EPS)
    return c * inv, inv


def spread(rows, h, extra):
    top = (h % 4) * DH
    parts = []
    if top:
        parts.append(jnp.zeros((top, N), bf16))
    parts.append(rows)
    if top < 96:
        parts.append(jnp.zeros((96 - top, N), bf16))
    parts.append(extra)
    return jnp.concatenate(parts, axis=0)


def fwd_kernel(x_ref, live_ref, wq, wk, wv, wg, we, wl, wr,
               p_ref, o_ref, g_ref, a_ref, l_ref, r_ref,
               wt, wlt, bias_s):
    k = pl.program_id(0)

    @pl.when(k == 0)
    def _():
        for n, w in enumerate((wq, wv, wg, we)):
            wt[n] = w[...].T
        wlt[0] = wl[...].T
        wlt[1] = wr[...].T
        b = (live_ref[...] - 1.0) * BIG
        b = jnp.concatenate([b, jnp.zeros((120, N), f32)], axis=0)
        bias_s[...] = b.T.astype(bf16)

    xin = x_ref[...].reshape(N, F)
    xhat, _ = norm(xin.astype(f32), 1)
    xb = xhat.astype(bf16)
    xbt = xb.T
    qt = (mm(wt[0], xbt) * SCALE).astype(bf16)
    vt = mm(wt[1], xbt).astype(bf16)
    kk = mm(xb, wk[...]).astype(bf16)
    gt = jax.nn.sigmoid(mm(wt[2], xbt))
    g_ref[0] = gt
    extra = (lax.broadcasted_iota(jnp.int32, (128, N), 0) == k).astype(f32).astype(bf16)
    bias = bias_s[...]
    for h in range(H):
        grp = h // 4
        lhs = jnp.concatenate([kk[:, 128 * grp:128 * grp + 128], bias], axis=1)
        st = mm(lhs, spread(qt[DH * h:DH * h + DH], h, extra))
        m = jnp.max(st, 0, keepdims=True)
        e = jnp.exp(st - m)
        s = jnp.sum(e, 0, keepdims=True)
        p = (e * (1.0 / s)).astype(bf16)
        p_ref[0, h] = p
        o_ref[0, pl.ds(DH * h, DH), :] = mm(vt[DH * h:DH * h + DH], p)
    gated = (gt * o_ref[0]).astype(bf16)
    up = mm(wt[3], gated)
    after = (xin.T.astype(f32) + up).astype(bf16)
    a_ref[0] = after
    yhat, _ = norm(after.astype(f32), 0)
    yb = yhat.astype(bf16)
    live = live_ref[pl.ds(k, 1), :]
    l_ref[0] = (mm(wlt[0], yb) * live).astype(bf16)
    r_ref[0] = (mm(wlt[1], yb) * live).astype(bf16)


def mid_kernel(a_ref, up_ref, lg_ref, rg_ref, wl, wr, it_ref, i_ref):
    yhat, inv = norm(a_ref[0].astype(f32), 0)
    dy = mm(wl[...], lg_ref[0]) + mm(wr[...], rg_ref[0])
    m1 = jnp.mean(dy, 0, keepdims=True)
    m2 = jnp.mean(dy * yhat, 0, keepdims=True)
    upt = up_ref[...].reshape(N, F).T.astype(f32)
    out = (inv * (dy - m1 - yhat * m2) + upt).astype(bf16)
    it_ref[0] = out
    i_ref[...] = out.T.reshape(i_ref.shape)


def bwd_kernel(x_ref, d_ref, p_ref, o_ref, g_ref, wq, wk, wv, wg, we,
               out_ref, wkt, acc_k, acc_v, acc_q):
    @pl.when(pl.program_id(0) == 0)
    def _():
        wkt[...] = wk[...].T

    xin = x_ref[...].reshape(N, F)
    xhat, _ = norm(xin.astype(f32), 1)
    xb = xhat.astype(bf16)
    xbt = xb.T
    q = (mm(xb, wq[...]) * SCALE).astype(bf16)
    v = mm(xb, wv[...]).astype(bf16)
    kt = mm(wkt[...], xbt).astype(bf16)
    gt = g_ref[0]
    ot = o_ref[0]
    dt = d_ref[0]
    dg = mm(we[...], dt).astype(bf16).astype(f32)
    dot_ = (dg * gt).astype(bf16)
    dpre = (dg * ot * gt * (1.0 - gt)).astype(bf16)
    do = dot_.T
    prod = dot_.astype(f32) * ot
    row = lax.broadcasted_iota(jnp.int32, (128, N), 0)
    col = lax.broadcasted_iota(jnp.int32, (N, 128), 1)
    ones = (col < 2).astype(f32).astype(bf16)
    lane = lax.broadcasted_iota(jnp.int32, (N, F), 1) // DH
    dk = jnp.zeros((N, F), f32)
    dv = jnp.zeros((N, F), f32)
    for h in range(H):
        grp = h // 4
        sl = slice(DH * h, DH * h + DH)
        dd = -jnp.sum(prod[sl], 0, keepdims=True)
        hi = dd.astype(bf16).astype(f32)
        lo = dd - hi
        extra = jnp.where(row == 0, hi, jnp.where(row == 1, lo, 0.0)).astype(bf16)
        lhs = jnp.concatenate([v[:, 128 * grp:128 * grp + 128], ones], axis=1)
        dp = mm(lhs, spread(dot_[sl], h, extra))
        p = p_ref[0, h]
        ds = (p.astype(f32) * dp).astype(bf16)
        mask = lane == h
        zero = jnp.zeros((), bf16)
        dv = dv + mm(p, jnp.where(mask, do, zero))
        dk = dk + mm(ds, jnp.where(mask, q, zero))
        acc_q[sl, :] = mm(kt[sl], ds)
    dq = (acc_q[...].astype(bf16).astype(f32) * SCALE).astype(bf16)
    dx = (mm(wq[...], dq) + mm(wg[...], dpre)
          + mmt(wk[...], dk.astype(bf16)) + mmt(wv[...], dv.astype(bf16)))
    dx = dx.astype(bf16).astype(f32)
    xt = xin.T.astype(f32)
    xh, inv = norm(xt, 0)
    m1 = jnp.mean(dx, 0, keepdims=True)
    m2 = jnp.mean(dx * xh, 0, keepdims=True)
    dln = (inv * (dx - m1 - xh * m2)).astype(bf16)
    out = (dt.astype(f32) + dln.astype(f32)).astype(bf16)
    out_ref[...] = out.T.reshape(out_ref.shape)


def whole(shape):
    return pl.BlockSpec(shape, lambda k: (0,) * len(shape))


def percol(shape):
    return pl.BlockSpec((1, *shape), lambda k: (k,) + (0,) * len(shape))


COLS = pl.BlockSpec((8, 1, 64, F), lambda k: (0, k, 0, 0))
PARAMS = pltpu.CompilerParams(vmem_limit_bytes=60 * 1024 * 1024, dimension_semantics=("arbitrary",))


def fwd(x, livet, wq, wk, wv, wg, we, wl, wr):
    C = x.shape[1]
    sd = jax.ShapeDtypeStruct
    return pl.pallas_call(
        fwd_kernel,
        grid=(C,),
        in_specs=[COLS, whole((8, N))] + [whole((F, F))] * 5 + [whole((F, CW))] * 2,
        out_specs=[percol((H, N, N)), percol((F, N)), percol((F, N)), percol((F, N)), percol((CW, N)), percol((CW, N))],
        out_shape=[sd((C, H, N, N), bf16), sd((C, F, N), f32), sd((C, F, N), f32), sd((C, F, N), bf16), sd((C, CW, N), bf16), sd((C, CW, N), bf16)],
        scratch_shapes=[pltpu.VMEM((4, F, F), bf16), pltpu.VMEM((2, CW, F), bf16), pltpu.VMEM((N, 128), bf16)],
        compiler_params=PARAMS,
        name="attention_forward",
        cost_estimate=pl.CostEstimate(flops=20_000_000_000, bytes_accessed=30_000_000, transcendentals=8_000_000),
    )(x, livet, wq, wk, wv, wg, we, wl, wr)


def mid(at, up, lg, rg, wl, wr):
    C = at.shape[0]
    sd = jax.ShapeDtypeStruct
    return pl.pallas_call(
        mid_kernel,
        grid=(C,),
        in_specs=[percol((F, N)), COLS, percol((CW, N)), percol((CW, N)), whole((F, CW)), whole((F, CW))],
        out_specs=[percol((F, N)), COLS],
        out_shape=[sd((C, F, N), bf16), sd((8, C, 64, F), bf16)],
        compiler_params=PARAMS,
        name="middle",
        cost_estimate=pl.CostEstimate(flops=500_000_000, bytes_accessed=5_000_000, transcendentals=0),
    )(at, up, lg, rg, wl, wr)


def bwd(x, dt, p, o, g, wq, wk, wv, wg, we):
    C = x.shape[1]
    sd = jax.ShapeDtypeStruct
    return pl.pallas_call(
        bwd_kernel,
        grid=(C,),
        in_specs=[COLS, percol((F, N)), percol((H, N, N)), percol((F, N)), percol((F, N))] + [whole((F, F))] * 5,
        out_specs=COLS,
        out_shape=sd((8, C, 64, F), bf16),
        scratch_shapes=[pltpu.VMEM((F, F), bf16), pltpu.VMEM((N, F), f32), pltpu.VMEM((N, F), f32), pltpu.VMEM((F, N), f32)],
        compiler_params=PARAMS,
        name="attention_backward",
        cost_estimate=pl.CostEstimate(flops=40_000_000_000, bytes_accessed=30_000_000, transcendentals=0),
    )(x, dt, p, o, g, wq, wk, wv, wg, we)


def outer_kernel(pd_ref, rc_ref, w_ref, oc1_ref, oc2_ref, perm):
    @pl.when(pl.program_id(0) == 0)
    def _():
        a = lax.broadcasted_iota(jnp.int32, (1024, 1024), 0)
        b = lax.broadcasted_iota(jnp.int32, (1024, 1024), 1)
        hit = ((a // CW) == (b % CW)) & ((a % CW) == (b // CW))
        perm[...] = hit.astype(f32).astype(bf16)

    z = (mmt(w_ref[...], pd_ref[...]) * rc_ref[...]).astype(bf16)
    rows = []
    for j in range(8):
        rows.append(jnp.concatenate([z[CW * c:CW * c + CW, CW * j:CW * j + CW] for c in range(CW)], axis=1))
    y = mm(jnp.concatenate(rows, axis=0), perm[...]).astype(bf16)
    oc1_ref[...] = y
    oc2_ref[...] = y.T


def outer(pd, recip, w):
    sd = jax.ShapeDtypeStruct
    return pl.pallas_call(
        outer_kernel,
        grid=(8,),
        in_specs=[pl.BlockSpec((256, 128), lambda k: (k, 0)), pl.BlockSpec((1, 256), lambda k: (0, k)), pl.BlockSpec((1024, 128), lambda k: (0, 0))],
        out_specs=[pl.BlockSpec((256, 1024), lambda k: (k, 0)), pl.BlockSpec((1024, 256), lambda k: (0, k))],
        out_shape=[sd((2048, 1024), bf16), sd((1024, 2048), bf16)],
        scratch_shapes=[pltpu.VMEM((1024, 1024), bf16)],
        compiler_params=PARAMS,
        name="outer_cotangent",
        cost_estimate=pl.CostEstimate(flops=5_000_000_000, bytes_accessed=10_000_000, transcendentals=0),
    )(pd, recip, w)


def on_device(msa, present, pair, upstream, wq, wk, wv, wg, we, wl, wr, wo):
    d = lax.axis_index("dep")
    D = lax.axis_size("dep")
    R = lax.axis_size("res")

    def to_columns(a):
        a = a.transpose(1, 0, 2).reshape(D, 4, 64, F)
        return lax.all_to_all(a, "dep", 0, 0, tiled=True)

    def to_rows(a):
        a = lax.all_to_all(a, "dep", 0, 0, tiled=True)
        return a.reshape(4 * D, 64, F).transpose(1, 0, 2)

    x = to_columns(msa)
    live_b = present.T.astype(bf16)
    live_i = lax.all_gather(live_b, "dep", axis=1, tiled=True)
    live_own = lax.dynamic_slice_in_dim(live_i, 4 * d, 4, 0)
    live_j = lax.all_gather(live_own, "res", axis=0, tiled=True)
    counts = mmt(live_j, live_i)
    recip = 1.0 / (0.001 + counts)
    up = to_columns(upstream)
    pd = pair.reshape(32, 2, D, 4, CZ).transpose(2, 1, 3, 0, 4)
    pd = lax.all_to_all(pd, "dep", 0, 0, tiled=True)
    oc1, oc2 = outer(pd.reshape(-1, CZ), recip.reshape(1, -1), wo)
    live4 = live_own.astype(f32)
    livet = jnp.pad(live4, ((0, 4), (0, 0)))
    p, o, g, at, lt, rt = fwd(x, livet, wq, wk, wv, wg, we, wl, wr)
    lall = lax.all_gather(lt.reshape(4 * CW, N), "dep", axis=0, tiled=True)
    rall = lax.all_gather(rt.reshape(4 * CW, N), "res", axis=0, tiled=True)
    lp = mm(oc2, rall).astype(bf16).reshape(D, 4 * CW, N)
    rp = mm(oc1, lall).astype(bf16).reshape(R, 4 * CW, N)
    lp = lax.all_to_all(lp, "dep", 0, 0, tiled=True).astype(f32).sum(0).reshape(4, CW, N)
    rp = lax.all_to_all(rp, "res", 0, 0, tiled=True).astype(f32).sum(0).reshape(4, CW, N)
    lg = (lp * live4[:, None, :]).astype(bf16)
    rg = (rp * live4[:, None, :]).astype(bf16)
    dt, inter = mid(at, up, lg, rg, wl, wr)
    grad = bwd(x, dt, p, o, g, wq, wk, wv, wg, we)
    return to_rows(grad), to_rows(inter)


def solution(mesh):
    rows = P("dep", "res", None)
    in_specs = (rows, P("dep", "res"), P("res", "dep", None), rows) + (P(),) * 8
    return jax.shard_map(on_device, mesh=mesh, in_specs=in_specs, out_specs=(rows, rows), check_vma=False)
```

time: 664 us -> 305 us (0.46); the launches traced: 650 us -> 305 us
  matrix products: 260 us -> 12.5 us
  other arithmetic: 117 us -> 1.2 us
  local copies, waits for them, and re-layouts: 126 us -> 14.6 us
  Pallas kernels: 0 us -> 67.7 us
  blocking collectives: 43.8 us -> 81.6 us
  waiting for transfers between devices: 61.3 us -> 86.8 us
    dot_general x85 -> x3, matrix products: 260 us -> 12.5 us  [the longest x2 12.3 us: mm(): return jnp.dot(a, b, preferred_element_type=f32)]
    pallas_call x0 -> x4, Pallas kernels: none -> 67.6 us  [the longest x1 25.7 us: fwd(): pl.pallas_call(fwd_kernel, grid=(C,), in_specs=[COLS, whole((8, N))] + [w...]
    dynamic_update_slice x28 -> x0, other arithmetic: 60.9 us -> none  [vertical_attention_whole(): lax.map(per_column, (jnp.swapaxes(block_cols, 0, 1), jnp.swapaxes(live_co...]
    dynamic_slice x80 -> x0, local copies, waits for them, and re-layouts: 58.7 us -> none  [the longest x32 19 us: vertical_attention_whole(): lax.map(per_column, (jnp.swapaxes(block_cols, 0, 1), jnp.swapaxes(live_co...]
    all_gather x4 -> x2, waiting for transfers between devices: 0.06 us -> 47.9 us  [the longest x1 47.9 us: on_device(): rall = lax.all_gather(rt.reshape(4 * CW, N), 'res', axis=0, tiled=True)]
    reduce_sum x23 -> x2, other arithmetic: 41.4 us -> 0.44 us  [the longest x1 0.29 us: on_device(): lax.all_to_all(rp, 'res', 0, 0, tiled=True).astype(f32).sum(0)]
    all_gather x1 -> x2, blocking collectives: 25 us -> 62 us  [the longest x1 37.6 us: on_device(): live_i = lax.all_gather(live_b, 'dep', axis=1, tiled=True)]
    all_to_all x6, waiting for transfers between devices: 60.5 us -> 38.2 us  [the longest x2 13.8 us: to_columns(): return lax.all_to_all(a, 'dep', 0, 0, tiled=True)]
  transfers between devices with their start and end apart: 10 -> 8, of which waited for: 5 -> 4; matrix products, arithmetic and copies ran while one was open for 37% -> 7% of each run, Pallas kernels for 0% -> 4%
where the time goes in v1:
time: 305 us
  waiting for transfers between devices  86.8 us (28%)
  blocking collectives  81.6 us (27%)
  Pallas kernels  67.7 us (22%)
  starting transfers between devices  26.1 us (9%)
  local copies, waits for them, and re-layouts  14.6 us (5%)
  between operations  14.2 us (5%)
  matrix products  12.5 us (4%)
    all_gather x1, waiting for transfers between devices, on_device(): rall = lax.all_gather(rt.reshape(4 * CW, N), 'res', axis=0, tiled=True)  47.9 us
    all_gather x1, blocking collectives, on_device(): live_i = lax.all_gather(live_b, 'dep', axis=1, tiled=True)  37.6 us
    pallas_call x1, Pallas kernels, fwd(): pl.pallas_call(fwd_kernel, grid=(C,), in_specs=[COLS, whole((8, N))] + [w...  25.7 us
    pallas_call x1, Pallas kernels, bwd(): pl.pallas_call(bwd_kernel, grid=(C,), in_specs=[COLS, percol((F, N)), per...  25.4 us
    all_gather x1, blocking collectives, on_device(): live_j = lax.all_gather(live_own, 'res', axis=0, tiled=True)  24.4 us
    all_to_all x1, blocking collectives, to_rows(): a = lax.all_to_all(a, 'dep', 0, 0, tiled=True)  19.7 us
    all_to_all x2, waiting for transfers between devices, to_columns(): return lax.all_to_all(a, 'dep', 0, 0, tiled=True)  13.8 us
    all_to_all x1, waiting for transfers between devices, on_device(): lax.all_to_all(lp, 'dep', 0, 0, tiled=True).astype(f32).sum(0)  12.4 us
  transfers between devices with their start and end apart: 8, of which 4 were waited for; matrix products, arithmetic and copies ran while one was open for 7% of the time, Pallas kernels for 4%

profile of v1, /device:TPU:0, one launch (start us, length us, event | category | flops | bytes accessed | tf_op | source)
XLA Modules:
  0.0 304.5 jit_solution(8323495992607697654)
XLA Ops:
  7.2 2.8 copy.36
  10.0 6.4 %all-to-all-start = ((bf16[8,4,64,256]{3,2,1,0:T(8,128)(2,1)}), bf16[8,4,64,256]{3,2,1,0:T(8,128)(2,1)S(1)}, u32[]{:S(2)}, u32[]{:S(2)}) async-start(bf16[8,4,64,256]{3,2,1,0:T(8,128)(2,1)} %bitcast.1), calls=%async_computation | async-start | bytes 2097152 | tf_op jit(solution)/shard_map/all_to_all | solution.py:260
  16.4 37.6 %all-gather = bf16[8,64,32]{1,2,0:T(8,128)(2,1)S(1)} all-gather(bf16[1,64,32]{1,2,0:T(8,128)(2,1)S(1)} %convert_bitcast_fusion), channel_id=1, replica_groups=mesh['dep'=8,'res'=16] {'dep'}, dimensions={0}, use_global_device_ids=true | all-gather | bytes 36864 | tf_op jit(solution)/shard_map/all_gather | solution.py:268
  57.2 25.7 %attention_forward.1 = (bf16[4,8,512,512]{3,2,1,0:T(8,128)(2,1)}, f32[4,256,512]{2,1,0:T(8,128)}, f32[4,256,512]{2,1,0:T(8,128)}, bf16[4,256,512]{2,1,0:T(8,128)...) custom-call(bf16[8,4,64,256]{3,2,1,0:T(8,128)(2,1)} %copy-done, f32[8,512]{1,0:T(8,128)} %pad.4.live_ref, ...), custom_call_target="tpu_custom_call" | custom-call | flops 20000000000 | bytes 30000000 | tf_op jit(solution)/shard_map/attention_forward/pallas_call | solution.py:177
  83.7 1.1 copy.52
  84.8 3.5 %all-to-all-start.2 = ((bf16[8,2,4,32,128]{4,3,2,1,0:T(8,128)(2,1)}), bf16[8,2,4,32,128]{4,3,2,1,0:T(8,128)(2,1)S(1)}, u32[]{:S(2)}, u32[]{:S(2)}) async-start(bf16[8,2,4,32,128]{4,3,2,1,0:T(8,128)(2,1)} %bitcast.37), calls=%async_computation.2 | async-start | bytes 1048576 | tf_op jit(solution)/shard_map/all_to_all | solution.py:275
  88.3 24.4 %all-gather.1 = bf16[16,4,512]{2,1,0:T(4,128)(2,1)S(1)} all-gather(bf16[1,4,512]{2,1,0:T(4,128)(2,1)S(1)} %get-tuple-element.22), channel_id=1, replica_groups=mesh['dep'=8,'res'=16] {'res'}, dimensions={0}, use_global_device_ids=true | all-gather | bytes 69632 | tf_op jit(solution)/shard_map/all_gather | solution.py:270
  114.5 11.8 %outer_cotangent.1 = (bf16[2048,1024]{1,0:T(8,128)(2,1)}, bf16[1024,2048]{1,0:T(8,128)(2,1)}) custom-call(bf16[2048,128]{1,0:T(8,128)(2,1)} %bitcast.50, f32[1,2048]{1,0:T(1,128)} %reshape.48.rc_ref, bf16[1024,128]{1,0:T(8,128)(2,1)} %w_ref.1), custom_call_target="tpu_custom_call" | custom-call | flops 5000000000 | bytes 10000000 | tf_op jit(solution)/shard_map/outer_cotangent/pallas_call | solution.py:240
  126.2 6.1 %convolution_convert_fusion = bf16[2048,512]{1,0:T(8,128)(2,1)} fusion(bf16[2048,1024]{1,0:T(8,128)(2,1)} %get-tuple-element.15, bf16[1024,512]{1,0:T(8,128)(2,1)} %all-gather.7.cloned.1.call-done), kind=kOutput, calls=%fused_computation.1 | convolution fusion | flops 2148532224 | bytes 7340032 | tf_op jit(solution)/shard_map/dot_general | solution.py:23
  132.4 3.9 %all-to-all-start.4 = ((bf16[16,128,512]{2,1,0:T(8,128)(2,1)}), bf16[16,128,512]{2,1,0:T(8,128)(2,1)S(1)}, u32[]{:S(2)}, u32[]{:S(2)}) async-start(bf16[16,128,512]{2,1,0:T(8,128)(2,1)} %bitcast.41), calls=%async_computation.4 | async-start | bytes 4194304 | tf_op jit(solution)/shard_map/all_to_all | solution.py:285
  136.3 47.9 %all-gather.5.cloned.1.call-done = bf16[2048,512]{1,0:T(8,128)(2,1)} async-done(((bf16[128,512]{1,0:T(8,128)(2,1)}), bf16[2048,512]{1,0:T(8,128)(2,1)}) %all-gather.5.cloned.1.call-update) | async-done | bytes 2097168 | tf_op jit(solution)/shard_map/all_gather | solution.py:281
  184.2 6.2 %convolution_convert_fusion.1 = bf16[1024,512]{1,0:T(8,128)(2,1)} fusion(bf16[1024,2048]{1,0:T(8,128)(2,1)} %get-tuple-element.13, bf16[2048,512]{1,0:T(8,128)(2,1)} %all-gather.5.cloned.1.call-done), kind=kOutput, calls=%fused_computation.3 | convolution fusion | flops 2148007936 | bytes 7340032 | tf_op jit(solution)/shard_map/dot_general | solution.py:23
  190.4 4.4 %all-to-all-start.3 = ((bf16[8,128,512]{2,1,0:T(8,128)(2,1)}), bf16[8,128,512]{2,1,0:T(8,128)(2,1)S(1)}, u32[]{:S(2)}, u32[]{:S(2)}) async-start(bf16[8,128,512]{2,1,0:T(8,128)(2,1)} %bitcast.48), calls=%async_computation.3 | async-start | bytes 2097152 | tf_op jit(solution)/shard_map/all_to_all | solution.py:284
  194.8 2.8 copy.40
  197.6 12.4 %all-to-all-done.3 = bf16[8,128,512]{2,1,0:T(8,128)(2,1)S(1)} async-done(((bf16[8,128,512]{2,1,0:T(8,128)(2,1)}), bf16[8,128,512]{2,1,0:T(8,128)(2,1)S(1)}, u32[]{:S(2)}, u32[]{:S(2)}) %all-to-all-start.3) | async-done | bytes 1048608 | tf_op jit(solution)/shard_map/all_to_all | solution.py:284
  210.0 4.2 %all-to-all-start.1 = ((bf16[8,4,64,256]{3,2,1,0:T(8,128)(2,1)}), bf16[8,4,64,256]{3,2,1,0:T(8,128)(2,1)}, u32[]{:S(2)}, u32[]{:S(2)}) async-start(bf16[8,4,64,256]{3,2,1,0:T(8,128)(2,1)} %bitcast.38), calls=%async_computation.1 | async-start | bytes 2097152 | tf_op jit(solution)/shard_map/all_to_all | solution.py:260
  215.5 13.8 %all-to-all-done.1.up_ref = bf16[8,4,64,256]{3,2,1,0:T(8,128)(2,1)} async-done(((bf16[8,4,64,256]{3,2,1,0:T(8,128)(2,1)}), bf16[8,4,64,256]{3,2,1,0:T(8,128)(2,1)}, u32[]{:S(2)}, u32[]{:S(2)}) %all-to-all-start.1) | async-done | bytes 1048608 | tf_op jit(solution)/shard_map/all_to_all | solution.py:260
  229.2 4.7 %middle.1 = (bf16[4,256,512]{2,1,0:T(8,128)(2,1)}, bf16[8,4,64,256]{3,2,1,0:T(8,128)(2,1)}) custom-call(bf16[4,256,512]{2,1,0:T(8,128)(2,1)} %get-tuple-element.12.a_ref, bf16[8,4,64,256]{3,2,1,0:T(8,128)(2,1)} %all-to-all-done.1.up_ref, bf16[4,32,512]{2,1,0:T(8,128)(2,1)} %get-tuple-element.25.lg_ref, bf16[4,32,512]{2,1,0:T(8,128)(2,1)} %get-tuple-element.24.rg_ref, ...), custom_call_target="tpu_custom_call" | custom-call | flops 500000000 | bytes 5000000 | tf_op jit(solution)/shard_map/middle/pallas_call | solution.py:193
  233.9 25.4 %attention_backward.1 = bf16[8,4,64,256]{3,2,1,0:T(8,128)(2,1)} custom-call(bf16[8,4,64,256]{3,2,1,0:T(8,128)(2,1)} %copy-done, bf16[4,256,512]{2,1,0:T(8,128)(2,1)} %get-tuple-element.17.d_ref, bf16[4,8,512,512]{3,2,1,0:T(8,128)(2,1)} %get-tuple-element.18.p_ref, f32[4,256,512]{2,1,0:T(8,128)} %get-tuple-element.19.o_ref, ...), custom_call_target="tpu_custom_call" | custom-call | flops 40000000000 | bytes 30000000 | tf_op jit(solution)/shard_map/attention_backward/pallas_call | solution.py:208
  259.4 19.7 %all_to_all.35 = bf16[8,4,64,256]{3,2,1,0:T(8,128)(2,1)S(1)} all-to-all(bf16[8,4,64,256]{3,2,1,0:T(8,128)(2,1)} %attention_backward.1), channel_id=1, replica_groups=mesh['dep'=8,'res'=16] {'dep'}, dimensions={0} | all-to-all | bytes 2097152 | tf_op jit(solution)/shard_map/all_to_all | solution.py:263
  279.0 3.6 %all-to-all-start.6 = ((bf16[8,4,64,256]{3,2,1,0:T(8,128)(2,1)}), bf16[8,4,64,256]{3,2,1,0:T(8,128)(2,1)S(1)}, u32[]{:S(2)}, u32[]{:S(2)}) async-start(bf16[8,4,64,256]{3,2,1,0:T(8,128)(2,1)} %get-tuple-element.21), calls=%async_computation.6 | async-start | bytes 2097152 | tf_op jit(solution)/shard_map/all_to_all | solution.py:263
  282.6 1.6 copy.51
  284.1 12.0 %all-to-all-done.6 = bf16[8,4,64,256]{3,2,1,0:T(8,128)(2,1)S(1)} async-done(((bf16[8,4,64,256]{3,2,1,0:T(8,128)(2,1)}), bf16[8,4,64,256]{3,2,1,0:T(8,128)(2,1)S(1)}, u32[]{:S(2)}, u32[]{:S(2)}) %all-to-all-start.6) | async-done | bytes 1048608 | tf_op jit(solution)/shard_map/all_to_all | solution.py:263
  296.1 1.6 copy.50
  (34 shorter events, 6.9 us)
Async XLA Ops:
  7.2 9.2 %copy-start.5 = (s32[64,32]{0,1:T(8,128)S(1)}, s32[64,32]{0,1:T(8,128)}, u32[]{:S(2)}) copy-start(s32[64,32]{0,1:T(8,128)} %param.13) | copy-start | bytes 24580
  7.2 47.0 %copy-start.3 = (bf16[256,32]{0,1:T(8,128)(2,1)S(1)}, bf16[256,32]{0,1:T(8,128)(2,1)}, u32[]{:S(2)}) copy-start(bf16[256,32]{0,1:T(8,128)(2,1)} %param.21) | copy-start | bytes 49156
  7.2 47.7 %copy-start.4 = (bf16[256,32]{0,1:T(8,128)(2,1)S(1)}, bf16[256,32]{0,1:T(8,128)(2,1)}, u32[]{:S(2)}) copy-start(bf16[256,32]{0,1:T(8,128)(2,1)} %param.22) | copy-start | bytes 49156
  10.0 46.2 %all-to-all-start = ((bf16[8,4,64,256]{3,2,1,0:T(8,128)(2,1)}), bf16[8,4,64,256]{3,2,1,0:T(8,128)(2,1)S(1)}, u32[]{:S(2)}, u32[]{:S(2)}) async-start(bf16[8,4,64,256]{3,2,1,0:T(8,128)(2,1)} %bitcast.1), calls=%async_computation | async-start | bytes 2097152 | tf_op jit(solution)/shard_map/all_to_all | solution.py:260
  16.3 109.9 %all-gather.7.cloned.1.call-start = ((), (), s32[]{:S(2)}) async-start(), calls=%async_computation.8 | async-start | bytes 1179648 | tf_op jit(solution)/shard_map/all_gather | solution.py:280
  56.2 27.5 %copy-start.1 = (bf16[32,64,128]{2,1,0:T(8,128)(2,1)S(1)}, bf16[32,64,128]{2,1,0:T(8,128)(2,1)}, u32[]{:S(2)}) copy-start(bf16[32,64,128]{2,1,0:T(8,128)(2,1)} %param.14) | copy-start | bytes 1572868
  56.2 1.0 copy-start
  82.9 101.3 %all-gather.5.cloned.1.call-start = ((), (), s32[]{:S(2)}) async-start(), calls=%async_computation.7 | async-start | bytes 2228224 | tf_op jit(solution)/shard_map/all_gather | solution.py:281
  84.8 28.8 %all-to-all-start.2 = ((bf16[8,2,4,32,128]{4,3,2,1,0:T(8,128)(2,1)}), bf16[8,2,4,32,128]{4,3,2,1,0:T(8,128)(2,1)S(1)}, u32[]{:S(2)}, u32[]{:S(2)}) async-start(bf16[8,2,4,32,128]{4,3,2,1,0:T(8,128)(2,1)} %bitcast.37), calls=%async_computation.2 | async-start | bytes 1048576 | tf_op jit(solution)/shard_map/all_to_all | solution.py:275
  113.7 0.8 copy-start.2
  132.4 58.0 %all-to-all-start.4 = ((bf16[16,128,512]{2,1,0:T(8,128)(2,1)}), bf16[16,128,512]{2,1,0:T(8,128)(2,1)S(1)}, u32[]{:S(2)}, u32[]{:S(2)}) async-start(bf16[16,128,512]{2,1,0:T(8,128)(2,1)} %bitcast.41), calls=%async_computation.4 | async-start | bytes 4194304 | tf_op jit(solution)/shard_map/all_to_all | solution.py:285
  190.4 19.6 %all-to-all-start.3 = ((bf16[8,128,512]{2,1,0:T(8,128)(2,1)}), bf16[8,128,512]{2,1,0:T(8,128)(2,1)S(1)}, u32[]{:S(2)}, u32[]{:S(2)}) async-start(bf16[8,128,512]{2,1,0:T(8,128)(2,1)} %bitcast.48), calls=%async_computation.3 | async-start | bytes 2097152 | tf_op jit(solution)/shard_map/all_to_all | solution.py:284
  210.0 19.2 %all-to-all-start.1 = ((bf16[8,4,64,256]{3,2,1,0:T(8,128)(2,1)}), bf16[8,4,64,256]{3,2,1,0:T(8,128)(2,1)}, u32[]{:S(2)}, u32[]{:S(2)}) async-start(bf16[8,4,64,256]{3,2,1,0:T(8,128)(2,1)} %bitcast.38), calls=%async_computation.1 | async-start | bytes 2097152 | tf_op jit(solution)/shard_map/all_to_all | solution.py:260
  279.0 17.1 %all-to-all-start.6 = ((bf16[8,4,64,256]{3,2,1,0:T(8,128)(2,1)}), bf16[8,4,64,256]{3,2,1,0:T(8,128)(2,1)S(1)}, u32[]{:S(2)}, u32[]{:S(2)}) async-start(bf16[8,4,64,256]{3,2,1,0:T(8,128)(2,1)} %get-tuple-element.21), calls=%async_computation.6 | async-start | bytes 2097152 | tf_op jit(solution)/shard_map/all_to_all | solution.py:263
Sparse Core Ops, SparseCore 0:
  83.1 37.5 all-gather.6
  123.1 61.0 all-gather.4

commit v2 on v1

--- a/solution.py
+++ b/solution.py
@@ -218,42 +218,154 @@
     )(x, dt, p, o, g, wq, wk, wv, wg, we)
 
 
-def outer_kernel(pd_ref, rc_ref, w_ref, oc1_ref, oc2_ref, perm):
-    @pl.when(pl.program_id(0) == 0)
-    def _():
-        a = lax.broadcasted_iota(jnp.int32, (1024, 1024), 0)
-        b = lax.broadcasted_iota(jnp.int32, (1024, 1024), 1)
-        hit = ((a // CW) == (b % CW)) & ((a % CW) == (b // CW))
-        perm[...] = hit.astype(f32).astype(bf16)
-
-    z = (mmt(w_ref[...], pd_ref[...]) * rc_ref[...]).astype(bf16)
-    rows = []
-    for j in range(8):
-        rows.append(jnp.concatenate([z[CW * c:CW * c + CW, CW * j:CW * j + CW] for c in range(CW)], axis=1))
-    y = mm(jnp.concatenate(rows, axis=0), perm[...]).astype(bf16)
-    oc1_ref[...] = y
-    oc2_ref[...] = y.T
-
-
-def outer(pd, recip, w):
+MESH = pl.DeviceIdType.MESH
+
+
+def remote(src, dst, send, recv, dep, res):
+    return pltpu.make_async_remote_copy(src_ref=src, dst_ref=dst, send_sem=send, recv_sem=recv,
+                                        device_id={"dep": dep, "res": res}, device_id_type=MESH)
+
+
+def greet(peers):
+    bar = pltpu.get_barrier_semaphore()
+    for dep, res in peers:
+        pl.semaphore_signal(bar, inc=1, device_id={"dep": dep, "res": res}, device_id_type=MESH)
+    pl.semaphore_wait(bar, len(peers))
+
+
+def opm_kernel(lt, rt, pd, rc, wo, live, lo, ro,
+               perm, oc1, oc2, lbuf, rbuf, lsend, lrecv, psend, precv, rsend, rrecv, lacc, racc,
+               ls, lr, rs, rr, fs, fr, ps, pr, s2, r2, s3, r3):
+    d = lax.axis_index("dep")
+    r = lax.axis_index("res")
+    core = lax.rem(r, 2)
+    chip = r // 2
+    partner = 2 * chip + 1 - core
+
+    def dep_at(k):
+        return lax.rem(d + k, 8)
+
+    def chip_at(k):
+        return lax.rem(chip + k, 8)
+
+    greet([(dep_at(k), r) for k in range(1, 8)]
+          + [(d, 2 * chip_at(k) + core) for k in range(1, 8)] + [(d, partner)])
+
+    gl = [remote(lt, lbuf.at[d], ls.at[k], lr.at[k], dep_at(k), r) for k in range(1, 8)]
+    gr = [remote(rt, rbuf.at[r], rs.at[k], rr.at[k], d, 2 * chip_at(k) + core) for k in range(1, 8)]
+    first = remote(rt, rbuf.at[r], fs.at[0], fr.at[0], d, partner)
+    for a, b in zip(gl, gr):
+        b.start()
+        a.start()
+    first.start()
+    lbuf[d] = lt[...]
+    rbuf[r] = rt[...]
+
+    a = lax.broadcasted_iota(jnp.int32, (1024, 1024), 0)
+    b = lax.broadcasted_iota(jnp.int32, (1024, 1024), 1)
+    hit = ((a // CW) == (b % CW)) & ((a % CW) == (b // CW))
+    perm[...] = hit.astype(f32).astype(bf16)
+
+    def forward(k):
+        slot = 2 * lax.rem(chip + 8 - k, 8) + core
+        return remote(rbuf.at[slot], rbuf.at[slot], fs.at[k], fr.at[k], d, partner)
+
+    def outer_step(n, carry):
+        at = pl.multiple_of(256 * n, 256)
+        z = (mmt(wo[...], pd[pl.ds(at, 256), :]) * rc[pl.ds(n, 1), :]).astype(bf16)
+        rows = []
+        for j in range(8):
+            rows.append(jnp.concatenate([z[CW * c:CW * c + CW, CW * j:CW * j + CW] for c in range(CW)], axis=1))
+        y = mm(jnp.concatenate(rows, axis=0), perm[...]).astype(bf16)
+        oc1[pl.ds(at, 256), :] = y
+        oc2[:, pl.ds(at, 256)] = y.T
+
+        @pl.when(n > 0)
+        def _():
+            remote(rt, rbuf.at[r], rs.at[n], rr.at[n], d, partner).wait_recv()
+            forward(n).start()
+        return carry
+
+    lax.fori_loop(0, 8, outer_step, 0)
+    for c in gl:
+        c.wait_recv()
+    lall = lbuf[...].reshape(1024, N)
+    part = []
+    for k in [1, 2, 3, 4, 5, 6, 7, 0]:
+        q = chip_at(k)
+        at = pl.multiple_of(256 * q + 128 * (1 - core), 128)
+        psend[k] = mm(oc1[pl.ds(at, 128), :], lall).astype(bf16)
+        c = remote(psend.at[k], precv.at[k], ps.at[k], pr.at[k], d, partner)
+        c.start()
+        part.append(c)
+    second = []
+    for k in [1, 2, 3, 4, 5, 6, 7, 0]:
+        q = chip_at(k)
+        at = pl.multiple_of(256 * q + 128 * core, 128)
+        own = mm(oc1[pl.ds(at, 128), :], lall)
+        remote(psend.at[k], precv.at[k], ps.at[k], pr.at[k], d, partner).wait_recv()
+        own = own + precv[k].astype(f32)
+        if k:
+            rsend[k] = own.astype(bf16)
+            c = remote(rsend.at[k], rrecv.at[k], s2.at[k], r2.at[k], d, 2 * q + core)
+            c.start()
+            second.append(c)
+        else:
+            racc[...] = own
+    first.wait_recv()
+    for k in range(1, 8):
+        forward(k).wait_recv()
+    rall = rbuf[...].reshape(2048, N)
+    third = []
+    for k in [1, 2, 3, 4, 5, 6, 7, 0]:
+        at = pl.multiple_of(128 * dep_at(k), 128)
+        own = mm(oc2[pl.ds(at, 128), :], rall)
+        if k:
+            lsend[k] = own.astype(bf16)
+            c = remote(lsend.at[k], lrecv.at[k], s3.at[k], r3.at[k], dep_at(k), r)
+            c.start()
+            third.append(c)
+        else:
+            lacc[...] = own
+    for c in second:
+        c.wait_recv()
+    racc[...] += jnp.sum(rrecv[1:8].astype(f32), 0)
+    for n in range(4):
+        ro[n] = (racc[CW * n:CW * n + CW, :] * live[n:n + 1, :]).astype(bf16)
+    for c in third:
+        c.wait_recv()
+    lacc[...] += jnp.sum(lrecv[1:8].astype(f32), 0)
+    for n in range(4):
+        lo[n] = (lacc[CW * n:CW * n + CW, :] * live[n:n + 1, :]).astype(bf16)
+    for c in gl + gr + [first] + part + second + third:
+        c.wait_send()
+    for k in range(1, 8):
+        forward(k).wait_send()
+
+
+def opm(lt, rt, pd, rc, wo, live):
     sd = jax.ShapeDtypeStruct
+    vm = pl.BlockSpec(memory_space=pltpu.VMEM)
+    chunk = (128, N)
+    V = pltpu.VMEM
+    dma = pltpu.SemaphoreType.DMA((8,))
     return pl.pallas_call(
-        outer_kernel,
-        grid=(8,),
-        in_specs=[pl.BlockSpec((256, 128), lambda k: (k, 0)), pl.BlockSpec((1, 256), lambda k: (0, k)), pl.BlockSpec((1024, 128), lambda k: (0, 0))],
-        out_specs=[pl.BlockSpec((256, 1024), lambda k: (k, 0)), pl.BlockSpec((1024, 256), lambda k: (0, k))],
-        out_shape=[sd((2048, 1024), bf16), sd((1024, 2048), bf16)],
-        scratch_shapes=[pltpu.VMEM((1024, 1024), bf16)],
-        compiler_params=PARAMS,
-        name="outer_cotangent",
-        cost_estimate=pl.CostEstimate(flops=5_000_000_000, bytes_accessed=10_000_000, transcendentals=0),
-    )(pd, recip, w)
+        opm_kernel,
+        in_specs=[vm] * 6,
+        out_specs=[vm] * 2,
+        out_shape=[sd((4, CW, N), bf16)] * 2,
+        scratch_shapes=[V((1024, 1024), bf16), V((2048, 1024), bf16), V((1024, 2048), bf16),
+                        V((8, *chunk), bf16), V((16, *chunk), bf16)] + [V((8, *chunk), bf16)] * 6
+        + [V(chunk, f32)] * 2 + [dma] * 12,
+        compiler_params=pltpu.CompilerParams(vmem_limit_bytes=60 * 1024 * 1024, collective_id=1, has_side_effects=True),
+        name="outer_product",
+        cost_estimate=pl.CostEstimate(flops=10_000_000_000, bytes_accessed=10_000_000, transcendentals=0),
+    )(lt, rt, pd, rc, wo, live)
 
 
 def on_device(msa, present, pair, upstream, wq, wk, wv, wg, we, wl, wr, wo):
     d = lax.axis_index("dep")
     D = lax.axis_size("dep")
-    R = lax.axis_size("res")
 
     def to_columns(a):
         a = a.transpose(1, 0, 2).reshape(D, 4, 64, F)
@@ -273,18 +385,10 @@
     up = to_columns(upstream)
     pd = pair.reshape(32, 2, D, 4, CZ).transpose(2, 1, 3, 0, 4)
     pd = lax.all_to_all(pd, "dep", 0, 0, tiled=True)
-    oc1, oc2 = outer(pd.reshape(-1, CZ), recip.reshape(1, -1), wo)
     live4 = live_own.astype(f32)
     livet = jnp.pad(live4, ((0, 4), (0, 0)))
     p, o, g, at, lt, rt = fwd(x, livet, wq, wk, wv, wg, we, wl, wr)
-    lall = lax.all_gather(lt.reshape(4 * CW, N), "dep", axis=0, tiled=True)
-    rall = lax.all_gather(rt.reshape(4 * CW, N), "res", axis=0, tiled=True)
-    lp = mm(oc2, rall).astype(bf16).reshape(D, 4 * CW, N)
-    rp = mm(oc1, lall).astype(bf16).reshape(R, 4 * CW, N)
-    lp = lax.all_to_all(lp, "dep", 0, 0, tiled=True).astype(f32).sum(0).reshape(4, CW, N)
-    rp = lax.all_to_all(rp, "res", 0, 0, tiled=True).astype(f32).sum(0).reshape(4, CW, N)
-    lg = (lp * live4[:, None, :]).astype(bf16)
-    rg = (rp * live4[:, None, :]).astype(bf16)
+    lg, rg = opm(lt.reshape(4 * CW, N), rt.reshape(4 * CW, N), pd.reshape(-1, CZ), recip.reshape(8, 256), wo, livet)
     dt, inter = mid(at, up, lg, rg, wl, wr)
     grad = bwd(x, dt, p, o, g, wq, wk, wv, wg, we)
     return to_rows(grad), to_rows(inter)

time: 305 us -> 246 us (0.81)
  waiting for transfers between devices: 86.8 us -> 10.8 us
  Pallas kernels: 67.7 us -> 116 us
  between operations: 14.2 us -> 0.77 us
  matrix products: 12.5 us -> 0.14 us
  starting transfers between devices: 26.1 us -> 19.1 us
  blocking collectives: 81.6 us -> 86.6 us
    all_gather x2 -> x0, waiting for transfers between devices: 47.9 us -> none  [the longest x1 47.9 us: on_device(): rall = lax.all_gather(rt.reshape(4 * CW, N), 'res', axis=0, tiled=True)]
    pallas_call x1, Pallas kernels: 11.8 us -> 59.7 us  [opm(): pl.pallas_call(opm_kernel, in_specs=[vm] * 6, out_specs=[vm] * 2, out_sha...]
    all_to_all x2, waiting for transfers between devices: 13.8 us -> 0.01 us  [to_columns(): return lax.all_to_all(a, 'dep', 0, 0, tiled=True)]
    all_to_all x2 -> x0, waiting for transfers between devices: 12.4 us -> none  [the longest x1 12.4 us: on_device(): lax.all_to_all(lp, 'dep', 0, 0, tiled=True).astype(f32).sum(0)]
    dot_general x2 -> x0, matrix products: 12.3 us -> none  [mm(): return jnp.dot(a, b, preferred_element_type=f32)]
    all_to_all x2 -> x0, starting transfers between devices: 8.33 us -> none  [the longest x1 4.43 us: on_device(): lax.all_to_all(lp, 'dep', 0, 0, tiled=True).astype(f32).sum(0)]
    all_to_all x1, blocking collectives: 19.7 us -> 24.6 us  [to_rows(): a = lax.all_to_all(a, 'dep', 0, 0, tiled=True)]
  transfers between devices with their start and end apart: 8 -> 4, of which waited for: 4 -> 1; matrix products, arithmetic and copies ran while one was open for 7% -> 3% of each run, Pallas kernels for 4% -> 35%
where the time goes in v2:
time: 246 us
  Pallas kernels  116 us (47%)
  blocking collectives  86.6 us (35%)
  starting transfers between devices  19.1 us (8%)
  local copies, waits for them, and re-layouts  12.1 us (5%)
  waiting for transfers between devices  10.8 us (4%)
    pallas_call x1, Pallas kernels, opm(): pl.pallas_call(opm_kernel, in_specs=[vm] * 6, out_specs=[vm] * 2, out_sha...  59.7 us
    all_gather x1, blocking collectives, on_device(): live_i = lax.all_gather(live_b, 'dep', axis=1, tiled=True)  37.6 us
    pallas_call x1, Pallas kernels, fwd(): pl.pallas_call(fwd_kernel, grid=(C,), in_specs=[COLS, whole((8, N))] + [w...  25.8 us
    pallas_call x1, Pallas kernels, bwd(): pl.pallas_call(bwd_kernel, grid=(C,), in_specs=[COLS, percol((F, N)), per...  25.4 us
    all_to_all x1, blocking collectives, to_rows(): a = lax.all_to_all(a, 'dep', 0, 0, tiled=True)  24.6 us
    all_gather x1, blocking collectives, on_device(): live_j = lax.all_gather(live_own, 'res', axis=0, tiled=True)  24.4 us
    all_to_all x2, starting transfers between devices, to_columns(): return lax.all_to_all(a, 'dep', 0, 0, tiled=True)  12.1 us
    all_to_all x1, waiting for transfers between devices, to_rows(): a = lax.all_to_all(a, 'dep', 0, 0, tiled=True)  10.8 us
  transfers between devices with their start and end apart: 4, of which 1 were waited for; matrix products, arithmetic and copies ran while one was open for 3% of the time, Pallas kernels for 35%

profile of v2, /device:TPU:0, one launch (start us, length us, event | category | flops | bytes accessed | tf_op | source)
XLA Modules:
  0.0 245.8 jit_solution(4566018498599262933)
XLA Ops:
  0.7 2.8 %copy.36 = bf16[32,64,256]{2,1,0:T(8,128)(2,1)} copy(bf16[32,64,256]{2,0,1:T(8,128)(2,1)} %bitcast.32) | data formatting | bytes 2097152 | tf_op jit(solution)/shard_map/transpose | solution.py:371
  3.5 6.5 %all-to-all-start = ((bf16[8,4,64,256]{3,2,1,0:T(8,128)(2,1)}), bf16[8,4,64,256]{3,2,1,0:T(8,128)(2,1)S(1)}, u32[]{:S(2)}, u32[]{:S(2)}) async-start(bf16[8,4,64,256]{3,2,1,0:T(8,128)(2,1)} %bitcast.1), calls=%async_computation | async-start | bytes 2097152 | tf_op jit(solution)/shard_map/all_to_all | solution.py:372
  10.0 37.6 %all-gather = bf16[8,64,32]{1,2,0:T(8,128)(2,1)S(1)} all-gather(bf16[1,64,32]{1,2,0:T(8,128)(2,1)S(1)} %convert_bitcast_fusion), channel_id=1, replica_groups=mesh['dep'=8,'res'=16] {'dep'}, dimensions={0}, use_global_device_ids=true | all-gather | bytes 36864 | tf_op jit(solution)/shard_map/all_gather | solution.py:380
  47.7 0.1 reshape.41
  47.8 24.4 %all-gather.1 = bf16[16,4,512]{2,1,0:T(4,128)(2,1)S(1)} all-gather(bf16[1,4,512]{2,1,0:T(4,128)(2,1)S(1)} %get-tuple-element.22), channel_id=1, replica_groups=mesh['dep'=8,'res'=16] {'res'}, dimensions={0}, use_global_device_ids=true | all-gather | bytes 69632 | tf_op jit(solution)/shard_map/all_gather | solution.py:382
  72.2 0.1 fusion
  72.4 0.7 reshape.37.rc
  73.1 0.7 copy.38.wl
  73.8 0.7 copy.39.wr
  74.6 1.2 copy.52
  75.7 1.6 copy.40
  77.3 0.6 pad_convert_fusion.live_ref.live
  77.9 3.5 %all-to-all-start.2 = ((bf16[8,2,4,32,128]{4,3,2,1,0:T(8,128)(2,1)}), bf16[8,2,4,32,128]{4,3,2,1,0:T(8,128)(2,1)S(1)}, u32[]{:S(2)}, u32[]{:S(2)}) async-start(bf16[8,2,4,32,128]{4,3,2,1,0:T(8,128)(2,1)} %bitcast.29), calls=%async_computation.2 | async-start | bytes 1048576 | tf_op jit(solution)/shard_map/all_to_all | solution.py:387
  81.4 25.8 %attention_forward.1 = (bf16[4,8,512,512]{3,2,1,0:T(8,128)(2,1)}, f32[4,256,512]{2,1,0:T(8,128)}, f32[4,256,512]{2,1,0:T(8,128)}, bf16[4,256,512]{2,1,0:T(8,128)...) custom-call(bf16[8,4,64,256]{3,2,1,0:T(8,128)(2,1)} %copy-done.2, ...), custom_call_target="tpu_custom_call" | custom-call | flops 20000000000 | bytes 30000000 | tf_op jit(solution)/shard_map/attention_forward/pallas_call | solution.py:177
  107.2 5.6 %all-to-all-start.1 = ((bf16[8,4,64,256]{3,2,1,0:T(8,128)(2,1)}), bf16[8,4,64,256]{3,2,1,0:T(8,128)(2,1)S(1)}, u32[]{:S(2)}, u32[]{:S(2)}) async-start(bf16[8,4,64,256]{3,2,1,0:T(8,128)(2,1)} %bitcast.5), calls=%async_computation.1 | async-start | bytes 2097152 | tf_op jit(solution)/shard_map/all_to_all | solution.py:372
  112.8 59.7 %outer_product.1 = (bf16[4,32,512]{2,1,0:T(8,128)(2,1)}, bf16[4,32,512]{2,1,0:T(8,128)(2,1)}) custom-call(bf16[128,512]{1,0:T(8,128)(2,1)} %bitcast.38, bf16[128,512]{1,0:T(8,128)(2,1)} %bitcast.39, bf16[2048,128]{1,0:T(8,128)(2,1)} %bitcast.37, f32[8,256]{1,0:T(8,128)} %reshape.37.rc, bf16[1024,128]{1,0:T(8,128)(2,1)} %wo.1, ...), custom_call_target="tpu_custom_call" | custom-call | flops 10000000000 | bytes 10000000 | tf_op jit(solution)/shard_map/outer_product/pallas_call | solution.py:352
  172.5 1.0 copy-done
  173.5 4.8 %middle.1 = (bf16[4,256,512]{2,1,0:T(8,128)(2,1)}, bf16[8,4,64,256]{3,2,1,0:T(8,128)(2,1)}) custom-call(bf16[4,256,512]{2,1,0:T(8,128)(2,1)} %get-tuple-element.12.a_ref, bf16[8,4,64,256]{3,2,1,0:T(8,128)(2,1)} %copy-done, bf16[4,32,512]{2,1,0:T(8,128)(2,1)} %get-tuple-element.15.lg_ref, bf16[4,32,512]{2,1,0:T(8,128)(2,1)} %get-tuple-element.16.rg_ref, ...), custom_call_target="tpu_custom_call" | custom-call | flops 500000000 | bytes 5000000 | tf_op jit(solution)/shard_map/middle/pallas_call | solution.py:193
  178.3 25.4 %attention_backward.1 = bf16[8,4,64,256]{3,2,1,0:T(8,128)(2,1)} custom-call(bf16[8,4,64,256]{3,2,1,0:T(8,128)(2,1)} %copy-done.2, bf16[4,256,512]{2,1,0:T(8,128)(2,1)} %get-tuple-element.17.d_ref, bf16[4,8,512,512]{3,2,1,0:T(8,128)(2,1)} %get-tuple-element.18.p_ref, f32[4,256,512]{2,1,0:T(8,128)} %get-tuple-element.19.o_ref, ...), custom_call_target="tpu_custom_call" | custom-call | flops 40000000000 | bytes 30000000 | tf_op jit(solution)/shard_map/attention_backward/pallas_call | solution.py:208
  203.7 24.6 %all_to_all.25 = bf16[8,4,64,256]{3,2,1,0:T(8,128)(2,1)S(1)} all-to-all(bf16[8,4,64,256]{3,2,1,0:T(8,128)(2,1)} %attention_backward.1), channel_id=1, replica_groups=mesh['dep'=8,'res'=16] {'dep'}, dimensions={0} | all-to-all | bytes 2097152 | tf_op jit(solution)/shard_map/all_to_all | solution.py:375
  228.3 3.6 %all-to-all-start.4 = ((bf16[8,4,64,256]{3,2,1,0:T(8,128)(2,1)}), bf16[8,4,64,256]{3,2,1,0:T(8,128)(2,1)S(1)}, u32[]{:S(2)}, u32[]{:S(2)}) async-start(bf16[8,4,64,256]{3,2,1,0:T(8,128)(2,1)} %get-tuple-element.21), calls=%async_computation.4 | async-start | bytes 2097152 | tf_op jit(solution)/shard_map/all_to_all | solution.py:375
  231.9 1.6 copy.51
  233.4 10.8 %all-to-all-done.4 = bf16[8,4,64,256]{3,2,1,0:T(8,128)(2,1)S(1)} async-done(((bf16[8,4,64,256]{3,2,1,0:T(8,128)(2,1)}), bf16[8,4,64,256]{3,2,1,0:T(8,128)(2,1)S(1)}, u32[]{:S(2)}, u32[]{:S(2)}) %all-to-all-start.4) | async-done | bytes 1048608 | tf_op jit(solution)/shard_map/all_to_all | solution.py:375
  244.2 1.6 copy.50
  (23 shorter events, 0.2 us)
Async XLA Ops:
  0.6 9.4 %copy-start.7 = (s32[64,32]{0,1:T(8,128)S(1)}, s32[64,32]{0,1:T(8,128)}, u32[]{:S(2)}) copy-start(s32[64,32]{0,1:T(8,128)} %param.13) | copy-start | bytes 24580
  0.6 72.5 %copy-start.5 = (bf16[256,32]{0,1:T(8,128)(2,1)S(1)}, bf16[256,32]{0,1:T(8,128)(2,1)}, u32[]{:S(2)}) copy-start(bf16[256,32]{0,1:T(8,128)(2,1)} %param.21) | copy-start | bytes 49156
  0.7 73.2 %copy-start.6 = (bf16[256,32]{0,1:T(8,128)(2,1)S(1)}, bf16[256,32]{0,1:T(8,128)(2,1)}, u32[]{:S(2)}) copy-start(bf16[256,32]{0,1:T(8,128)(2,1)} %param.22) | copy-start | bytes 49156
  0.7 73.9 %copy-start.3 = (bf16[32,64,128]{2,1,0:T(8,128)(2,1)S(1)}, bf16[32,64,128]{2,1,0:T(8,128)(2,1)}, u32[]{:S(2)}) copy-start(bf16[32,64,128]{2,1,0:T(8,128)(2,1)} %param.14) | copy-start | bytes 1572868
  3.5 72.2 %copy-start.1 = (bf16[64,32,256]{2,1,0:T(8,128)(2,1)S(1)}, bf16[64,32,256]{2,1,0:T(8,128)(2,1)}, u32[]{:S(2)}) copy-start(bf16[64,32,256]{2,1,0:T(8,128)(2,1)} %param.15) | copy-start | bytes 3145732
  3.5 74.4 %all-to-all-start = ((bf16[8,4,64,256]{3,2,1,0:T(8,128)(2,1)}), bf16[8,4,64,256]{3,2,1,0:T(8,128)(2,1)S(1)}, u32[]{:S(2)}, u32[]{:S(2)}) async-start(bf16[8,4,64,256]{3,2,1,0:T(8,128)(2,1)} %bitcast.1), calls=%async_computation | async-start | bytes 2097152 | tf_op jit(solution)/shard_map/all_to_all | solution.py:372
  77.9 3.5 %copy-start.2 = (bf16[8,4,64,256]{3,2,1,0:T(8,128)(2,1)}, bf16[8,4,64,256]{3,2,1,0:T(8,128)(2,1)S(1)}, u32[]{:S(2)}) copy-start(bf16[8,4,64,256]{3,2,1,0:T(8,128)(2,1)S(1)} %all-to-all-done.x_ref) | copy-start | bytes 3145732
  77.9 29.3 %all-to-all-start.2 = ((bf16[8,2,4,32,128]{4,3,2,1,0:T(8,128)(2,1)}), bf16[8,2,4,32,128]{4,3,2,1,0:T(8,128)(2,1)S(1)}, u32[]{:S(2)}, u32[]{:S(2)}) async-start(bf16[8,2,4,32,128]{4,3,2,1,0:T(8,128)(2,1)} %bitcast.29), calls=%async_computation.2 | async-start | bytes 1048576 | tf_op jit(solution)/shard_map/all_to_all | solution.py:387
  107.2 5.6 %copy-start.4 = (bf16[8,2,4,32,128]{4,3,2,1,0:T(8,128)(2,1)}, bf16[8,2,4,32,128]{4,3,2,1,0:T(8,128)(2,1)S(1)}, u32[]{:S(2)}) copy-start(bf16[8,2,4,32,128]{4,3,2,1,0:T(8,128)(2,1)S(1)} %all-to-all-done.2) | copy-start | bytes 1572868
  107.2 65.3 %all-to-all-start.1 = ((bf16[8,4,64,256]{3,2,1,0:T(8,128)(2,1)}), bf16[8,4,64,256]{3,2,1,0:T(8,128)(2,1)S(1)}, u32[]{:S(2)}, u32[]{:S(2)}) async-start(bf16[8,4,64,256]{3,2,1,0:T(8,128)(2,1)} %bitcast.5), calls=%async_computation.1 | async-start | bytes 2097152 | tf_op jit(solution)/shard_map/all_to_all | solution.py:372
  172.5 1.0 copy-start
  228.3 15.9 %all-to-all-start.4 = ((bf16[8,4,64,256]{3,2,1,0:T(8,128)(2,1)}), bf16[8,4,64,256]{3,2,1,0:T(8,128)(2,1)S(1)}, u32[]{:S(2)}, u32[]{:S(2)}) async-start(bf16[8,4,64,256]{3,2,1,0:T(8,128)(2,1)} %get-tuple-element.21), calls=%async_computation.4 | async-start | bytes 2097152 | tf_op jit(solution)/shard_map/all_to_all | solution.py:375

commit v3 on v2

--- a/solution.py
+++ b/solution.py
@@ -45,22 +45,117 @@
     return jnp.concatenate(parts, axis=0)
 
 
-def fwd_kernel(x_ref, live_ref, wq, wk, wv, wg, we, wl, wr,
-               p_ref, o_ref, g_ref, a_ref, l_ref, r_ref,
-               wt, wlt, bias_s):
+MESH = pl.DeviceIdType.MESH
+
+
+def remote(src, dst, send, recv, dep, res):
+    return pltpu.make_async_remote_copy(src_ref=src, dst_ref=dst, send_sem=send, recv_sem=recv,
+                                        device_id={"dep": dep, "res": res}, device_id_type=MESH)
+
+
+def greet(peers):
+    bar = pltpu.get_barrier_semaphore()
+    for dep, res in peers:
+        pl.semaphore_signal(bar, inc=1, device_id={"dep": dep, "res": res}, device_id_type=MESH)
+    pl.semaphore_wait(bar, len(peers))
+
+
+def fwd_kernel(hx, ux, px, live_in, wq, wk, wv, wg, we, wl, wr,
+               x_ref, p_ref, o_ref, g_ref, a_ref, l_ref, r_ref, up_out, pd_out, rc_ref, live_out,
+               wt, wlt, bias_s, xbuf, lbuf, livet, jbuf, mine, ustage, pstage,
+               xs, xr, us, ur, ps, pr, ls, lr, js, jr, own):
     k = pl.program_id(0)
+    d = lax.axis_index("dep")
+    r = lax.axis_index("res")
+
+    def dep_at(n):
+        return lax.rem(d + n, 8)
+
+    def res_at(n):
+        return lax.rem(r + n, 16)
+
+    def x_copy(c, n):
+        return remote(hx.at[dep_at(n), c], xbuf.at[c, d], xs.at[c, n], xr.at[c, n], dep_at(n), r)
+
+    def up_copy(n):
+        return remote(ux.at[dep_at(n)], up_out.at[d], us.at[n], ur.at[n], dep_at(n), r)
+
+    def pd_copy(n):
+        return remote(px.at[dep_at(n)], pd_out.at[d], ps.at[n], pr.at[n], dep_at(n), r)
+
+    def live_copy(n):
+        return remote(live_in, lbuf.at[d], ls.at[n], lr.at[n], dep_at(n), r)
+
+    def row_copy(n):
+        return remote(mine, jbuf.at[r], js.at[n], jr.at[n], d, res_at(n))
+
+    def own_x(c):
+        return pltpu.make_async_copy(hx.at[d, c], xbuf.at[c, d], own.at[c])
+
+    own_up = pltpu.make_async_copy(ux.at[d], ustage, own.at[4])
+    own_pd = pltpu.make_async_copy(px.at[d], pstage, own.at[5])
+    own_up2 = pltpu.make_async_copy(ustage, up_out.at[d], own.at[6])
+    own_pd2 = pltpu.make_async_copy(pstage, pd_out.at[d], own.at[7])
 
     @pl.when(k == 0)
     def _():
+        for c in range(4):
+            own_x(c).start()
+        own_up.start()
+        own_pd.start()
+        greet([(dep_at(n), r) for n in range(1, 8)] + [(d, res_at(n)) for n in range(1, 16)])
+        for n in range(1, 8):
+            live_copy(n).start()
+        for c in range(4):
+            for n in range(1, 8):
+                x_copy(c, n).start()
+        for n in range(1, 8):
+            pd_copy(n).start()
+        for n in range(1, 8):
+            up_copy(n).start()
+        lbuf[d] = live_in[...]
         for n, w in enumerate((wq, wv, wg, we)):
             wt[n] = w[...].T
         wlt[0] = wl[...].T
         wlt[1] = wr[...].T
-        b = (live_ref[...] - 1.0) * BIG
-        b = jnp.concatenate([b, jnp.zeros((120, N), f32)], axis=0)
-        bias_s[...] = b.T.astype(bf16)
-
-    xin = x_ref[...].reshape(N, F)
+        for n in range(1, 8):
+            live_copy(n).wait_recv()
+        live = lbuf[...].reshape(N, 128).astype(f32)
+        bias_s[...] = ((live - 1.0) * BIG).astype(bf16)
+        livet[...] = live.T
+        rows = [livet[pl.ds(4 * d + n, 1), :] for n in range(4)]
+        held = jnp.concatenate(rows + [jnp.zeros((4, N), f32)], axis=0)
+        mine[...] = held
+        live_out[...] = held
+        jbuf[r] = held
+        for n in range(1, 16):
+            row_copy(n).start()
+
+    @pl.when(k == 1)
+    def _():
+        own_up.wait()
+        own_pd.wait()
+        own_up2.start()
+        own_pd2.start()
+
+    @pl.when(k == 3)
+    def _():
+        for n in range(1, 16):
+            row_copy(n).wait_recv()
+        counts = mm(jbuf[...].reshape(128, N).astype(bf16), lbuf[...].reshape(N, 128))
+        rec = 1.0 / (0.001 + counts)
+        for n in range(8):
+            pieces = []
+            for j in range(8):
+                at = 16 * n + 8 * (j // 4) + j % 4
+                pieces.append(rec[at:at + 1, :CW])
+            rc_ref[n:n + 1, :] = jnp.concatenate(pieces, axis=1)
+
+    own_x(k).wait()
+    for n in range(1, 8):
+        x_copy(k, n).wait_recv()
+    xin = xbuf[k].reshape(N, F)
+    x_ref[...] = xin.reshape(x_ref.shape)
     xhat, _ = norm(xin.astype(f32), 1)
     xb = xhat.astype(bf16)
     xbt = xb.T
@@ -69,7 +164,7 @@
     kk = mm(xb, wk[...]).astype(bf16)
     gt = jax.nn.sigmoid(mm(wt[2], xbt))
     g_ref[0] = gt
-    extra = (lax.broadcasted_iota(jnp.int32, (128, N), 0) == k).astype(f32).astype(bf16)
+    extra = (lax.broadcasted_iota(jnp.int32, (128, N), 0) == 4 * d + k).astype(f32).astype(bf16)
     bias = bias_s[...]
     for h in range(H):
         grp = h // 4
@@ -87,27 +182,62 @@
     a_ref[0] = after
     yhat, _ = norm(after.astype(f32), 0)
     yb = yhat.astype(bf16)
-    live = live_ref[pl.ds(k, 1), :]
+    live = livet[pl.ds(4 * d + k, 1), :]
     l_ref[0] = (mm(wlt[0], yb) * live).astype(bf16)
     r_ref[0] = (mm(wlt[1], yb) * live).astype(bf16)
 
-
-def mid_kernel(a_ref, up_ref, lg_ref, rg_ref, wl, wr, it_ref, i_ref):
-    yhat, inv = norm(a_ref[0].astype(f32), 0)
+    @pl.when(k == 3)
+    def _():
+        for n in range(1, 8):
+            pd_copy(n).wait_recv()
+            up_copy(n).wait_recv()
+        own_up2.wait()
+        own_pd2.wait()
+        for n in range(1, 8):
+            live_copy(n).wait_send()
+            pd_copy(n).wait_send()
+            up_copy(n).wait_send()
+            for c in range(4):
+                x_copy(c, n).wait_send()
+        for n in range(1, 16):
+            row_copy(n).wait_send()
+
+
+def bwd_kernel(x_ref, up_ref, at_ref, lg_ref, rg_ref, p_ref, o_ref, g_ref, wq, wk, wv, wg, we, wl, wr,
+               out_g, out_i, wkt, acc_q, sbuf, ss, rs, own):
+    k = pl.program_id(0)
+    d = lax.axis_index("dep")
+    r = lax.axis_index("res")
+    outs = (out_g, out_i)
+
+    def dep_at(n):
+        return lax.rem(d + n, 8)
+
+    def send(which, c, n):
+        return remote(sbuf.at[which, c, dep_at(n)], outs[which].at[d, c],
+                      ss.at[which, c, n], rs.at[which, c, n], dep_at(n), r)
+
+    def keep(which, c):
+        return pltpu.make_async_copy(sbuf.at[which, c, d], outs[which].at[d, c], own.at[which, c])
+
+    def ship(which, value):
+        sbuf[which, k] = value.T.reshape(8, 64, F)
+        for n in range(1, 8):
+            send(which, k, n).start()
+        keep(which, k).start()
+
+    @pl.when(k == 0)
+    def _():
+        wkt[...] = wk[...].T
+        greet([(dep_at(n), r) for n in range(1, 8)])
+
+    yhat, yinv = norm(at_ref[0].astype(f32), 0)
     dy = mm(wl[...], lg_ref[0]) + mm(wr[...], rg_ref[0])
     m1 = jnp.mean(dy, 0, keepdims=True)
     m2 = jnp.mean(dy * yhat, 0, keepdims=True)
     upt = up_ref[...].reshape(N, F).T.astype(f32)
-    out = (inv * (dy - m1 - yhat * m2) + upt).astype(bf16)
-    it_ref[0] = out
-    i_ref[...] = out.T.reshape(i_ref.shape)
-
-
-def bwd_kernel(x_ref, d_ref, p_ref, o_ref, g_ref, wq, wk, wv, wg, we,
-               out_ref, wkt, acc_k, acc_v, acc_q):
-    @pl.when(pl.program_id(0) == 0)
-    def _():
-        wkt[...] = wk[...].T
+    dt = (yinv * (dy - m1 - yhat * m2) + upt).astype(bf16)
+    ship(1, dt)
 
     xin = x_ref[...].reshape(N, F)
     xhat, _ = norm(xin.astype(f32), 1)
@@ -118,7 +248,6 @@
     kt = mm(wkt[...], xbt).astype(bf16)
     gt = g_ref[0]
     ot = o_ref[0]
-    dt = d_ref[0]
     dg = mm(we[...], dt).astype(bf16).astype(f32)
     dot_ = (dg * gt).astype(bf16)
     dpre = (dg * ot * gt * (1.0 - gt)).astype(bf16)
@@ -156,7 +285,16 @@
     m2 = jnp.mean(dx * xh, 0, keepdims=True)
     dln = (inv * (dx - m1 - xh * m2)).astype(bf16)
     out = (dt.astype(f32) + dln.astype(f32)).astype(bf16)
-    out_ref[...] = out.T.reshape(out_ref.shape)
+    ship(0, out)
+
+    @pl.when(k == 3)
+    def _():
+        for which in range(2):
+            for c in range(4):
+                keep(which, c).wait()
+                for n in range(1, 8):
+                    send(which, c, n).wait_recv()
+                    send(which, c, n).wait_send()
 
 
 def whole(shape):
@@ -168,69 +306,48 @@
 
 
 COLS = pl.BlockSpec((8, 1, 64, F), lambda k: (0, k, 0, 0))
-PARAMS = pltpu.CompilerParams(vmem_limit_bytes=60 * 1024 * 1024, dimension_semantics=("arbitrary",))
-
-
-def fwd(x, livet, wq, wk, wv, wg, we, wl, wr):
-    C = x.shape[1]
+ANY = pl.BlockSpec(memory_space=pl.ANY)
+
+
+def fwd(hx, ux, px, live, wq, wk, wv, wg, we, wl, wr):
     sd = jax.ShapeDtypeStruct
+    V = pltpu.VMEM
+    dma = pltpu.SemaphoreType.DMA
     return pl.pallas_call(
         fwd_kernel,
-        grid=(C,),
-        in_specs=[COLS, whole((8, N))] + [whole((F, F))] * 5 + [whole((F, CW))] * 2,
-        out_specs=[percol((H, N, N)), percol((F, N)), percol((F, N)), percol((F, N)), percol((CW, N)), percol((CW, N))],
-        out_shape=[sd((C, H, N, N), bf16), sd((C, F, N), f32), sd((C, F, N), f32), sd((C, F, N), bf16), sd((C, CW, N), bf16), sd((C, CW, N), bf16)],
-        scratch_shapes=[pltpu.VMEM((4, F, F), bf16), pltpu.VMEM((2, CW, F), bf16), pltpu.VMEM((N, 128), bf16)],
-        compiler_params=PARAMS,
+        grid=(4,),
+        in_specs=[ANY] * 3 + [whole((64, 128))] + [whole((F, F))] * 5 + [whole((F, CW))] * 2,
+        out_specs=[COLS, percol((H, N, N)), percol((F, N)), percol((F, N)), percol((F, N)), percol((CW, N)),
+                   percol((CW, N)), ANY, ANY, whole((8, 256)), whole((8, N))],
+        out_shape=[sd((8, 4, 64, F), bf16), sd((4, H, N, N), bf16), sd((4, F, N), f32), sd((4, F, N), f32),
+                   sd((4, F, N), bf16), sd((4, CW, N), bf16), sd((4, CW, N), bf16),
+                   sd(ux.shape, bf16), sd(px.shape, bf16), sd((8, 256), f32), sd((8, N), f32)],
+        scratch_shapes=[V((4, F, F), bf16), V((2, CW, F), bf16), V((N, 128), bf16), V((4, 8, 64, F), bf16),
+                        V((8, 64, 128), bf16), V((128, N), f32), V((16, 8, N), f32), V((8, N), f32), V(ux.shape[1:], bf16),
+                        V(px.shape[1:], bf16), dma((4, 8)), dma((4, 8))] + [dma((8,))] * 6 + [dma((16,))] * 2 + [dma((8,))],
+        compiler_params=pltpu.CompilerParams(vmem_limit_bytes=60 * 1024 * 1024, collective_id=2, has_side_effects=True,
+                                             dimension_semantics=("arbitrary",)),
         name="attention_forward",
-        cost_estimate=pl.CostEstimate(flops=20_000_000_000, bytes_accessed=30_000_000, transcendentals=8_000_000),
-    )(x, livet, wq, wk, wv, wg, we, wl, wr)
-
-
-def mid(at, up, lg, rg, wl, wr):
-    C = at.shape[0]
+    )(hx, ux, px, live, wq, wk, wv, wg, we, wl, wr)
+
+
+def bwd(x, up, at, lg, rg, p, o, g, wq, wk, wv, wg, we, wl, wr):
     sd = jax.ShapeDtypeStruct
-    return pl.pallas_call(
-        mid_kernel,
-        grid=(C,),
-        in_specs=[percol((F, N)), COLS, percol((CW, N)), percol((CW, N)), whole((F, CW)), whole((F, CW))],
-        out_specs=[percol((F, N)), COLS],
-        out_shape=[sd((C, F, N), bf16), sd((8, C, 64, F), bf16)],
-        compiler_params=PARAMS,
-        name="middle",
-        cost_estimate=pl.CostEstimate(flops=500_000_000, bytes_accessed=5_000_000, transcendentals=0),
-    )(at, up, lg, rg, wl, wr)
-
-
-def bwd(x, dt, p, o, g, wq, wk, wv, wg, we):
-    C = x.shape[1]
-    sd = jax.ShapeDtypeStruct
+    V = pltpu.VMEM
+    dma = pltpu.SemaphoreType.DMA
     return pl.pallas_call(
         bwd_kernel,
-        grid=(C,),
-        in_specs=[COLS, percol((F, N)), percol((H, N, N)), percol((F, N)), percol((F, N))] + [whole((F, F))] * 5,
-        out_specs=COLS,
-        out_shape=sd((8, C, 64, F), bf16),
-        scratch_shapes=[pltpu.VMEM((F, F), bf16), pltpu.VMEM((N, F), f32), pltpu.VMEM((N, F), f32), pltpu.VMEM((F, N), f32)],
-        compiler_params=PARAMS,
+        grid=(4,),
+        in_specs=[COLS, COLS, percol((F, N)), percol((CW, N)), percol((CW, N)), percol((H, N, N)), percol((F, N)),
+                  percol((F, N))] + [whole((F, F))] * 5 + [whole((F, CW))] * 2,
+        out_specs=[ANY, ANY],
+        out_shape=[sd((8, 4, 64, F), bf16)] * 2,
+        scratch_shapes=[V((F, F), bf16), V((F, N), f32), V((2, 4, 8, 64, F), bf16),
+                        dma((2, 4, 8)), dma((2, 4, 8)), dma((2, 4))],
+        compiler_params=pltpu.CompilerParams(vmem_limit_bytes=60 * 1024 * 1024, collective_id=3, has_side_effects=True,
+                                             dimension_semantics=("arbitrary",)),
         name="attention_backward",
-        cost_estimate=pl.CostEstimate(flops=40_000_000_000, bytes_accessed=30_000_000, transcendentals=0),
-    )(x, dt, p, o, g, wq, wk, wv, wg, we)
-
-
-MESH = pl.DeviceIdType.MESH
-
-
-def remote(src, dst, send, recv, dep, res):
-    return pltpu.make_async_remote_copy(src_ref=src, dst_ref=dst, send_sem=send, recv_sem=recv,
-                                        device_id={"dep": dep, "res": res}, device_id_type=MESH)
-
-
-def greet(peers):
-    bar = pltpu.get_barrier_semaphore()
-    for dep, res in peers:
-        pl.semaphore_signal(bar, inc=1, device_id={"dep": dep, "res": res}, device_id_type=MESH)
-    pl.semaphore_wait(bar, len(peers))
+    )(x, up, at, lg, rg, p, o, g, wq, wk, wv, wg, we, wl, wr)
 
 
 def opm_kernel(lt, rt, pd, rc, wo, live, lo, ro,
@@ -364,34 +481,19 @@
 
 
 def on_device(msa, present, pair, upstream, wq, wk, wv, wg, we, wl, wr, wo):
-    d = lax.axis_index("dep")
-    D = lax.axis_size("dep")
-
-    def to_columns(a):
-        a = a.transpose(1, 0, 2).reshape(D, 4, 64, F)
-        return lax.all_to_all(a, "dep", 0, 0, tiled=True)
-
-    def to_rows(a):
-        a = lax.all_to_all(a, "dep", 0, 0, tiled=True)
-        return a.reshape(4 * D, 64, F).transpose(1, 0, 2)
-
-    x = to_columns(msa)
-    live_b = present.T.astype(bf16)
-    live_i = lax.all_gather(live_b, "dep", axis=1, tiled=True)
-    live_own = lax.dynamic_slice_in_dim(live_i, 4 * d, 4, 0)
-    live_j = lax.all_gather(live_own, "res", axis=0, tiled=True)
-    counts = mmt(live_j, live_i)
-    recip = 1.0 / (0.001 + counts)
-    up = to_columns(upstream)
-    pd = pair.reshape(32, 2, D, 4, CZ).transpose(2, 1, 3, 0, 4)
-    pd = lax.all_to_all(pd, "dep", 0, 0, tiled=True)
-    live4 = live_own.astype(f32)
-    livet = jnp.pad(live4, ((0, 4), (0, 0)))
-    p, o, g, at, lt, rt = fwd(x, livet, wq, wk, wv, wg, we, wl, wr)
-    lg, rg = opm(lt.reshape(4 * CW, N), rt.reshape(4 * CW, N), pd.reshape(-1, CZ), recip.reshape(8, 256), wo, livet)
-    dt, inter = mid(at, up, lg, rg, wl, wr)
-    grad = bwd(x, dt, p, o, g, wq, wk, wv, wg, we)
-    return to_rows(grad), to_rows(inter)
+    def by_column(a):
+        return a.transpose(1, 0, 2).reshape(8, 4, 64, F)
+
+    def by_row(a):
+        return a.reshape(32, 64, F).transpose(1, 0, 2)
+
+    live = jnp.pad(present.astype(bf16), ((0, 0), (0, 96)))
+    pd = pair.reshape(32, 2, 8, 4, CZ).transpose(2, 1, 3, 0, 4)
+    x, p, o, g, at, lt, rt, up, pd, recip, livet = fwd(
+        by_column(msa), by_column(upstream), pd, live, wq, wk, wv, wg, we, wl, wr)
+    lg, rg = opm(lt.reshape(4 * CW, N), rt.reshape(4 * CW, N), pd.reshape(-1, CZ), recip, wo, livet)
+    grad, inter = bwd(x, up, at, lg, rg, p, o, g, wq, wk, wv, wg, we, wl, wr)
+    return by_row(grad), by_row(inter)
 
 
 def solution(mesh):

time: 246 us -> 167 us (0.68)
  blocking collectives: 86.6 us -> 0 us
  Pallas kernels: 116 us -> 151 us
  starting transfers between devices: 19.1 us -> 0 us
  waiting for transfers between devices: 10.8 us -> 0 us
    all_gather x2 -> x0, blocking collectives: 62 us -> none  [the longest x1 37.6 us: on_device(): live_i = lax.all_gather(live_b, 'dep', axis=1, tiled=True)]
    pallas_call x3 -> x2, Pallas kernels: 56 us -> 94 us  [the longest x1 53.3 us: fwd(): pl.pallas_call(fwd_kernel, grid=(4,), in_specs=[ANY] * 3 + [whole((64, 12...]
    all_to_all x1 -> x0, blocking collectives: 24.6 us -> none  [to_rows(): a = lax.all_to_all(a, 'dep', 0, 0, tiled=True)]
    all_to_all x4 -> x0, starting transfers between devices: 19.1 us -> none  [the longest x2 12.1 us: to_columns(): return lax.all_to_all(a, 'dep', 0, 0, tiled=True)]
    all_to_all x4 -> x0, waiting for transfers between devices: 10.8 us -> none  [the longest x1 10.8 us: to_rows(): a = lax.all_to_all(a, 'dep', 0, 0, tiled=True)]
    transpose x2 -> x3, local copies, waits for them, and re-layouts: 4.39 us -> 8.36 us  [the longest x2 4.33 us: by_column(): return a.transpose(1, 0, 2).reshape(8, 4, 64, F)]
    pallas_call x1, Pallas kernels: 59.7 us -> 56.9 us  [opm(): pl.pallas_call(opm_kernel, in_specs=[vm] * 6, out_specs=[vm] * 2, out_sha...]
    reshape x4 -> x1, local copies, waits for them, and re-layouts: 4.96 us -> 2.22 us  [on_device(): pd = pair.reshape(32, 2, 8, 4, CZ).transpose(2, 1, 3, 0, 4)]
  transfers between devices with their start and end apart: 4 -> 0, of which waited for: 1 -> 0; matrix products, arithmetic and copies ran while one was open for 3% -> 0% of each run, Pallas kernels for 35% -> 0%
where the time goes in v3:
time: 167 us
  Pallas kernels  151 us (90%)
  local copies, waits for them, and re-layouts  14.2 us (9%)
    pallas_call x1, Pallas kernels, opm(): pl.pallas_call(opm_kernel, in_specs=[vm] * 6, out_specs=[vm] * 2, out_sha...  56.9 us
    pallas_call x1, Pallas kernels, fwd(): pl.pallas_call(fwd_kernel, grid=(4,), in_specs=[ANY] * 3 + [whole((64, 12...  53.3 us
    pallas_call x1, Pallas kernels, bwd(): pl.pallas_call(bwd_kernel, grid=(4,), in_specs=[COLS, COLS, percol((F, N)...  40.7 us
    transpose x2, local copies, waits for them, and re-layouts, by_column(): return a.transpose(1, 0, 2).reshape(8, 4, 64, F)  4.33 us
    transpose x1, local copies, waits for them, and re-layouts, by_row(): return a.reshape(32, 64, F).transpose(1, 0, 2)  4.03 us

profile of v3, /device:TPU:0, one launch (start us, length us, event | category | flops | bytes accessed | tf_op | source)
XLA Modules:
  0.0 166.6 jit_solution(9052314091802598363)
XLA Ops:
  0.6 0.0 copy-start
  0.6 0.8 convert_element_type.5
  1.4 0.1 copy.38
  1.5 0.6 pad.4.live_in
  2.2 1.4 copy.39.wl
  3.6 1.4 copy.40.wr
  5.1 2.2 %copy.50 = bf16[32,2,8,4,128]{4,0,3,1,2:T(8,128)(2,1)} copy(bf16[32,2,8,4,128]{4,3,2,1,0:T(4,128)(2,1)} %bitcast.24) | data formatting | bytes 1048576 | tf_op jit(solution)/shard_map/reshape | solution.py:491
  7.3 2.8 %copy.34 = bf16[32,64,256]{2,1,0:T(8,128)(2,1)} copy(bf16[32,64,256]{2,0,1:T(8,128)(2,1)} %bitcast.20) | data formatting | bytes 2097152 | tf_op jit(solution)/shard_map/transpose | solution.py:485
  10.0 0.0 copy-done
  10.0 1.6 copy.35
  11.6 53.3 %attention_forward.1 = (bf16[8,4,64,256]{3,2,1,0:T(8,128)(2,1)}, bf16[4,8,512,512]{3,2,1,0:T(8,128)(2,1)}, f32[4,256,512]{2,1,0:T(8,128)}, f32[4,256,512]{2,1,0:...) custom-call(bf16[8,4,64,256]{3,2,1,0:T(8,128)(2,1)} %bitcast.17, ...), custom_call_target="tpu_custom_call" | custom-call | tf_op jit(solution)/shard_map/attention_forward/pallas_call | solution.py:316
  64.9 56.9 %outer_product.1 = (bf16[4,32,512]{2,1,0:T(8,128)(2,1)}, bf16[4,32,512]{2,1,0:T(8,128)(2,1)}) custom-call(bf16[128,512]{1,0:T(8,128)(2,1)} %bitcast.26, bf16[128,512]{1,0:T(8,128)(2,1)} %bitcast.27, bf16[2048,128]{1,0:T(8,128)(2,1)} %bitcast.25, f32[8,256]{1,0:T(8,128)} %get-tuple-element.23.rc, bf16[1024,128]{1,0:T(8,128)(2,1)} %wo.1, ...), custom_call_target="tpu_custom_call" | custom-call | flops 10000000000 | bytes 10000000 | tf_op jit(solution)/shard_map/outer_product/pallas_call | solution.py:469
  121.8 40.7 %attention_backward.1 = (bf16[8,4,64,256]{3,2,1,0:T(8,128)(2,1)}, bf16[8,4,64,256]{3,2,1,0:T(8,128)(2,1)}) custom-call(bf16[8,4,64,256]{3,2,1,0:T(8,128)(2,1)} %get-tuple-element.17.x_ref, bf16[8,4,64,256]{3,2,1,0:T(8,128)(2,1)} %get-tuple-element.18.up_ref, bf16[4,256,512]{2,1,0:T(8,128)(2,1)} %get-tuple-element.19.at_ref, ...), custom_call_target="tpu_custom_call" | custom-call | tf_op jit(solution)/shard_map/attention_backward/pallas_call | solution.py:338
  162.6 4.0 %copy_bitcast_fusion = (bf16[64,32,256]{2,1,0:T(8,128)(2,1)}, bf16[64,32,256]{2,1,0:T(8,128)(2,1)}) fusion(bf16[32,64,256]{2,1,0:T(8,128)(2,1)} %bitcast.23, bf16[32,64,256]{2,1,0:T(8,128)(2,1)} %bitcast.22), kind=kLoop, calls=%fused_computation | loop fusion | bytes 4194304 | tf_op jit(solution)/shard_map/transpose | solution.py:488
Async XLA Ops:
  0.6 9.4 %copy-start = (bf16[64,32,256]{2,1,0:T(8,128)(2,1)S(1)}, bf16[64,32,256]{2,1,0:T(8,128)(2,1)}, u32[]{:S(2)}) copy-start(bf16[64,32,256]{2,1,0:T(8,128)(2,1)} %param.15) | copy-start | bytes 3145732

commit v4 on v3

--- a/solution.py
+++ b/solution.py
@@ -62,7 +62,7 @@
 
 def fwd_kernel(hx, ux, px, live_in, wq, wk, wv, wg, we, wl, wr,
                x_ref, p_ref, o_ref, g_ref, a_ref, l_ref, r_ref, up_out, pd_out, rc_ref, live_out,
-               wt, wlt, bias_s, xbuf, lbuf, livet, jbuf, mine, ustage, pstage,
+               wt, bias_s, xbuf, lbuf, livet, jbuf, mine, ustage, pstage,
                xs, xr, us, ur, ps, pr, ls, lr, js, jr, own):
     k = pl.program_id(0)
     d = lax.axis_index("dep")
@@ -77,8 +77,8 @@
     def x_copy(c, n):
         return remote(hx.at[dep_at(n), c], xbuf.at[c, d], xs.at[c, n], xr.at[c, n], dep_at(n), r)
 
-    def up_copy(n):
-        return remote(ux.at[dep_at(n)], up_out.at[d], us.at[n], ur.at[n], dep_at(n), r)
+    def up_copy(c, n):
+        return remote(ux.at[dep_at(n), c], up_out.at[d, c], us.at[c, n], ur.at[c, n], dep_at(n), r)
 
     def pd_copy(n):
         return remote(px.at[dep_at(n)], pd_out.at[d], ps.at[n], pr.at[n], dep_at(n), r)
@@ -106,18 +106,11 @@
         greet([(dep_at(n), r) for n in range(1, 8)] + [(d, res_at(n)) for n in range(1, 16)])
         for n in range(1, 8):
             live_copy(n).start()
-        for c in range(4):
-            for n in range(1, 8):
-                x_copy(c, n).start()
-        for n in range(1, 8):
-            pd_copy(n).start()
-        for n in range(1, 8):
-            up_copy(n).start()
+        for n in range(1, 8):
+            x_copy(0, n).start()
         lbuf[d] = live_in[...]
         for n, w in enumerate((wq, wv, wg, we)):
             wt[n] = w[...].T
-        wlt[0] = wl[...].T
-        wlt[1] = wr[...].T
         for n in range(1, 8):
             live_copy(n).wait_recv()
         live = lbuf[...].reshape(N, 128).astype(f32)
@@ -130,16 +123,30 @@
         jbuf[r] = held
         for n in range(1, 16):
             row_copy(n).start()
+        for n in range(1, 8):
+            x_copy(0, n).wait_send()
+        for n in range(1, 8):
+            x_copy(1, n).start()
 
     @pl.when(k == 1)
     def _():
+        for n in range(1, 8):
+            x_copy(3, n).start()
         own_up.wait()
         own_pd.wait()
         own_up2.start()
         own_pd2.start()
 
+    @pl.when(k == 2)
+    def _():
+        for n in range(1, 8):
+            up_copy(0, n).start()
+
     @pl.when(k == 3)
     def _():
+        for c in (2, 3):
+            for n in range(1, 8):
+                up_copy(c, n).start()
         for n in range(1, 16):
             row_copy(n).wait_recv()
         counts = mm(jbuf[...].reshape(128, N).astype(bf16), lbuf[...].reshape(N, 128))
@@ -167,6 +174,21 @@
     extra = (lax.broadcasted_iota(jnp.int32, (128, N), 0) == 4 * d + k).astype(f32).astype(bf16)
     bias = bias_s[...]
     for h in range(H):
+        if h == 4:
+            @pl.when(k == 0)
+            def _():
+                for n in range(1, 8):
+                    x_copy(2, n).start()
+
+            @pl.when(k == 1)
+            def _():
+                for n in range(1, 8):
+                    pd_copy(n).start()
+
+            @pl.when(k == 2)
+            def _():
+                for n in range(1, 8):
+                    up_copy(1, n).start()
         grp = h // 4
         lhs = jnp.concatenate([kk[:, 128 * grp:128 * grp + 128], bias], axis=1)
         st = mm(lhs, spread(qt[DH * h:DH * h + DH], h, extra))
@@ -183,28 +205,30 @@
     yhat, _ = norm(after.astype(f32), 0)
     yb = yhat.astype(bf16)
     live = livet[pl.ds(4 * d + k, 1), :]
-    l_ref[0] = (mm(wlt[0], yb) * live).astype(bf16)
-    r_ref[0] = (mm(wlt[1], yb) * live).astype(bf16)
+    l_ref[0] = (mm(wl[...], yb) * live).astype(bf16)
+    r_ref[0] = (mm(wr[...], yb) * live).astype(bf16)
 
     @pl.when(k == 3)
     def _():
         for n in range(1, 8):
             pd_copy(n).wait_recv()
-            up_copy(n).wait_recv()
+            for c in range(4):
+                up_copy(c, n).wait_recv()
         own_up2.wait()
         own_pd2.wait()
         for n in range(1, 8):
             live_copy(n).wait_send()
             pd_copy(n).wait_send()
-            up_copy(n).wait_send()
             for c in range(4):
-                x_copy(c, n).wait_send()
+                up_copy(c, n).wait_send()
+                if c:
+                    x_copy(c, n).wait_send()
         for n in range(1, 16):
             row_copy(n).wait_send()
 
 
 def bwd_kernel(x_ref, up_ref, at_ref, lg_ref, rg_ref, p_ref, o_ref, g_ref, wq, wk, wv, wg, we, wl, wr,
-               out_g, out_i, wkt, acc_q, sbuf, ss, rs, own):
+               out_g, out_i, wkt, acc_q, dt_s, sbuf, ss, rs, own):
     k = pl.program_id(0)
     d = lax.axis_index("dep")
     r = lax.axis_index("res")
@@ -220,24 +244,25 @@
     def keep(which, c):
         return pltpu.make_async_copy(sbuf.at[which, c, d], outs[which].at[d, c], own.at[which, c])
 
-    def ship(which, value):
-        sbuf[which, k] = value.T.reshape(8, 64, F)
-        for n in range(1, 8):
-            send(which, k, n).start()
-        keep(which, k).start()
+    def ship(which, c, value):
+        sbuf[which, c] = value.T.reshape(8, 64, F)
+        for n in range(1, 8):
+            send(which, c, n).start()
+        keep(which, c).start()
 
     @pl.when(k == 0)
     def _():
         wkt[...] = wk[...].T
+        wlt, wrt = wl[...].T, wr[...].T
         greet([(dep_at(n), r) for n in range(1, 8)])
-
-    yhat, yinv = norm(at_ref[0].astype(f32), 0)
-    dy = mm(wl[...], lg_ref[0]) + mm(wr[...], rg_ref[0])
-    m1 = jnp.mean(dy, 0, keepdims=True)
-    m2 = jnp.mean(dy * yhat, 0, keepdims=True)
-    upt = up_ref[...].reshape(N, F).T.astype(f32)
-    dt = (yinv * (dy - m1 - yhat * m2) + upt).astype(bf16)
-    ship(1, dt)
+        for c in range(4):
+            yhat, yinv = norm(at_ref[c].astype(f32), 0)
+            dy = mm(wlt, lg_ref[c]) + mm(wrt, rg_ref[c])
+            m1 = jnp.mean(dy, 0, keepdims=True)
+            m2 = jnp.mean(dy * yhat, 0, keepdims=True)
+            upt = up_ref[:, c].reshape(N, F).T.astype(f32)
+            dt_s[c] = (yinv * (dy - m1 - yhat * m2) + upt).astype(bf16)
+            ship(1, c, dt_s[c])
 
     xin = x_ref[...].reshape(N, F)
     xhat, _ = norm(xin.astype(f32), 1)
@@ -248,6 +273,7 @@
     kt = mm(wkt[...], xbt).astype(bf16)
     gt = g_ref[0]
     ot = o_ref[0]
+    dt = dt_s[k]
     dg = mm(we[...], dt).astype(bf16).astype(f32)
     dot_ = (dg * gt).astype(bf16)
     dpre = (dg * ot * gt * (1.0 - gt)).astype(bf16)
@@ -285,7 +311,7 @@
     m2 = jnp.mean(dx * xh, 0, keepdims=True)
     dln = (inv * (dx - m1 - xh * m2)).astype(bf16)
     out = (dt.astype(f32) + dln.astype(f32)).astype(bf16)
-    ship(0, out)
+    ship(0, k, out)
 
     @pl.when(k == 3)
     def _():
@@ -316,15 +342,15 @@
     return pl.pallas_call(
         fwd_kernel,
         grid=(4,),
-        in_specs=[ANY] * 3 + [whole((64, 128))] + [whole((F, F))] * 5 + [whole((F, CW))] * 2,
+        in_specs=[ANY] * 3 + [whole((64, 128))] + [whole((F, F))] * 5 + [whole((CW, F))] * 2,
         out_specs=[COLS, percol((H, N, N)), percol((F, N)), percol((F, N)), percol((F, N)), percol((CW, N)),
                    percol((CW, N)), ANY, ANY, whole((8, 256)), whole((8, N))],
         out_shape=[sd((8, 4, 64, F), bf16), sd((4, H, N, N), bf16), sd((4, F, N), f32), sd((4, F, N), f32),
                    sd((4, F, N), bf16), sd((4, CW, N), bf16), sd((4, CW, N), bf16),
                    sd(ux.shape, bf16), sd(px.shape, bf16), sd((8, 256), f32), sd((8, N), f32)],
-        scratch_shapes=[V((4, F, F), bf16), V((2, CW, F), bf16), V((N, 128), bf16), V((4, 8, 64, F), bf16),
+        scratch_shapes=[V((4, F, F), bf16), V((N, 128), bf16), V((4, 8, 64, F), bf16),
                         V((8, 64, 128), bf16), V((128, N), f32), V((16, 8, N), f32), V((8, N), f32), V(ux.shape[1:], bf16),
-                        V(px.shape[1:], bf16), dma((4, 8)), dma((4, 8))] + [dma((8,))] * 6 + [dma((16,))] * 2 + [dma((8,))],
+                        V(px.shape[1:], bf16), dma((4, 8)), dma((4, 8)), dma((4, 8)), dma((4, 8))] + [dma((8,))] * 4 + [dma((16,))] * 2 + [dma((8,))],
         compiler_params=pltpu.CompilerParams(vmem_limit_bytes=60 * 1024 * 1024, collective_id=2, has_side_effects=True,
                                              dimension_semantics=("arbitrary",)),
         name="attention_forward",
@@ -338,11 +364,11 @@
     return pl.pallas_call(
         bwd_kernel,
         grid=(4,),
-        in_specs=[COLS, COLS, percol((F, N)), percol((CW, N)), percol((CW, N)), percol((H, N, N)), percol((F, N)),
-                  percol((F, N))] + [whole((F, F))] * 5 + [whole((F, CW))] * 2,
+        in_specs=[COLS, whole((8, 4, 64, F)), whole((4, F, N)), whole((4, CW, N)), whole((4, CW, N)), percol((H, N, N)), percol((F, N)),
+                  percol((F, N))] + [whole((F, F))] * 5 + [whole((CW, F))] * 2,
         out_specs=[ANY, ANY],
         out_shape=[sd((8, 4, 64, F), bf16)] * 2,
-        scratch_shapes=[V((F, F), bf16), V((F, N), f32), V((2, 4, 8, 64, F), bf16),
+        scratch_shapes=[V((F, F), bf16), V((F, N), f32), V((4, F, N), bf16), V((2, 4, 8, 64, F), bf16),
                         dma((2, 4, 8)), dma((2, 4, 8)), dma((2, 4))],
         compiler_params=pltpu.CompilerParams(vmem_limit_bytes=60 * 1024 * 1024, collective_id=3, has_side_effects=True,
                                              dimension_semantics=("arbitrary",)),
@@ -490,9 +516,9 @@
     live = jnp.pad(present.astype(bf16), ((0, 0), (0, 96)))
     pd = pair.reshape(32, 2, 8, 4, CZ).transpose(2, 1, 3, 0, 4)
     x, p, o, g, at, lt, rt, up, pd, recip, livet = fwd(
-        by_column(msa), by_column(upstream), pd, live, wq, wk, wv, wg, we, wl, wr)
+        by_column(msa), by_column(upstream), pd, live, wq, wk, wv, wg, we, wl.T, wr.T)
     lg, rg = opm(lt.reshape(4 * CW, N), rt.reshape(4 * CW, N), pd.reshape(-1, CZ), recip, wo, livet)
-    grad, inter = bwd(x, up, at, lg, rg, p, o, g, wq, wk, wv, wg, we, wl, wr)
+    grad, inter = bwd(x, up, at, lg, rg, p, o, g, wq, wk, wv, wg, we, wl.T, wr.T)
     return by_row(grad), by_row(inter)
 
 

time: 167 us -> 157 us (0.940)
  Pallas kernels: 151 us -> 144 us
  local copies, waits for them, and re-layouts: 14.2 us -> 11.3 us
    pallas_call x1, Pallas kernels: 56.9 us -> 52.8 us  [opm(): pl.pallas_call(opm_kernel, in_specs=[vm] * 6, out_specs=[vm] * 2, out_sha...]
    pallas_call x1, Pallas kernels: 53.3 us -> 49.7 us  [fwd(): pl.pallas_call(fwd_kernel, grid=(4,), in_specs=[ANY] * 3 + [whole((64, 12...]
    unnamed x4 -> x2, local copies, waits for them, and re-layouts: 2.89 us -> 0.01 us
where the time goes in v4:
time: 157 us
  Pallas kernels  144 us (92%)
  local copies, waits for them, and re-layouts  11.3 us (7%)
    pallas_call x1, Pallas kernels, opm(): pl.pallas_call(opm_kernel, in_specs=[vm] * 6, out_specs=[vm] * 2, out_sha...  52.8 us
    pallas_call x1, Pallas kernels, fwd(): pl.pallas_call(fwd_kernel, grid=(4,), in_specs=[ANY] * 3 + [whole((64, 12...  49.7 us
    pallas_call x1, Pallas kernels, bwd(): pl.pallas_call(bwd_kernel, grid=(4,), in_specs=[COLS, whole((8, 4, 64, F)...  41.5 us
    transpose x2, local copies, waits for them, and re-layouts, by_column(): return a.transpose(1, 0, 2).reshape(8, 4, 64, F)  4.33 us
    transpose x1, local copies, waits for them, and re-layouts, by_row(): return a.reshape(32, 64, F).transpose(1, 0, 2)  4.03 us

profile of v4, /device:TPU:0, one launch (start us, length us, event | category | flops | bytes accessed | tf_op | source)
XLA Modules:
  0.0 156.8 jit_solution(17929363027942157033)
XLA Ops:
  0.6 0.0 copy-start
  0.6 0.8 convert_element_type.5
  1.4 0.1 copy.30
  1.5 0.6 pad.4.live_in
  2.2 2.2 %copy.38 = bf16[32,2,8,4,128]{4,0,3,1,2:T(8,128)(2,1)} copy(bf16[32,2,8,4,128]{4,3,2,1,0:T(4,128)(2,1)} %bitcast.26) | data formatting | bytes 1048576 | tf_op jit(solution)/shard_map/reshape | solution.py:517
  4.4 2.8 %copy.26 = bf16[32,64,256]{2,1,0:T(8,128)(2,1)} copy(bf16[32,64,256]{2,0,1:T(8,128)(2,1)} %bitcast.22) | data formatting | bytes 2097152 | tf_op jit(solution)/shard_map/transpose | solution.py:511
  7.2 0.0 copy-done
  7.2 1.6 copy.27
  8.7 49.7 %attention_forward.1 = (bf16[8,4,64,256]{3,2,1,0:T(8,128)(2,1)}, bf16[4,8,512,512]{3,2,1,0:T(8,128)(2,1)}, f32[4,256,512]{2,1,0:T(8,128)}, f32[4,256,512]{2,1,0:...) custom-call(bf16[8,4,64,256]{3,2,1,0:T(8,128)(2,1)} %bitcast.19, ...), custom_call_target="tpu_custom_call" | custom-call | tf_op jit(solution)/shard_map/attention_forward/pallas_call | solution.py:342
  58.5 52.8 %outer_product.1 = (bf16[4,32,512]{2,1,0:T(8,128)(2,1)}, bf16[4,32,512]{2,1,0:T(8,128)(2,1)}) custom-call(bf16[128,512]{1,0:T(8,128)(2,1)} %bitcast.32, bf16[128,512]{1,0:T(8,128)(2,1)} %bitcast.33, bf16[2048,128]{1,0:T(8,128)(2,1)} %bitcast.31, f32[8,256]{1,0:T(8,128)} %get-tuple-element.23.rc, bf16[1024,128]{1,0:T(8,128)(2,1)} %wo.1, ...), custom_call_target="tpu_custom_call" | custom-call | flops 10000000000 | bytes 10000000 | tf_op jit(solution)/shard_map/outer_product/pallas_call | solution.py:495
  111.2 41.5 %attention_backward.1 = (bf16[8,4,64,256]{3,2,1,0:T(8,128)(2,1)}, bf16[8,4,64,256]{3,2,1,0:T(8,128)(2,1)}) custom-call(bf16[8,4,64,256]{3,2,1,0:T(8,128)(2,1)} %get-tuple-element.17.x_ref, bf16[8,4,64,256]{3,2,1,0:T(8,128)(2,1)} %get-tuple-element.18.up_ref, bf16[4,256,512]{2,1,0:T(8,128)(2,1)} %get-tuple-element.19.at_ref, ...), custom_call_target="tpu_custom_call" | custom-call | tf_op jit(solution)/shard_map/attention_backward/pallas_call | solution.py:364
  152.8 4.0 %copy_bitcast_fusion = (bf16[64,32,256]{2,1,0:T(8,128)(2,1)}, bf16[64,32,256]{2,1,0:T(8,128)(2,1)}) fusion(bf16[32,64,256]{2,1,0:T(8,128)(2,1)} %bitcast.25, bf16[32,64,256]{2,1,0:T(8,128)(2,1)} %bitcast.24), kind=kLoop, calls=%fused_computation | loop fusion | bytes 4194304 | tf_op jit(solution)/shard_map/transpose | solution.py:514
Async XLA Ops:
  0.6 6.5 %copy-start = (bf16[64,32,256]{2,1,0:T(8,128)(2,1)S(1)}, bf16[64,32,256]{2,1,0:T(8,128)(2,1)}, u32[]{:S(2)}) copy-start(bf16[64,32,256]{2,1,0:T(8,128)(2,1)} %param.15) | copy-start | bytes 3145732

commit v5 on v4

--- a/solution.py
+++ b/solution.py
@@ -377,30 +377,52 @@
 
 
 def opm_kernel(lt, rt, pd, rc, wo, live, lo, ro,
-               perm, oc1, oc2, lbuf, rbuf, lsend, lrecv, psend, precv, rsend, rrecv, lacc, racc,
+               perm, oc1, oc2, lbuf, rbuf, lsend, lrecv, psend, precv, rsend, rrecv, both, lkeep, lacc,
                ls, lr, rs, rr, fs, fr, ps, pr, s2, r2, s3, r3):
     d = lax.axis_index("dep")
     r = lax.axis_index("res")
-    core = lax.rem(r, 2)
-    chip = r // 2
-    partner = 2 * chip + 1 - core
-
-    def dep_at(k):
-        return lax.rem(d + k, 8)
-
-    def chip_at(k):
-        return lax.rem(chip + k, 8)
-
-    greet([(dep_at(k), r) for k in range(1, 8)]
-          + [(d, 2 * chip_at(k) + core) for k in range(1, 8)] + [(d, partner)])
-
-    gl = [remote(lt, lbuf.at[d], ls.at[k], lr.at[k], dep_at(k), r) for k in range(1, 8)]
-    gr = [remote(rt, rbuf.at[r], rs.at[k], rr.at[k], d, 2 * chip_at(k) + core) for k in range(1, 8)]
-    first = remote(rt, rbuf.at[r], fs.at[0], fr.at[0], d, partner)
-    for a, b in zip(gl, gr):
-        b.start()
-        a.start()
-    first.start()
+    xl, z = d // 4, lax.rem(d, 4)
+    y, xh, core = r // 4, lax.rem(r // 2, 2), lax.rem(r, 2)
+
+    def dep_of(flip, step):
+        return 4 * lax.rem(xl + flip, 2) + lax.rem(z + step + 4, 4)
+
+    def chip_of(flip, step):
+        return 2 * lax.rem(y + step + 4, 4) + lax.rem(xh + flip, 2)
+
+    def res_of(flip, step):
+        return 2 * chip_of(flip, step) + core
+
+    partner = 2 * chip_of(0, 0) + 1 - core
+    greet([(dep_of(0, n), r) for n in range(1, 4)] + [(dep_of(1, 0), r)]
+          + [(d, res_of(0, n)) for n in range(1, 4)] + [(d, res_of(1, 0)), (d, partner)])
+
+    def left_copy(n):
+        if n == 0:
+            return remote(lt, lbuf.at[d], ls.at[0], lr.at[0], dep_of(1, 0), r)
+        if n < 4:
+            return remote(lt, lbuf.at[d], ls.at[n], lr.at[n], dep_of(0, n), r)
+        slot = dep_of(1, 0)
+        return remote(lbuf.at[slot], lbuf.at[slot], ls.at[n], lr.at[n], dep_of(0, n - 3), r)
+
+    def right_copy(n):
+        if n == 0:
+            return remote(rt, rbuf.at[r], rs.at[0], rr.at[0], d, res_of(1, 0))
+        if n < 4:
+            return remote(rt, rbuf.at[r], rs.at[n], rr.at[n], d, res_of(0, n))
+        slot = res_of(1, 0)
+        return remote(rbuf.at[slot], rbuf.at[slot], rs.at[n], rr.at[n], d, res_of(0, n - 3))
+
+    def across(n):
+        if n == 7:
+            return remote(rt, rbuf.at[r], fs.at[7], fr.at[7], d, partner)
+        slot = res_of(1, 0) if n == 0 else res_of(0, -n) if n < 4 else res_of(1, 3 - n)
+        return remote(rbuf.at[slot], rbuf.at[slot], fs.at[n], fr.at[n], d, partner)
+
+    for n in range(4):
+        left_copy(n).start()
+        right_copy(n).start()
+    across(7).start()
     lbuf[d] = lt[...]
     rbuf[r] = rt[...]
 
@@ -409,81 +431,111 @@
     hit = ((a // CW) == (b % CW)) & ((a % CW) == (b // CW))
     perm[...] = hit.astype(f32).astype(bf16)
 
-    def forward(k):
-        slot = 2 * lax.rem(chip + 8 - k, 8) + core
-        return remote(rbuf.at[slot], rbuf.at[slot], fs.at[k], fr.at[k], d, partner)
-
     def outer_step(n, carry):
         at = pl.multiple_of(256 * n, 256)
-        z = (mmt(wo[...], pd[pl.ds(at, 256), :]) * rc[pl.ds(n, 1), :]).astype(bf16)
+        zz = (mmt(wo[...], pd[pl.ds(at, 256), :]) * rc[pl.ds(n, 1), :]).astype(bf16)
         rows = []
         for j in range(8):
-            rows.append(jnp.concatenate([z[CW * c:CW * c + CW, CW * j:CW * j + CW] for c in range(CW)], axis=1))
-        y = mm(jnp.concatenate(rows, axis=0), perm[...]).astype(bf16)
-        oc1[pl.ds(at, 256), :] = y
-        oc2[:, pl.ds(at, 256)] = y.T
-
-        @pl.when(n > 0)
+            rows.append(jnp.concatenate([zz[CW * c:CW * c + CW, CW * j:CW * j + CW] for c in range(CW)], axis=1))
+        yy = mm(jnp.concatenate(rows, axis=0), perm[...]).astype(bf16)
+        oc1[pl.ds(at, 256), :] = yy
+        oc2[:, pl.ds(at, 256)] = yy.T
+
+        @pl.when(n == 1)
         def _():
-            remote(rt, rbuf.at[r], rs.at[n], rr.at[n], d, partner).wait_recv()
-            forward(n).start()
+            left_copy(0).wait_recv()
+            for i in range(4, 7):
+                left_copy(i).start()
+
+        @pl.when(n == 2)
+        def _():
+            right_copy(0).wait_recv()
+            for i in range(4, 7):
+                right_copy(i).start()
+            across(0).start()
+
+        @pl.when(n == 5)
+        def _():
+            for i in range(1, 4):
+                right_copy(i).wait_recv()
+                across(i).start()
         return carry
 
     lax.fori_loop(0, 8, outer_step, 0)
-    for c in gl:
-        c.wait_recv()
+    for n in range(1, 7):
+        left_copy(n).wait_recv()
+    for n in range(4, 7):
+        right_copy(n).wait_recv()
+        across(n).start()
+
+    order = [(1, 1), (1, 2), (1, 3), (1, 0), (0, 1), (0, 2), (0, 3), (0, 0)]
+
+    def pass_over(i):
+        return remote(psend.at[i], precv.at[i], ps.at[i], pr.at[i], d, partner)
+
+    def right_part(i):
+        target = res_of(1, 0) if i == 3 else res_of(0, order[i][1])
+        return remote(rsend.at[i], rrecv.at[i], s2.at[i], r2.at[i], d, target)
+
+    def left_part(i):
+        target = dep_of(1, 0) if i == 3 else dep_of(0, order[i][1])
+        return remote(lsend.at[i], lrecv.at[i], s3.at[i], r3.at[i], target, r)
+
+    mine = pl.ds(pl.multiple_of(128 * core, 128), 128)
+    theirs = pl.ds(pl.multiple_of(128 * (1 - core), 128), 128)
     lall = lbuf[...].reshape(1024, N)
-    part = []
-    for k in [1, 2, 3, 4, 5, 6, 7, 0]:
-        q = chip_at(k)
-        at = pl.multiple_of(256 * q + 128 * (1 - core), 128)
-        psend[k] = mm(oc1[pl.ds(at, 128), :], lall).astype(bf16)
-        c = remote(psend.at[k], precv.at[k], ps.at[k], pr.at[k], d, partner)
-        c.start()
-        part.append(c)
-    second = []
-    for k in [1, 2, 3, 4, 5, 6, 7, 0]:
-        q = chip_at(k)
-        at = pl.multiple_of(256 * q + 128 * core, 128)
-        own = mm(oc1[pl.ds(at, 128), :], lall)
-        remote(psend.at[k], precv.at[k], ps.at[k], pr.at[k], d, partner).wait_recv()
-        own = own + precv[k].astype(f32)
-        if k:
-            rsend[k] = own.astype(bf16)
-            c = remote(rsend.at[k], rrecv.at[k], s2.at[k], r2.at[k], d, 2 * q + core)
-            c.start()
-            second.append(c)
+    for i, (flip, step) in enumerate(order):
+        at = pl.multiple_of(256 * chip_of(flip, step), 256)
+        both[i] = mm(oc1[pl.ds(at, 256), :], lall)
+        psend[i] = both[i, theirs, :].astype(bf16)
+        pass_over(i).start()
+    for i in range(8):
+        pass_over(i).wait_recv()
+        own = both[i, mine, :] + precv[i].astype(f32)
+        if i in (3, 7):
+            both[i, mine, :] = own
         else:
-            racc[...] = own
-    first.wait_recv()
-    for k in range(1, 8):
-        forward(k).wait_recv()
+            rsend[i] = own.astype(bf16)
+            right_part(i).start()
+    for n in range(8):
+        across(n).wait_recv()
     rall = rbuf[...].reshape(2048, N)
-    third = []
-    for k in [1, 2, 3, 4, 5, 6, 7, 0]:
-        at = pl.multiple_of(128 * dep_at(k), 128)
+    for i, (flip, step) in enumerate(order):
+        at = pl.multiple_of(128 * dep_of(flip, step), 128)
         own = mm(oc2[pl.ds(at, 128), :], rall)
-        if k:
-            lsend[k] = own.astype(bf16)
-            c = remote(lsend.at[k], lrecv.at[k], s3.at[k], r3.at[k], dep_at(k), r)
-            c.start()
-            third.append(c)
+        if i == 3:
+            lkeep[...] = own
+        elif i == 7:
+            lacc[...] = own
         else:
-            lacc[...] = own
-    for c in second:
-        c.wait_recv()
-    racc[...] += jnp.sum(rrecv[1:8].astype(f32), 0)
+            lsend[i] = own.astype(bf16)
+            left_part(i).start()
+    for i in range(3):
+        right_part(i).wait_recv()
+    rsend[3] = (both[3, mine, :] + jnp.sum(rrecv[0:3].astype(f32), 0)).astype(bf16)
+    right_part(3).start()
+    for i in range(3):
+        left_part(i).wait_recv()
+    lsend[3] = (lkeep[...] + jnp.sum(lrecv[0:3].astype(f32), 0)).astype(bf16)
+    left_part(3).start()
+    for i in range(3, 7):
+        right_part(i).wait_recv()
+    racc = both[7, mine, :] + jnp.sum(rrecv[3:7].astype(f32), 0)
     for n in range(4):
         ro[n] = (racc[CW * n:CW * n + CW, :] * live[n:n + 1, :]).astype(bf16)
-    for c in third:
-        c.wait_recv()
-    lacc[...] += jnp.sum(lrecv[1:8].astype(f32), 0)
+    for i in range(3, 7):
+        left_part(i).wait_recv()
+    lsum = lacc[...] + jnp.sum(lrecv[3:7].astype(f32), 0)
     for n in range(4):
-        lo[n] = (lacc[CW * n:CW * n + CW, :] * live[n:n + 1, :]).astype(bf16)
-    for c in gl + gr + [first] + part + second + third:
-        c.wait_send()
-    for k in range(1, 8):
-        forward(k).wait_send()
+        lo[n] = (lsum[CW * n:CW * n + CW, :] * live[n:n + 1, :]).astype(bf16)
+    for n in range(7):
+        left_copy(n).wait_send()
+        right_copy(n).wait_send()
+        right_part(n).wait_send()
+        left_part(n).wait_send()
+    for n in range(8):
+        across(n).wait_send()
+        pass_over(n).wait_send()
 
 
 def opm(lt, rt, pd, rc, wo, live):
@@ -499,10 +551,9 @@
         out_shape=[sd((4, CW, N), bf16)] * 2,
         scratch_shapes=[V((1024, 1024), bf16), V((2048, 1024), bf16), V((1024, 2048), bf16),
                         V((8, *chunk), bf16), V((16, *chunk), bf16)] + [V((8, *chunk), bf16)] * 6
-        + [V(chunk, f32)] * 2 + [dma] * 12,
+        + [V((8, 256, N), f32)] + [V(chunk, f32)] * 2 + [dma] * 12,
         compiler_params=pltpu.CompilerParams(vmem_limit_bytes=60 * 1024 * 1024, collective_id=1, has_side_effects=True),
         name="outer_product",
-        cost_estimate=pl.CostEstimate(flops=10_000_000_000, bytes_accessed=10_000_000, transcendentals=0),
     )(lt, rt, pd, rc, wo, live)
 
 

time: 157 us -> 138 us (0.88)
  Pallas kernels: 144 us -> 125 us
    pallas_call x1, Pallas kernels: 52.8 us -> 38 us  [opm(): pl.pallas_call(opm_kernel, in_specs=[vm] * 6, out_specs=[vm] * 2, out_sha...]
    pallas_call x1, Pallas kernels: 41.5 us -> 37.2 us  [bwd(): pl.pallas_call(bwd_kernel, grid=(4,), in_specs=[COLS, whole((8, 4, 64, F)...]
where the time goes in v5:
time: 138 us
  Pallas kernels  125 us (91%)
  local copies, waits for them, and re-layouts  11.3 us (8%)
    pallas_call x1, Pallas kernels, fwd(): pl.pallas_call(fwd_kernel, grid=(4,), in_specs=[ANY] * 3 + [whole((64, 12...  49.7 us
    pallas_call x1, Pallas kernels, opm(): pl.pallas_call(opm_kernel, in_specs=[vm] * 6, out_specs=[vm] * 2, out_sha...  38 us
    pallas_call x1, Pallas kernels, bwd(): pl.pallas_call(bwd_kernel, grid=(4,), in_specs=[COLS, whole((8, 4, 64, F)...  37.2 us
    transpose x2, local copies, waits for them, and re-layouts, by_column(): return a.transpose(1, 0, 2).reshape(8, 4, 64, F)  4.33 us
    transpose x1, local copies, waits for them, and re-layouts, by_row(): return a.reshape(32, 64, F).transpose(1, 0, 2)  4.03 us

profile of v5, /device:TPU:0, one launch (start us, length us, event | category | flops | bytes accessed | tf_op | source)
XLA Modules:
  0.0 137.7 jit_solution(3872927418956294505)
XLA Ops:
  0.6 0.0 copy-start
  0.6 0.8 convert_element_type.5
  1.4 0.1 copy.30
  1.5 0.6 pad.4.live_in
  2.2 2.2 %copy.38 = bf16[32,2,8,4,128]{4,0,3,1,2:T(8,128)(2,1)} copy(bf16[32,2,8,4,128]{4,3,2,1,0:T(4,128)(2,1)} %bitcast.26) | data formatting | bytes 1048576 | tf_op jit(solution)/shard_map/reshape | solution.py:568
  4.4 2.8 %copy.26 = bf16[32,64,256]{2,1,0:T(8,128)(2,1)} copy(bf16[32,64,256]{2,0,1:T(8,128)(2,1)} %bitcast.22) | data formatting | bytes 2097152 | tf_op jit(solution)/shard_map/transpose | solution.py:562
  7.2 0.0 copy-done
  7.2 1.6 %copy.27 = bf16[32,64,256]{2,1,0:T(8,128)(2,1)} copy(bf16[32,64,256]{2,0,1:T(8,128)(2,1)S(1)} %bitcast.23) | data formatting | bytes 2097152 | tf_op jit(solution)/shard_map/transpose | solution.py:562
  8.7 49.7 %attention_forward.1 = (bf16[8,4,64,256]{3,2,1,0:T(8,128)(2,1)}, bf16[4,8,512,512]{3,2,1,0:T(8,128)(2,1)}, f32[4,256,512]{2,1,0:T(8,128)}, f32[4,256,512]{2,1,0:...) custom-call(bf16[8,4,64,256]{3,2,1,0:T(8,128)(2,1)} %bitcast.19, ...), custom_call_target="tpu_custom_call" | custom-call | tf_op jit(solution)/shard_map/attention_forward/pallas_call | solution.py:342
  58.5 38.0 %outer_product.1 = (bf16[4,32,512]{2,1,0:T(8,128)(2,1)}, bf16[4,32,512]{2,1,0:T(8,128)(2,1)}) custom-call(bf16[128,512]{1,0:T(8,128)(2,1)} %bitcast.28, bf16[128,512]{1,0:T(8,128)(2,1)} %bitcast.29, bf16[2048,128]{1,0:T(8,128)(2,1)} %bitcast.27, f32[8,256]{1,0:T(8,128)} %get-tuple-element.23.rc, bf16[1024,128]{1,0:T(8,128)(2,1)} %wo.1, ...), custom_call_target="tpu_custom_call" | custom-call | tf_op jit(solution)/shard_map/outer_product/pallas_call | solution.py:547
  96.5 37.2 %attention_backward.1 = (bf16[8,4,64,256]{3,2,1,0:T(8,128)(2,1)}, bf16[8,4,64,256]{3,2,1,0:T(8,128)(2,1)}) custom-call(bf16[8,4,64,256]{3,2,1,0:T(8,128)(2,1)} %get-tuple-element.17.x_ref, bf16[8,4,64,256]{3,2,1,0:T(8,128)(2,1)} %get-tuple-element.18.up_ref, bf16[4,256,512]{2,1,0:T(8,128)(2,1)} %get-tuple-element.19.at_ref, ...), custom_call_target="tpu_custom_call" | custom-call | tf_op jit(solution)/shard_map/attention_backward/pallas_call | solution.py:364
  133.7 4.0 %copy_bitcast_fusion = (bf16[64,32,256]{2,1,0:T(8,128)(2,1)}, bf16[64,32,256]{2,1,0:T(8,128)(2,1)}) fusion(bf16[32,64,256]{2,1,0:T(8,128)(2,1)} %bitcast.25, bf16[32,64,256]{2,1,0:T(8,128)(2,1)} %bitcast.24), kind=kLoop, calls=%fused_computation | loop fusion | bytes 4194304 | tf_op jit(solution)/shard_map/transpose | solution.py:565
Async XLA Ops:
  0.6 6.5 %copy-start = (bf16[64,32,256]{2,1,0:T(8,128)(2,1)S(1)}, bf16[64,32,256]{2,1,0:T(8,128)(2,1)}, u32[]{:S(2)}) copy-start(bf16[64,32,256]{2,1,0:T(8,128)(2,1)} %param.15) | copy-start | bytes 3145732

commit v6 on v5

--- a/solution.py
+++ b/solution.py
@@ -1,3 +1,5 @@
+import functools
+
 import jax
 import jax.numpy as jnp
 from jax import lax
@@ -53,16 +55,24 @@
                                         device_id={"dep": dep, "res": res}, device_id_type=MESH)
 
 
-def greet(peers):
+def hail(peers):
     bar = pltpu.get_barrier_semaphore()
     for dep, res in peers:
         pl.semaphore_signal(bar, inc=1, device_id={"dep": dep, "res": res}, device_id_type=MESH)
-    pl.semaphore_wait(bar, len(peers))
-
-
-def fwd_kernel(hx, ux, px, live_in, wq, wk, wv, wg, we, wl, wr,
-               x_ref, p_ref, o_ref, g_ref, a_ref, l_ref, r_ref, up_out, pd_out, rc_ref, live_out,
-               wt, bias_s, xbuf, lbuf, livet, jbuf, mine, ustage, pstage,
+
+
+def gather_all(count):
+    pl.semaphore_wait(pltpu.get_barrier_semaphore(), count)
+
+
+def greet(peers):
+    hail(peers)
+    gather_all(len(peers))
+
+
+def fwd_kernel(hx, ux, px, present, wq, wk, wv, wg, we, wl, wr,
+               x_ref, p_ref, o_ref, g_ref, a_ref, l_ref, r_ref, q_ref, v_ref, kt_ref, up_out, pd_out, rc_ref, live_out,
+               wt, bias_s, st_s, live_in, xbuf, lbuf, livet, jbuf, mine, ustage, pstage,
                xs, xr, us, ur, ps, pr, ls, lr, js, jr, own):
     k = pl.program_id(0)
     d = lax.axis_index("dep")
@@ -92,7 +102,7 @@
     def own_x(c):
         return pltpu.make_async_copy(hx.at[d, c], xbuf.at[c, d], own.at[c])
 
-    own_up = pltpu.make_async_copy(ux.at[d], ustage, own.at[4])
+    own_up = pltpu.make_async_copy(ux.at[d, pl.ds(0, 2)], ustage, own.at[4])
     own_pd = pltpu.make_async_copy(px.at[d], pstage, own.at[5])
     own_up2 = pltpu.make_async_copy(ustage, up_out.at[d], own.at[6])
     own_pd2 = pltpu.make_async_copy(pstage, pd_out.at[d], own.at[7])
@@ -103,14 +113,17 @@
             own_x(c).start()
         own_up.start()
         own_pd.start()
-        greet([(dep_at(n), r) for n in range(1, 8)] + [(d, res_at(n)) for n in range(1, 16)])
-        for n in range(1, 8):
-            live_copy(n).start()
-        for n in range(1, 8):
-            x_copy(0, n).start()
-        lbuf[d] = live_in[...]
+        hail([(dep_at(n), r) for n in range(1, 8)] + [(d, res_at(n)) for n in range(1, 16)])
         for n, w in enumerate((wq, wv, wg, we)):
             wt[n] = w[...].T
+        held = jnp.concatenate([present[...].astype(f32), jnp.zeros((64, 96), f32)], axis=1).astype(bf16)
+        live_in[...] = held
+        lbuf[d] = held
+        gather_all(22)
+        for n in range(1, 8):
+            live_copy(n).start()
+        for n in range(1, 8):
+            x_copy(0, n).start()
         for n in range(1, 8):
             live_copy(n).wait_recv()
         live = lbuf[...].reshape(N, 128).astype(f32)
@@ -131,7 +144,7 @@
     @pl.when(k == 1)
     def _():
         for n in range(1, 8):
-            x_copy(3, n).start()
+            pd_copy(n).start()
         own_up.wait()
         own_pd.wait()
         own_up2.start()
@@ -140,13 +153,10 @@
     @pl.when(k == 2)
     def _():
         for n in range(1, 8):
-            up_copy(0, n).start()
+            up_copy(1, n).start()
 
     @pl.when(k == 3)
     def _():
-        for c in (2, 3):
-            for n in range(1, 8):
-                up_copy(c, n).start()
         for n in range(1, 16):
             row_copy(n).wait_recv()
         counts = mm(jbuf[...].reshape(128, N).astype(bf16), lbuf[...].reshape(N, 128))
@@ -170,34 +180,66 @@
     vt = mm(wt[1], xbt).astype(bf16)
     kk = mm(xb, wk[...]).astype(bf16)
     gt = jax.nn.sigmoid(mm(wt[2], xbt))
+    q_ref[0] = qt.T
+    v_ref[0] = vt.T
+    kt_ref[0] = kk.T
     g_ref[0] = gt
     extra = (lax.broadcasted_iota(jnp.int32, (128, N), 0) == 4 * d + k).astype(f32).astype(bf16)
     bias = bias_s[...]
+    PIECE = 128
+
+    def operands(h):
+        grp = h // 4
+        return jnp.concatenate([kk[:, 128 * grp:128 * grp + 128], bias], axis=1), spread(qt[DH * h:DH * h + DH], h, extra)
+
+    def score(ops, h, i):
+        val = mm(ops[0][i:i + PIECE], ops[1])
+        st_s[h % 2, i:i + PIECE, :] = val
+        return jnp.max(val, 0, keepdims=True)
+
+    def blend(h):
+        o_ref[0, DH * h:DH * h + DH, :] = mm(vt[DH * h:DH * h + DH], p_ref[0, h])
+
+    ops = operands(0)
+    peak = functools.reduce(jnp.maximum, [score(ops, 0, i) for i in range(0, N, PIECE)])
+    def push_x(at, c):
+        @pl.when(k == at)
+        def _():
+            for n in range(1, 8):
+                x_copy(c, n).start()
+
+    def push_up(at, c):
+        @pl.when(k == at)
+        def _():
+            for n in range(1, 8):
+                up_copy(c, n).start()
+
     for h in range(H):
+        if h == 2:
+            push_x(0, 2)
         if h == 4:
-            @pl.when(k == 0)
-            def _():
-                for n in range(1, 8):
-                    x_copy(2, n).start()
-
-            @pl.when(k == 1)
-            def _():
-                for n in range(1, 8):
-                    pd_copy(n).start()
-
-            @pl.when(k == 2)
-            def _():
-                for n in range(1, 8):
-                    up_copy(1, n).start()
-        grp = h // 4
-        lhs = jnp.concatenate([kk[:, 128 * grp:128 * grp + 128], bias], axis=1)
-        st = mm(lhs, spread(qt[DH * h:DH * h + DH], h, extra))
-        m = jnp.max(st, 0, keepdims=True)
-        e = jnp.exp(st - m)
-        s = jnp.sum(e, 0, keepdims=True)
-        p = (e * (1.0 / s)).astype(bf16)
-        p_ref[0, h] = p
-        o_ref[0, pl.ds(DH * h, DH), :] = mm(vt[DH * h:DH * h + DH], p)
+            push_up(1, 0)
+        if h == 5:
+            push_x(0, 3)
+        b = h % 2
+        if h + 1 < H:
+            ops = operands(h + 1)
+        nxt = []
+        tot = jnp.zeros((1, N), f32)
+        for i in range(0, N, PIECE):
+            if h + 1 < H:
+                nxt.append(score(ops, h + 1, i))
+            e = jnp.exp(st_s[b, i:i + PIECE, :] - peak)
+            st_s[b, i:i + PIECE, :] = e
+            tot = tot + jnp.sum(e, 0, keepdims=True)
+        if h:
+            blend(h - 1)
+        inv = 1.0 / tot
+        for i in range(0, N, PIECE):
+            p_ref[0, h, i:i + PIECE, :] = (st_s[b, i:i + PIECE, :] * inv).astype(bf16)
+        if nxt:
+            peak = functools.reduce(jnp.maximum, nxt)
+    blend(H - 1)
     gated = (gt * o_ref[0]).astype(bf16)
     up = mm(wt[3], gated)
     after = (xin.T.astype(f32) + up).astype(bf16)
@@ -212,23 +254,23 @@
     def _():
         for n in range(1, 8):
             pd_copy(n).wait_recv()
-            for c in range(4):
+            for c in range(2):
                 up_copy(c, n).wait_recv()
         own_up2.wait()
         own_pd2.wait()
         for n in range(1, 8):
             live_copy(n).wait_send()
             pd_copy(n).wait_send()
-            for c in range(4):
+            for c in range(2):
                 up_copy(c, n).wait_send()
-                if c:
-                    x_copy(c, n).wait_send()
+            for c in range(1, 4):
+                x_copy(c, n).wait_send()
         for n in range(1, 16):
             row_copy(n).wait_send()
 
 
-def bwd_kernel(x_ref, up_ref, at_ref, lg_ref, rg_ref, p_ref, o_ref, g_ref, wq, wk, wv, wg, we, wl, wr,
-               out_g, out_i, wkt, acc_q, dt_s, sbuf, ss, rs, own):
+def bwd_kernel(x_ref, ua_ref, ub_ref, at_ref, lg_ref, rg_ref, p_ref, o_ref, g_ref, q_ref, v_ref, kt_ref, wq, wk, wv, wg, we, wl, wr,
+               out_g, out_i, ds_s, acc_q, acc_v, acc_t, dt_s, sbuf, ss, rs, own):
     k = pl.program_id(0)
     d = lax.axis_index("dep")
     r = lax.axis_index("res")
@@ -252,7 +294,6 @@
 
     @pl.when(k == 0)
     def _():
-        wkt[...] = wk[...].T
         wlt, wrt = wl[...].T, wr[...].T
         greet([(dep_at(n), r) for n in range(1, 8)])
         for c in range(4):
@@ -260,50 +301,67 @@
             dy = mm(wlt, lg_ref[c]) + mm(wrt, rg_ref[c])
             m1 = jnp.mean(dy, 0, keepdims=True)
             m2 = jnp.mean(dy * yhat, 0, keepdims=True)
-            upt = up_ref[:, c].reshape(N, F).T.astype(f32)
+            upt = (ua_ref if c < 2 else ub_ref)[:, c % 2].reshape(N, F).T.astype(f32)
             dt_s[c] = (yinv * (dy - m1 - yhat * m2) + upt).astype(bf16)
             ship(1, c, dt_s[c])
 
     xin = x_ref[...].reshape(N, F)
-    xhat, _ = norm(xin.astype(f32), 1)
-    xb = xhat.astype(bf16)
-    xbt = xb.T
-    q = (mm(xb, wq[...]) * SCALE).astype(bf16)
-    v = mm(xb, wv[...]).astype(bf16)
-    kt = mm(wkt[...], xbt).astype(bf16)
+    q = q_ref[0]
+    v = v_ref[0]
+    kt = kt_ref[0]
     gt = g_ref[0]
     ot = o_ref[0]
     dt = dt_s[k]
     dg = mm(we[...], dt).astype(bf16).astype(f32)
     dot_ = (dg * gt).astype(bf16)
     dpre = (dg * ot * gt * (1.0 - gt)).astype(bf16)
-    do = dot_.T
     prod = dot_.astype(f32) * ot
     row = lax.broadcasted_iota(jnp.int32, (128, N), 0)
     col = lax.broadcasted_iota(jnp.int32, (N, 128), 1)
     ones = (col < 2).astype(f32).astype(bf16)
     lane = lax.broadcasted_iota(jnp.int32, (N, F), 1) // DH
-    dk = jnp.zeros((N, F), f32)
-    dv = jnp.zeros((N, F), f32)
-    for h in range(H):
+    zero = jnp.zeros((), bf16)
+
+    def back(h):
+        sl = slice(DH * h, DH * h + DH)
+        acc_q[sl, :] = mm(kt[sl], ds_s[h])
+
+    def dops(h):
         grp = h // 4
         sl = slice(DH * h, DH * h + DH)
         dd = -jnp.sum(prod[sl], 0, keepdims=True)
         hi = dd.astype(bf16).astype(f32)
         lo = dd - hi
         extra = jnp.where(row == 0, hi, jnp.where(row == 1, lo, 0.0)).astype(bf16)
-        lhs = jnp.concatenate([v[:, 128 * grp:128 * grp + 128], ones], axis=1)
-        dp = mm(lhs, spread(dot_[sl], h, extra))
-        p = p_ref[0, h]
-        ds = (p.astype(f32) * dp).astype(bf16)
-        mask = lane == h
-        zero = jnp.zeros((), bf16)
-        dv = dv + mm(p, jnp.where(mask, do, zero))
-        dk = dk + mm(ds, jnp.where(mask, q, zero))
-        acc_q[sl, :] = mm(kt[sl], ds)
+        return jnp.concatenate([v[:, 128 * grp:128 * grp + 128], ones], axis=1), spread(dot_[sl], h, extra)
+
+    def wide_v(h):
+        sl = slice(DH * h, DH * h + DH)
+        acc_v[sl, :] = mmt(dot_[sl], p_ref[0, h])
+
+    def tall_k(h, i):
+        ext = mm(ds_s[h, i:i + 256, :], jnp.where(lane == h, q, zero))
+        if h:
+            acc_t[i:i + 256, :] += ext
+        else:
+            acc_t[i:i + 256, :] = ext
+
+    for h in range(H):
+        ops = dops(h)
+        for i in range(0, N, 256):
+            dp = mm(ops[0][i:i + 256], ops[1])
+            ds_s[h, i:i + 256, :] = (p_ref[0, h, i:i + 256, :].astype(f32) * dp).astype(bf16)
+            if h:
+                tall_k(h - 1, i)
+        wide_v(h)
+        if h:
+            back(h - 1)
+    back(H - 1)
+    for i in range(0, N, 256):
+        tall_k(H - 1, i)
     dq = (acc_q[...].astype(bf16).astype(f32) * SCALE).astype(bf16)
     dx = (mm(wq[...], dq) + mm(wg[...], dpre)
-          + mmt(wk[...], dk.astype(bf16)) + mmt(wv[...], dv.astype(bf16)))
+          + mmt(wk[...], acc_t[...].astype(bf16)) + mm(wv[...], acc_v[...].astype(bf16)))
     dx = dx.astype(bf16).astype(f32)
     xt = xin.T.astype(f32)
     xh, inv = norm(xt, 0)
@@ -342,14 +400,14 @@
     return pl.pallas_call(
         fwd_kernel,
         grid=(4,),
-        in_specs=[ANY] * 3 + [whole((64, 128))] + [whole((F, F))] * 5 + [whole((CW, F))] * 2,
+        in_specs=[ANY] * 3 + [whole((64, CW))] + [whole((F, F))] * 5 + [whole((CW, F))] * 2,
         out_specs=[COLS, percol((H, N, N)), percol((F, N)), percol((F, N)), percol((F, N)), percol((CW, N)),
-                   percol((CW, N)), ANY, ANY, whole((8, 256)), whole((8, N))],
+                   percol((CW, N)), percol((N, F)), percol((N, F)), percol((F, N)), ANY, ANY, whole((8, 256)), whole((8, N))],
         out_shape=[sd((8, 4, 64, F), bf16), sd((4, H, N, N), bf16), sd((4, F, N), f32), sd((4, F, N), f32),
                    sd((4, F, N), bf16), sd((4, CW, N), bf16), sd((4, CW, N), bf16),
-                   sd(ux.shape, bf16), sd(px.shape, bf16), sd((8, 256), f32), sd((8, N), f32)],
-        scratch_shapes=[V((4, F, F), bf16), V((N, 128), bf16), V((4, 8, 64, F), bf16),
-                        V((8, 64, 128), bf16), V((128, N), f32), V((16, 8, N), f32), V((8, N), f32), V(ux.shape[1:], bf16),
+                   sd((4, N, F), bf16), sd((4, N, F), bf16), sd((4, F, N), bf16), sd((8, 2, 64, F), bf16), sd(px.shape, bf16), sd((8, 256), f32), sd((8, N), f32)],
+        scratch_shapes=[V((4, F, F), bf16), V((N, 128), bf16), V((2, N, N), f32), V((64, 128), bf16), V((4, 8, 64, F), bf16),
+                        V((8, 64, 128), bf16), V((128, N), f32), V((16, 8, N), f32), V((8, N), f32), V((2, 64, F), bf16),
                         V(px.shape[1:], bf16), dma((4, 8)), dma((4, 8)), dma((4, 8)), dma((4, 8))] + [dma((8,))] * 4 + [dma((16,))] * 2 + [dma((8,))],
         compiler_params=pltpu.CompilerParams(vmem_limit_bytes=60 * 1024 * 1024, collective_id=2, has_side_effects=True,
                                              dimension_semantics=("arbitrary",)),
@@ -357,28 +415,28 @@
     )(hx, ux, px, live, wq, wk, wv, wg, we, wl, wr)
 
 
-def bwd(x, up, at, lg, rg, p, o, g, wq, wk, wv, wg, we, wl, wr):
+def bwd(x, ua, ub, at, lg, rg, p, o, g, q, v, kt, wq, wk, wv, wg, we, wl, wr):
     sd = jax.ShapeDtypeStruct
     V = pltpu.VMEM
     dma = pltpu.SemaphoreType.DMA
     return pl.pallas_call(
         bwd_kernel,
         grid=(4,),
-        in_specs=[COLS, whole((8, 4, 64, F)), whole((4, F, N)), whole((4, CW, N)), whole((4, CW, N)), percol((H, N, N)), percol((F, N)),
-                  percol((F, N))] + [whole((F, F))] * 5 + [whole((CW, F))] * 2,
+        in_specs=[COLS, whole((8, 2, 64, F)), whole((8, 2, 64, F)), whole((4, F, N)), whole((4, CW, N)), whole((4, CW, N)), percol((H, N, N)), percol((F, N)),
+                  percol((F, N)), percol((N, F)), percol((N, F)), percol((F, N))] + [whole((F, F))] * 5 + [whole((CW, F))] * 2,
         out_specs=[ANY, ANY],
         out_shape=[sd((8, 4, 64, F), bf16)] * 2,
-        scratch_shapes=[V((F, F), bf16), V((F, N), f32), V((4, F, N), bf16), V((2, 4, 8, 64, F), bf16),
+        scratch_shapes=[V((H, N, N), bf16), V((F, N), f32), V((F, N), f32), V((N, F), f32), V((4, F, N), bf16), V((2, 4, 8, 64, F), bf16),
                         dma((2, 4, 8)), dma((2, 4, 8)), dma((2, 4))],
         compiler_params=pltpu.CompilerParams(vmem_limit_bytes=60 * 1024 * 1024, collective_id=3, has_side_effects=True,
                                              dimension_semantics=("arbitrary",)),
         name="attention_backward",
-    )(x, up, at, lg, rg, p, o, g, wq, wk, wv, wg, we, wl, wr)
-
-
-def opm_kernel(lt, rt, pd, rc, wo, live, lo, ro,
+    )(x, ua, ub, at, lg, rg, p, o, g, q, v, kt, wq, wk, wv, wg, we, wl, wr)
+
+
+def opm_kernel(lt, rt, pd, rc, wo, live, ux, lo, ro, up,
                perm, oc1, oc2, lbuf, rbuf, lsend, lrecv, psend, precv, rsend, rrecv, both, lkeep, lacc,
-               ls, lr, rs, rr, fs, fr, ps, pr, s2, r2, s3, r3):
+               ls, lr, rs, rr, fs, fr, ps, pr, s2, r2, s3, r3, us, ur, own):
     d = lax.axis_index("dep")
     r = lax.axis_index("res")
     xl, z = d // 4, lax.rem(d, 4)
@@ -394,7 +452,7 @@
         return 2 * chip_of(flip, step) + core
 
     partner = 2 * chip_of(0, 0) + 1 - core
-    greet([(dep_of(0, n), r) for n in range(1, 4)] + [(dep_of(1, 0), r)]
+    greet([(lax.rem(d + n, 8), r) for n in range(1, 8)]
           + [(d, res_of(0, n)) for n in range(1, 4)] + [(d, res_of(1, 0)), (d, partner)])
 
     def left_copy(n):
@@ -419,6 +477,12 @@
         slot = res_of(1, 0) if n == 0 else res_of(0, -n) if n < 4 else res_of(1, 3 - n)
         return remote(rbuf.at[slot], rbuf.at[slot], fs.at[n], fr.at[n], d, partner)
 
+    def up_copy(n):
+        dep = lax.rem(d + n, 8)
+        return remote(ux.at[dep, pl.ds(2, 2)], up.at[d], us.at[n], ur.at[n], dep, r)
+
+    own_up = pltpu.make_async_copy(ux.at[d, pl.ds(2, 2)], up.at[d], own)
+    own_up.start()
     for n in range(4):
         left_copy(n).start()
         right_copy(n).start()
@@ -453,6 +517,11 @@
             for i in range(4, 7):
                 right_copy(i).start()
             across(0).start()
+
+        @pl.when(n == 6)
+        def _():
+            for i in range(1, 8):
+                up_copy(i).start()
 
         @pl.when(n == 5)
         def _():
@@ -528,6 +597,10 @@
     lsum = lacc[...] + jnp.sum(lrecv[3:7].astype(f32), 0)
     for n in range(4):
         lo[n] = (lsum[CW * n:CW * n + CW, :] * live[n:n + 1, :]).astype(bf16)
+    own_up.wait()
+    for n in range(1, 8):
+        up_copy(n).wait_recv()
+        up_copy(n).wait_send()
     for n in range(7):
         left_copy(n).wait_send()
         right_copy(n).wait_send()
@@ -538,7 +611,7 @@
         pass_over(n).wait_send()
 
 
-def opm(lt, rt, pd, rc, wo, live):
+def opm(lt, rt, pd, rc, wo, live, ux):
     sd = jax.ShapeDtypeStruct
     vm = pl.BlockSpec(memory_space=pltpu.VMEM)
     chunk = (128, N)
@@ -546,15 +619,15 @@
     dma = pltpu.SemaphoreType.DMA((8,))
     return pl.pallas_call(
         opm_kernel,
-        in_specs=[vm] * 6,
-        out_specs=[vm] * 2,
-        out_shape=[sd((4, CW, N), bf16)] * 2,
+        in_specs=[vm] * 6 + [ANY],
+        out_specs=[vm] * 3,
+        out_shape=[sd((4, CW, N), bf16)] * 2 + [sd((8, 2, 64, F), bf16)],
         scratch_shapes=[V((1024, 1024), bf16), V((2048, 1024), bf16), V((1024, 2048), bf16),
                         V((8, *chunk), bf16), V((16, *chunk), bf16)] + [V((8, *chunk), bf16)] * 6
-        + [V((8, 256, N), f32)] + [V(chunk, f32)] * 2 + [dma] * 12,
+        + [V((8, 256, N), f32)] + [V(chunk, f32)] * 2 + [dma] * 14 + [pltpu.SemaphoreType.DMA],
         compiler_params=pltpu.CompilerParams(vmem_limit_bytes=60 * 1024 * 1024, collective_id=1, has_side_effects=True),
         name="outer_product",
-    )(lt, rt, pd, rc, wo, live)
+    )(lt, rt, pd, rc, wo, live, ux)
 
 
 def on_device(msa, present, pair, upstream, wq, wk, wv, wg, we, wl, wr, wo):
@@ -564,12 +637,12 @@
     def by_row(a):
         return a.reshape(32, 64, F).transpose(1, 0, 2)
 
-    live = jnp.pad(present.astype(bf16), ((0, 0), (0, 96)))
     pd = pair.reshape(32, 2, 8, 4, CZ).transpose(2, 1, 3, 0, 4)
-    x, p, o, g, at, lt, rt, up, pd, recip, livet = fwd(
-        by_column(msa), by_column(upstream), pd, live, wq, wk, wv, wg, we, wl.T, wr.T)
-    lg, rg = opm(lt.reshape(4 * CW, N), rt.reshape(4 * CW, N), pd.reshape(-1, CZ), recip, wo, livet)
-    grad, inter = bwd(x, up, at, lg, rg, p, o, g, wq, wk, wv, wg, we, wl.T, wr.T)
+    ux = by_column(upstream)
+    x, p, o, g, at, lt, rt, q, v, kt, ua, pd, recip, livet = fwd(
+        by_column(msa), ux, pd, present, wq, wk, wv, wg, we, wl.T, wr.T)
+    lg, rg, ub = opm(lt.reshape(4 * CW, N), rt.reshape(4 * CW, N), pd.reshape(-1, CZ), recip, wo, livet, ux)
+    grad, inter = bwd(x, ua, ub, at, lg, rg, p, o, g, q, v, kt, wq, wk, wv, wg, we, wl.T, wr.T)
     return by_row(grad), by_row(inter)
 
 

time: 138 us -> 132 us (0.957)
  Pallas kernels: 125 us -> 119 us
    pallas_call x3, Pallas kernels: 125 us -> 119 us  [the longest x1 43 us: fwd(): pl.pallas_call(fwd_kernel, grid=(4,), in_specs=[ANY] * 3 + [whole((64, CW...]
    unnamed x2 -> x3, local copies, waits for them, and re-layouts: 0.01 us -> 1.51 us
where the time goes in v6:
time: 132 us
  Pallas kernels  119 us (90%)
  local copies, waits for them, and re-layouts  12 us (9%)
    pallas_call x1, Pallas kernels, fwd(): pl.pallas_call(fwd_kernel, grid=(4,), in_specs=[ANY] * 3 + [whole((64, CW...  43 us
    pallas_call x1, Pallas kernels, opm(): pl.pallas_call(opm_kernel, in_specs=[vm] * 6 + [ANY], out_specs=[vm] * 3,...  41.7 us
    pallas_call x1, Pallas kernels, bwd(): pl.pallas_call(bwd_kernel, grid=(4,), in_specs=[COLS, whole((8, 2, 64, F)...  34.6 us
    transpose x2, local copies, waits for them, and re-layouts, by_column(): return a.transpose(1, 0, 2).reshape(8, 4, 64, F)  4.33 us
    transpose x1, local copies, waits for them, and re-layouts, by_row(): return a.reshape(32, 64, F).transpose(1, 0, 2)  4.03 us

profile of v6, /device:TPU:0, one launch (start us, length us, event | category | flops | bytes accessed | tf_op | source)
XLA Modules:
  0.0 132.0 jit_solution(10416660427346416851)
XLA Ops:
  0.6 0.0 copy-start
  0.6 1.5 %copy.23.present = s32[64,32]{1,0:T(8,128)} copy(s32[64,32]{0,1:T(8,128)} %param.13) | data formatting | bytes 16384 | tf_op args[1]
  2.1 2.2 %copy.31 = bf16[32,2,8,4,128]{4,0,3,1,2:T(8,128)(2,1)} copy(bf16[32,2,8,4,128]{4,3,2,1,0:T(4,128)(2,1)} %bitcast.27) | data formatting | bytes 1048576 | tf_op jit(solution)/shard_map/reshape | solution.py:640
  4.3 2.8 %copy.19 = bf16[32,64,256]{2,1,0:T(8,128)(2,1)} copy(bf16[32,64,256]{2,0,1:T(8,128)(2,1)} %bitcast.23) | data formatting | bytes 2097152 | tf_op jit(solution)/shard_map/transpose | solution.py:635
  7.1 0.0 copy-done
  7.1 1.6 %copy.20 = bf16[32,64,256]{2,1,0:T(8,128)(2,1)} copy(bf16[32,64,256]{2,0,1:T(8,128)(2,1)S(1)} %bitcast.24) | data formatting | bytes 2097152 | tf_op jit(solution)/shard_map/transpose | solution.py:635
  8.6 43.0 %attention_forward.1 = (bf16[8,4,64,256]{3,2,1,0:T(8,128)(2,1)}, bf16[4,8,512,512]{3,2,1,0:T(8,128)(2,1)}, f32[4,256,512]{2,1,0:T(8,128)}, f32[4,256,512]{2,1,0:...) custom-call(bf16[8,4,64,256]{3,2,1,0:T(8,128)(2,1)} %bitcast.21, ...), custom_call_target="tpu_custom_call" | custom-call | tf_op jit(solution)/shard_map/attention_forward/pallas_call | solution.py:400
  51.6 41.7 %outer_product.1 = (bf16[4,32,512]{2,1,0:T(8,128)(2,1)}, bf16[4,32,512]{2,1,0:T(8,128)(2,1)}, bf16[8,2,64,256]{3,2,1,0:T(8,128)(2,1)}) custom-call(bf16[128,512]{1,0:T(8,128)(2,1)} %bitcast.29, bf16[128,512]{1,0:T(8,128)(2,1)} %bitcast.30, bf16[2048,128]{1,0:T(8,128)(2,1)} %bitcast.28, f32[8,256]{1,0:T(8,128)} %get-tuple-element.26.rc, ...), custom_call_target="tpu_custom_call" | custom-call | tf_op jit(solution)/shard_map/outer_product/pallas_call | solution.py:620
  93.3 34.6 %attention_backward.1 = (bf16[8,4,64,256]{3,2,1,0:T(8,128)(2,1)}, bf16[8,4,64,256]{3,2,1,0:T(8,128)(2,1)}) custom-call(bf16[8,4,64,256]{3,2,1,0:T(8,128)(2,1)} %get-tuple-element.21.x_ref, bf16[8,2,64,256]{3,2,1,0:T(8,128)(2,1)} %get-tuple-element.22.ua_ref, bf16[8,2,64,256]{3,2,1,0:T(8,128)(2,1)} %get-tuple-element.28.ub_ref, ...), custom_call_target="tpu_custom_call" | custom-call | tf_op jit(solution)/shard_map/attention_backward/pallas_call | solution.py:422
  127.9 4.0 %copy_bitcast_fusion = (bf16[64,32,256]{2,1,0:T(8,128)(2,1)}, bf16[64,32,256]{2,1,0:T(8,128)(2,1)}) fusion(bf16[32,64,256]{2,1,0:T(8,128)(2,1)} %bitcast.26, bf16[32,64,256]{2,1,0:T(8,128)(2,1)} %bitcast.25), kind=kLoop, calls=%fused_computation | loop fusion | bytes 4194304 | tf_op jit(solution)/shard_map/transpose | solution.py:638
Async XLA Ops:
  0.6 6.5 %copy-start = (bf16[64,32,256]{2,1,0:T(8,128)(2,1)S(1)}, bf16[64,32,256]{2,1,0:T(8,128)(2,1)}, u32[]{:S(2)}) copy-start(bf16[64,32,256]{2,1,0:T(8,128)(2,1)} %param.15) | copy-start | bytes 3145732

commit v7 on v6

--- a/solution.py
+++ b/solution.py
@@ -70,9 +70,9 @@
     gather_all(len(peers))
 
 
-def fwd_kernel(hx, ux, px, present, wq, wk, wv, wg, we, wl, wr,
-               x_ref, p_ref, o_ref, g_ref, a_ref, l_ref, r_ref, q_ref, v_ref, kt_ref, up_out, pd_out, rc_ref, live_out,
-               wt, bias_s, st_s, live_in, xbuf, lbuf, livet, jbuf, mine, ustage, pstage,
+def fwd_kernel(x_in, u_in, pair_in, present, wq, wk, wv, wg, we, wl, wr,
+               x_ref, p_ref, o_ref, g_ref, a_ref, l_ref, r_ref, q_ref, v_ref, kt_ref, up_out, ut_out, pd_out, rc_ref, live_out,
+               wt, bias_s, st_s, live_in, hx, ux, px, xbuf, lbuf, livet, jbuf, mine,
                xs, xr, us, ur, ps, pr, ls, lr, js, jr, own):
     k = pl.program_id(0)
     d = lax.axis_index("dep")
@@ -91,7 +91,7 @@
         return remote(ux.at[dep_at(n), c], up_out.at[d, c], us.at[c, n], ur.at[c, n], dep_at(n), r)
 
     def pd_copy(n):
-        return remote(px.at[dep_at(n)], pd_out.at[d], ps.at[n], pr.at[n], dep_at(n), r)
+        return remote(px.at[:, dep_at(n)], pd_out.at[d], ps.at[n], pr.at[n], dep_at(n), r)
 
     def live_copy(n):
         return remote(live_in, lbuf.at[d], ls.at[n], lr.at[n], dep_at(n), r)
@@ -99,24 +99,16 @@
     def row_copy(n):
         return remote(mine, jbuf.at[r], js.at[n], jr.at[n], d, res_at(n))
 
-    def own_x(c):
-        return pltpu.make_async_copy(hx.at[d, c], xbuf.at[c, d], own.at[c])
-
-    own_up = pltpu.make_async_copy(ux.at[d, pl.ds(0, 2)], ustage, own.at[4])
-    own_pd = pltpu.make_async_copy(px.at[d], pstage, own.at[5])
-    own_up2 = pltpu.make_async_copy(ustage, up_out.at[d], own.at[6])
-    own_pd2 = pltpu.make_async_copy(pstage, pd_out.at[d], own.at[7])
+    own_up = pltpu.make_async_copy(ux.at[d, pl.ds(0, 2)], up_out.at[d], own.at[0])
+    own_pd = pltpu.make_async_copy(px.at[:, d], pd_out.at[d], own.at[1])
+    later_up = pltpu.make_async_copy(ux.at[:, pl.ds(2, 2)], ut_out, own.at[2])
 
     @pl.when(k == 0)
     def _():
-        for c in range(4):
-            own_x(c).start()
-        own_up.start()
-        own_pd.start()
         hail([(dep_at(n), r) for n in range(1, 8)] + [(d, res_at(n)) for n in range(1, 16)])
-        for n, w in enumerate((wq, wv, wg, we)):
-            wt[n] = w[...].T
-        held = jnp.concatenate([present[...].astype(f32), jnp.zeros((64, 96), f32)], axis=1).astype(bf16)
+        hx[...] = jnp.transpose(x_in[...], (1, 0, 2)).reshape(hx.shape)
+        flat = jnp.concatenate([present[...].astype(f32), jnp.zeros((CW, 64), f32)], axis=1)
+        held = jnp.concatenate([flat, jnp.zeros((96, 128), f32)], axis=0).T[:64].astype(bf16)
         live_in[...] = held
         lbuf[d] = held
         gather_all(22)
@@ -124,6 +116,12 @@
             live_copy(n).start()
         for n in range(1, 8):
             x_copy(0, n).start()
+        for c in range(4):
+            xbuf[c, d] = hx[d, c]
+        for n, w in enumerate((wq, wv, wg, we)):
+            wt[n] = w[...].T
+        px[...] = jnp.transpose(pair_in[...], (1, 0, 2)).reshape(px.shape)
+        ux[...] = jnp.transpose(u_in[...], (1, 0, 2)).reshape(ux.shape)
         for n in range(1, 8):
             live_copy(n).wait_recv()
         live = lbuf[...].reshape(N, 128).astype(f32)
@@ -145,10 +143,9 @@
     def _():
         for n in range(1, 8):
             pd_copy(n).start()
-        own_up.wait()
-        own_pd.wait()
-        own_up2.start()
-        own_pd2.start()
+        own_up.start()
+        own_pd.start()
+        later_up.start()
 
     @pl.when(k == 2)
     def _():
@@ -168,7 +165,6 @@
                 pieces.append(rec[at:at + 1, :CW])
             rc_ref[n:n + 1, :] = jnp.concatenate(pieces, axis=1)
 
-    own_x(k).wait()
     for n in range(1, 8):
         x_copy(k, n).wait_recv()
     xin = xbuf[k].reshape(N, F)
@@ -256,8 +252,9 @@
             pd_copy(n).wait_recv()
             for c in range(2):
                 up_copy(c, n).wait_recv()
-        own_up2.wait()
-        own_pd2.wait()
+        own_up.wait()
+        own_pd.wait()
+        later_up.wait()
         for n in range(1, 8):
             live_copy(n).wait_send()
             pd_copy(n).wait_send()
@@ -393,26 +390,26 @@
 ANY = pl.BlockSpec(memory_space=pl.ANY)
 
 
-def fwd(hx, ux, px, live, wq, wk, wv, wg, we, wl, wr):
+def fwd(msa, upstream, pair, live, wq, wk, wv, wg, we, wl, wr):
     sd = jax.ShapeDtypeStruct
     V = pltpu.VMEM
     dma = pltpu.SemaphoreType.DMA
     return pl.pallas_call(
         fwd_kernel,
         grid=(4,),
-        in_specs=[ANY] * 3 + [whole((64, CW))] + [whole((F, F))] * 5 + [whole((CW, F))] * 2,
+        in_specs=[whole((64, 32, F))] * 2 + [whole((32, 64, CZ)), whole((CW, 64))] + [whole((F, F))] * 5 + [whole((CW, F))] * 2,
         out_specs=[COLS, percol((H, N, N)), percol((F, N)), percol((F, N)), percol((F, N)), percol((CW, N)),
-                   percol((CW, N)), percol((N, F)), percol((N, F)), percol((F, N)), ANY, ANY, whole((8, 256)), whole((8, N))],
+                   percol((CW, N)), percol((N, F)), percol((N, F)), percol((F, N)), ANY, ANY, ANY, whole((8, 256)), whole((8, N))],
         out_shape=[sd((8, 4, 64, F), bf16), sd((4, H, N, N), bf16), sd((4, F, N), f32), sd((4, F, N), f32),
                    sd((4, F, N), bf16), sd((4, CW, N), bf16), sd((4, CW, N), bf16),
-                   sd((4, N, F), bf16), sd((4, N, F), bf16), sd((4, F, N), bf16), sd((8, 2, 64, F), bf16), sd(px.shape, bf16), sd((8, 256), f32), sd((8, N), f32)],
-        scratch_shapes=[V((4, F, F), bf16), V((N, 128), bf16), V((2, N, N), f32), V((64, 128), bf16), V((4, 8, 64, F), bf16),
-                        V((8, 64, 128), bf16), V((128, N), f32), V((16, 8, N), f32), V((8, N), f32), V((2, 64, F), bf16),
-                        V(px.shape[1:], bf16), dma((4, 8)), dma((4, 8)), dma((4, 8)), dma((4, 8))] + [dma((8,))] * 4 + [dma((16,))] * 2 + [dma((8,))],
+                   sd((4, N, F), bf16), sd((4, N, F), bf16), sd((4, F, N), bf16), sd((8, 2, 64, F), bf16), sd((8, 2, 64, F), bf16), sd((8, 2, 4, CW, CZ), bf16), sd((8, 256), f32), sd((8, N), f32)],
+        scratch_shapes=[V((4, F, F), bf16), V((N, 128), bf16), V((2, N, N), f32), V((64, 128), bf16), V((8, 4, 64, F), bf16), V((8, 4, 64, F), bf16), V((2, 8, 4, CW, CZ), bf16), V((4, 8, 64, F), bf16),
+                        V((8, 64, 128), bf16), V((128, N), f32), V((16, 8, N), f32), V((8, N), f32),
+                        dma((4, 8)), dma((4, 8)), dma((4, 8)), dma((4, 8))] + [dma((8,))] * 4 + [dma((16,))] * 2 + [dma((8,))],
         compiler_params=pltpu.CompilerParams(vmem_limit_bytes=60 * 1024 * 1024, collective_id=2, has_side_effects=True,
                                              dimension_semantics=("arbitrary",)),
         name="attention_forward",
-    )(hx, ux, px, live, wq, wk, wv, wg, we, wl, wr)
+    )(msa, upstream, pair, live, wq, wk, wv, wg, we, wl, wr)
 
 
 def bwd(x, ua, ub, at, lg, rg, p, o, g, q, v, kt, wq, wk, wv, wg, we, wl, wr):
@@ -479,9 +476,9 @@
 
     def up_copy(n):
         dep = lax.rem(d + n, 8)
-        return remote(ux.at[dep, pl.ds(2, 2)], up.at[d], us.at[n], ur.at[n], dep, r)
-
-    own_up = pltpu.make_async_copy(ux.at[d, pl.ds(2, 2)], up.at[d], own)
+        return remote(ux.at[dep], up.at[d], us.at[n], ur.at[n], dep, r)
+
+    own_up = pltpu.make_async_copy(ux.at[d], up.at[d], own)
     own_up.start()
     for n in range(4):
         left_copy(n).start()
@@ -631,17 +628,12 @@
 
 
 def on_device(msa, present, pair, upstream, wq, wk, wv, wg, we, wl, wr, wo):
-    def by_column(a):
-        return a.transpose(1, 0, 2).reshape(8, 4, 64, F)
-
     def by_row(a):
         return a.reshape(32, 64, F).transpose(1, 0, 2)
 
-    pd = pair.reshape(32, 2, 8, 4, CZ).transpose(2, 1, 3, 0, 4)
-    ux = by_column(upstream)
-    x, p, o, g, at, lt, rt, q, v, kt, ua, pd, recip, livet = fwd(
-        by_column(msa), ux, pd, present, wq, wk, wv, wg, we, wl.T, wr.T)
-    lg, rg, ub = opm(lt.reshape(4 * CW, N), rt.reshape(4 * CW, N), pd.reshape(-1, CZ), recip, wo, livet, ux)
+    x, p, o, g, at, lt, rt, q, v, kt, ua, ut, pd, recip, livet = fwd(
+        msa, upstream, pair, present.T, wq, wk, wv, wg, we, wl.T, wr.T)
+    lg, rg, ub = opm(lt.reshape(4 * CW, N), rt.reshape(4 * CW, N), pd.reshape(-1, CZ), recip, wo, livet, ut)
     grad, inter = bwd(x, ua, ub, at, lg, rg, p, o, g, q, v, kt, wq, wk, wv, wg, we, wl.T, wr.T)
     return by_row(grad), by_row(inter)
 

time: 132 us -> 125 us (0.947)
  local copies, waits for them, and re-layouts: 12 us -> 4.03 us
    transpose x2 -> x0, local copies, waits for them, and re-layouts: 4.33 us -> none  [by_column(): return a.transpose(1, 0, 2).reshape(8, 4, 64, F)]
    reshape x1 -> x0, local copies, waits for them, and re-layouts: 2.16 us -> none  [on_device(): pd = pair.reshape(32, 2, 8, 4, CZ).transpose(2, 1, 3, 0, 4)]
    unnamed x3 -> x0, local copies, waits for them, and re-layouts: 1.51 us -> none
where the time goes in v7:
time: 125 us
  Pallas kernels  120 us (96%)
  local copies, waits for them, and re-layouts  4.03 us (3%)
    pallas_call x1, Pallas kernels, fwd(): pl.pallas_call(fwd_kernel, grid=(4,), in_specs=[whole((64, 32, F))] * 2 +...  43.6 us
    pallas_call x1, Pallas kernels, opm(): pl.pallas_call(opm_kernel, in_specs=[vm] * 6 + [ANY], out_specs=[vm] * 3,...  41.8 us
    pallas_call x1, Pallas kernels, bwd(): pl.pallas_call(bwd_kernel, grid=(4,), in_specs=[COLS, whole((8, 2, 64, F)...  34.9 us
    transpose x1, local copies, waits for them, and re-layouts, by_row(): return a.reshape(32, 64, F).transpose(1, 0, 2)  4.03 us

profile of v7, /device:TPU:0, one launch (start us, length us, event | category | flops | bytes accessed | tf_op | source)
XLA Modules:
  0.0 124.9 jit_solution(13785165906556245054)
XLA Ops:
  0.6 43.6 %attention_forward.1 = (bf16[8,4,64,256]{3,2,1,0:T(8,128)(2,1)}, bf16[4,8,512,512]{3,2,1,0:T(8,128)(2,1)}, f32[4,256,512]{2,1,0:T(8,128)}, f32[4,256,512]{2,1,0:...) custom-call(bf16[64,32,256]{2,1,0:T(8,128)(2,1)} %x_in.1, ...), custom_call_target="tpu_custom_call" | custom-call | tf_op jit(solution)/shard_map/attention_forward/pallas_call | solution.py:397
  44.2 41.8 %outer_product.1 = (bf16[4,32,512]{2,1,0:T(8,128)(2,1)}, bf16[4,32,512]{2,1,0:T(8,128)(2,1)}, bf16[8,2,64,256]{3,2,1,0:T(8,128)(2,1)}) custom-call(bf16[128,512]{1,0:T(8,128)(2,1)} %bitcast.15, bf16[128,512]{1,0:T(8,128)(2,1)} %bitcast.16, bf16[2048,128]{1,0:T(8,128)(2,1)} %bitcast.14, f32[8,256]{1,0:T(8,128)} %get-tuple-element.27.rc, ...), custom_call_target="tpu_custom_call" | custom-call | tf_op jit(solution)/shard_map/outer_product/pallas_call | solution.py:617
  86.0 34.9 %attention_backward.1 = (bf16[8,4,64,256]{3,2,1,0:T(8,128)(2,1)}, bf16[8,4,64,256]{3,2,1,0:T(8,128)(2,1)}) custom-call(bf16[8,4,64,256]{3,2,1,0:T(8,128)(2,1)} %get-tuple-element.22.x_ref, bf16[8,2,64,256]{3,2,1,0:T(8,128)(2,1)} %get-tuple-element.23.ua_ref, bf16[8,2,64,256]{3,2,1,0:T(8,128)(2,1)} %get-tuple-element.30.ub_ref, ...), custom_call_target="tpu_custom_call" | custom-call | tf_op jit(solution)/shard_map/attention_backward/pallas_call | solution.py:419
  120.9 4.0 %copy_bitcast_fusion = (bf16[64,32,256]{2,1,0:T(8,128)(2,1)}, bf16[64,32,256]{2,1,0:T(8,128)(2,1)}) fusion(bf16[32,64,256]{2,1,0:T(8,128)(2,1)} %bitcast.13, bf16[32,64,256]{2,1,0:T(8,128)(2,1)} %bitcast.12), kind=kLoop, calls=%fused_computation | loop fusion | bytes 4194304 | tf_op jit(solution)/shard_map/transpose | solution.py:632

commit v8 on v7

--- a/solution.py
+++ b/solution.py
@@ -71,9 +71,9 @@
 
 
 def fwd_kernel(x_in, u_in, pair_in, present, wq, wk, wv, wg, we, wl, wr,
-               x_ref, p_ref, o_ref, g_ref, a_ref, l_ref, r_ref, q_ref, v_ref, kt_ref, up_out, ut_out, pd_out, rc_ref, live_out,
-               wt, bias_s, st_s, live_in, hx, ux, px, xbuf, lbuf, livet, jbuf, mine,
-               xs, xr, us, ur, ps, pr, ls, lr, js, jr, own):
+               x_ref, p_out, o_ref, g_ref, a_ref, l_ref, r_ref, q_ref, v_ref, kt_ref, ut_out, pd_out, rc_ref, live_out,
+               wt, bias_s, st_s, p_buf, live_in, hx, ux, px, xbuf, lbuf, livet, jbuf, mine,
+               xs, xr, ps, pr, ls, lr, js, jr, own, p_sem):
     k = pl.program_id(0)
     d = lax.axis_index("dep")
     r = lax.axis_index("res")
@@ -87,9 +87,6 @@
     def x_copy(c, n):
         return remote(hx.at[dep_at(n), c], xbuf.at[c, d], xs.at[c, n], xr.at[c, n], dep_at(n), r)
 
-    def up_copy(c, n):
-        return remote(ux.at[dep_at(n), c], up_out.at[d, c], us.at[c, n], ur.at[c, n], dep_at(n), r)
-
     def pd_copy(n):
         return remote(px.at[:, dep_at(n)], pd_out.at[d], ps.at[n], pr.at[n], dep_at(n), r)
 
@@ -99,9 +96,18 @@
     def row_copy(n):
         return remote(mine, jbuf.at[r], js.at[n], jr.at[n], d, res_at(n))
 
-    own_up = pltpu.make_async_copy(ux.at[d, pl.ds(0, 2)], up_out.at[d], own.at[0])
     own_pd = pltpu.make_async_copy(px.at[:, d], pd_out.at[d], own.at[1])
-    later_up = pltpu.make_async_copy(ux.at[:, pl.ds(2, 2)], ut_out, own.at[2])
+    later_up = pltpu.make_async_copy(ux, ut_out, own.at[2])
+
+    half = lax.rem(k, 2)
+
+    def p_copy(at, h):
+        return pltpu.make_async_copy(p_buf.at[lax.rem(at, 2), h], p_out.at[at, h], p_sem.at[lax.rem(at, 2), h])
+
+    @pl.when(k > 1)
+    def _():
+        for h in range(H):
+            p_copy(k - 2, h).wait()
 
     @pl.when(k == 0)
     def _():
@@ -143,14 +149,8 @@
     def _():
         for n in range(1, 8):
             pd_copy(n).start()
-        own_up.start()
         own_pd.start()
         later_up.start()
-
-    @pl.when(k == 2)
-    def _():
-        for n in range(1, 8):
-            up_copy(1, n).start()
 
     @pl.when(k == 3)
     def _():
@@ -194,7 +194,7 @@
         return jnp.max(val, 0, keepdims=True)
 
     def blend(h):
-        o_ref[0, DH * h:DH * h + DH, :] = mm(vt[DH * h:DH * h + DH], p_ref[0, h])
+        o_ref[0, DH * h:DH * h + DH, :] = mm(vt[DH * h:DH * h + DH], p_buf[half, h])
 
     ops = operands(0)
     peak = functools.reduce(jnp.maximum, [score(ops, 0, i) for i in range(0, N, PIECE)])
@@ -204,17 +204,9 @@
             for n in range(1, 8):
                 x_copy(c, n).start()
 
-    def push_up(at, c):
-        @pl.when(k == at)
-        def _():
-            for n in range(1, 8):
-                up_copy(c, n).start()
-
     for h in range(H):
         if h == 2:
             push_x(0, 2)
-        if h == 4:
-            push_up(1, 0)
         if h == 5:
             push_x(0, 3)
         b = h % 2
@@ -232,7 +224,8 @@
             blend(h - 1)
         inv = 1.0 / tot
         for i in range(0, N, PIECE):
-            p_ref[0, h, i:i + PIECE, :] = (st_s[b, i:i + PIECE, :] * inv).astype(bf16)
+            p_buf[half, h, i:i + PIECE, :] = (st_s[b, i:i + PIECE, :] * inv).astype(bf16)
+        p_copy(k, h).start()
         if nxt:
             peak = functools.reduce(jnp.maximum, nxt)
     blend(H - 1)
@@ -250,24 +243,22 @@
     def _():
         for n in range(1, 8):
             pd_copy(n).wait_recv()
-            for c in range(2):
-                up_copy(c, n).wait_recv()
-        own_up.wait()
         own_pd.wait()
         later_up.wait()
+        for h in range(H):
+            p_copy(2, h).wait()
+            p_copy(3, h).wait()
         for n in range(1, 8):
             live_copy(n).wait_send()
             pd_copy(n).wait_send()
-            for c in range(2):
-                up_copy(c, n).wait_send()
             for c in range(1, 4):
                 x_copy(c, n).wait_send()
         for n in range(1, 16):
             row_copy(n).wait_send()
 
 
-def bwd_kernel(x_ref, ua_ref, ub_ref, at_ref, lg_ref, rg_ref, p_ref, o_ref, g_ref, q_ref, v_ref, kt_ref, wq, wk, wv, wg, we, wl, wr,
-               out_g, out_i, ds_s, acc_q, acc_v, acc_t, dt_s, sbuf, ss, rs, own):
+def bwd_kernel(x_ref, up_ref, at_ref, lg_ref, rg_ref, p_in, o_ref, g_ref, q_ref, v_ref, kt_ref, wq, wk, wv, wg, we, wl, wr,
+               out_g, out_i, p_buf, ds_s, acc_q, acc_v, acc_t, dt_s, sbuf, ss, rs, own, p_sem):
     k = pl.program_id(0)
     d = lax.axis_index("dep")
     r = lax.axis_index("res")
@@ -289,8 +280,15 @@
             send(which, c, n).start()
         keep(which, c).start()
 
+    half = lax.rem(k, 2)
+
+    def p_copy(at):
+        return pltpu.make_async_copy(p_in.at[at], p_buf.at[lax.rem(at, 2)], p_sem.at[lax.rem(at, 2)])
+
     @pl.when(k == 0)
     def _():
+        p_copy(0).start()
+        p_copy(1).start()
         wlt, wrt = wl[...].T, wr[...].T
         greet([(dep_at(n), r) for n in range(1, 8)])
         for c in range(4):
@@ -298,10 +296,11 @@
             dy = mm(wlt, lg_ref[c]) + mm(wrt, rg_ref[c])
             m1 = jnp.mean(dy, 0, keepdims=True)
             m2 = jnp.mean(dy * yhat, 0, keepdims=True)
-            upt = (ua_ref if c < 2 else ub_ref)[:, c % 2].reshape(N, F).T.astype(f32)
+            upt = up_ref[:, c].reshape(N, F).T.astype(f32)
             dt_s[c] = (yinv * (dy - m1 - yhat * m2) + upt).astype(bf16)
             ship(1, c, dt_s[c])
 
+    p_copy(k).wait()
     xin = x_ref[...].reshape(N, F)
     q = q_ref[0]
     v = v_ref[0]
@@ -334,7 +333,7 @@
 
     def wide_v(h):
         sl = slice(DH * h, DH * h + DH)
-        acc_v[sl, :] = mmt(dot_[sl], p_ref[0, h])
+        acc_v[sl, :] = mmt(dot_[sl], p_buf[half, h])
 
     def tall_k(h, i):
         ext = mm(ds_s[h, i:i + 256, :], jnp.where(lane == h, q, zero))
@@ -347,7 +346,7 @@
         ops = dops(h)
         for i in range(0, N, 256):
             dp = mm(ops[0][i:i + 256], ops[1])
-            ds_s[h, i:i + 256, :] = (p_ref[0, h, i:i + 256, :].astype(f32) * dp).astype(bf16)
+            ds_s[h, i:i + 256, :] = (p_buf[half, h, i:i + 256, :].astype(f32) * dp).astype(bf16)
             if h:
                 tall_k(h - 1, i)
         wide_v(h)
@@ -368,6 +367,10 @@
     out = (dt.astype(f32) + dln.astype(f32)).astype(bf16)
     ship(0, k, out)
 
+    @pl.when(k < 2)
+    def _():
+        p_copy(k + 2).start()
+
     @pl.when(k == 3)
     def _():
         for which in range(2):
@@ -398,37 +401,37 @@
         fwd_kernel,
         grid=(4,),
         in_specs=[whole((64, 32, F))] * 2 + [whole((32, 64, CZ)), whole((CW, 64))] + [whole((F, F))] * 5 + [whole((CW, F))] * 2,
-        out_specs=[COLS, percol((H, N, N)), percol((F, N)), percol((F, N)), percol((F, N)), percol((CW, N)),
-                   percol((CW, N)), percol((N, F)), percol((N, F)), percol((F, N)), ANY, ANY, ANY, whole((8, 256)), whole((8, N))],
+        out_specs=[COLS, ANY, percol((F, N)), percol((F, N)), percol((F, N)), percol((CW, N)),
+                   percol((CW, N)), percol((N, F)), percol((N, F)), percol((F, N)), ANY, ANY, whole((8, 256)), whole((8, N))],
         out_shape=[sd((8, 4, 64, F), bf16), sd((4, H, N, N), bf16), sd((4, F, N), f32), sd((4, F, N), f32),
                    sd((4, F, N), bf16), sd((4, CW, N), bf16), sd((4, CW, N), bf16),
-                   sd((4, N, F), bf16), sd((4, N, F), bf16), sd((4, F, N), bf16), sd((8, 2, 64, F), bf16), sd((8, 2, 64, F), bf16), sd((8, 2, 4, CW, CZ), bf16), sd((8, 256), f32), sd((8, N), f32)],
-        scratch_shapes=[V((4, F, F), bf16), V((N, 128), bf16), V((2, N, N), f32), V((64, 128), bf16), V((8, 4, 64, F), bf16), V((8, 4, 64, F), bf16), V((2, 8, 4, CW, CZ), bf16), V((4, 8, 64, F), bf16),
+                   sd((4, N, F), bf16), sd((4, N, F), bf16), sd((4, F, N), bf16), sd((8, 4, 64, F), bf16), sd((8, 2, 4, CW, CZ), bf16), sd((8, 256), f32), sd((8, N), f32)],
+        scratch_shapes=[V((4, F, F), bf16), V((N, 128), bf16), V((2, N, N), f32), V((2, H, N, N), bf16), V((64, 128), bf16), V((8, 4, 64, F), bf16), V((8, 4, 64, F), bf16), V((2, 8, 4, CW, CZ), bf16), V((4, 8, 64, F), bf16),
                         V((8, 64, 128), bf16), V((128, N), f32), V((16, 8, N), f32), V((8, N), f32),
-                        dma((4, 8)), dma((4, 8)), dma((4, 8)), dma((4, 8))] + [dma((8,))] * 4 + [dma((16,))] * 2 + [dma((8,))],
+                        dma((4, 8)), dma((4, 8))] + [dma((8,))] * 4 + [dma((16,))] * 2 + [dma((8,)), dma((2, 8))],
         compiler_params=pltpu.CompilerParams(vmem_limit_bytes=60 * 1024 * 1024, collective_id=2, has_side_effects=True,
                                              dimension_semantics=("arbitrary",)),
         name="attention_forward",
     )(msa, upstream, pair, live, wq, wk, wv, wg, we, wl, wr)
 
 
-def bwd(x, ua, ub, at, lg, rg, p, o, g, q, v, kt, wq, wk, wv, wg, we, wl, wr):
+def bwd(x, up, at, lg, rg, p, o, g, q, v, kt, wq, wk, wv, wg, we, wl, wr):
     sd = jax.ShapeDtypeStruct
     V = pltpu.VMEM
     dma = pltpu.SemaphoreType.DMA
     return pl.pallas_call(
         bwd_kernel,
         grid=(4,),
-        in_specs=[COLS, whole((8, 2, 64, F)), whole((8, 2, 64, F)), whole((4, F, N)), whole((4, CW, N)), whole((4, CW, N)), percol((H, N, N)), percol((F, N)),
+        in_specs=[COLS, whole((8, 4, 64, F)), whole((4, F, N)), whole((4, CW, N)), whole((4, CW, N)), ANY, percol((F, N)),
                   percol((F, N)), percol((N, F)), percol((N, F)), percol((F, N))] + [whole((F, F))] * 5 + [whole((CW, F))] * 2,
         out_specs=[ANY, ANY],
         out_shape=[sd((8, 4, 64, F), bf16)] * 2,
-        scratch_shapes=[V((H, N, N), bf16), V((F, N), f32), V((F, N), f32), V((N, F), f32), V((4, F, N), bf16), V((2, 4, 8, 64, F), bf16),
-                        dma((2, 4, 8)), dma((2, 4, 8)), dma((2, 4))],
+        scratch_shapes=[V((2, H, N, N), bf16), V((H, N, N), bf16), V((F, N), f32), V((F, N), f32), V((N, F), f32), V((4, F, N), bf16), V((2, 4, 8, 64, F), bf16),
+                        dma((2, 4, 8)), dma((2, 4, 8)), dma((2, 4)), dma((2,))],
         compiler_params=pltpu.CompilerParams(vmem_limit_bytes=60 * 1024 * 1024, collective_id=3, has_side_effects=True,
                                              dimension_semantics=("arbitrary",)),
         name="attention_backward",
-    )(x, ua, ub, at, lg, rg, p, o, g, q, v, kt, wq, wk, wv, wg, we, wl, wr)
+    )(x, up, at, lg, rg, p, o, g, q, v, kt, wq, wk, wv, wg, we, wl, wr)
 
 
 def opm_kernel(lt, rt, pd, rc, wo, live, ux, lo, ro, up,
@@ -618,7 +621,7 @@
         opm_kernel,
         in_specs=[vm] * 6 + [ANY],
         out_specs=[vm] * 3,
-        out_shape=[sd((4, CW, N), bf16)] * 2 + [sd((8, 2, 64, F), bf16)],
+        out_shape=[sd((4, CW, N), bf16)] * 2 + [sd((8, 4, 64, F), bf16)],
         scratch_shapes=[V((1024, 1024), bf16), V((2048, 1024), bf16), V((1024, 2048), bf16),
                         V((8, *chunk), bf16), V((16, *chunk), bf16)] + [V((8, *chunk), bf16)] * 6
         + [V((8, 256, N), f32)] + [V(chunk, f32)] * 2 + [dma] * 14 + [pltpu.SemaphoreType.DMA],
@@ -631,10 +634,10 @@
     def by_row(a):
         return a.reshape(32, 64, F).transpose(1, 0, 2)
 
-    x, p, o, g, at, lt, rt, q, v, kt, ua, ut, pd, recip, livet = fwd(
+    x, p, o, g, at, lt, rt, q, v, kt, ut, pd, recip, livet = fwd(
         msa, upstream, pair, present.T, wq, wk, wv, wg, we, wl.T, wr.T)
-    lg, rg, ub = opm(lt.reshape(4 * CW, N), rt.reshape(4 * CW, N), pd.reshape(-1, CZ), recip, wo, livet, ut)
-    grad, inter = bwd(x, ua, ub, at, lg, rg, p, o, g, q, v, kt, wq, wk, wv, wg, we, wl.T, wr.T)
+    lg, rg, up = opm(lt.reshape(4 * CW, N), rt.reshape(4 * CW, N), pd.reshape(-1, CZ), recip, wo, livet, ut)
+    grad, inter = bwd(x, up, at, lg, rg, p, o, g, q, v, kt, wq, wk, wv, wg, we, wl.T, wr.T)
     return by_row(grad), by_row(inter)
 
 

time: 125 us -> 126 us (level); the launches traced: 125 us -> 124 us
    pallas_call x1, Pallas kernels: 41.8 us -> 44.8 us  [opm(): pl.pallas_call(opm_kernel, in_specs=[vm] * 6 + [ANY], out_specs=[vm] * 3,...]
    pallas_call x1, Pallas kernels: 43.6 us -> 41.1 us  [fwd(): pl.pallas_call(fwd_kernel, grid=(4,), in_specs=[whole((64, 32, F))] * 2 +...]
where the time goes in v8:
time: 126 us; the launch traced here: 124 us
  Pallas kernels  120 us (95%)
  local copies, waits for them, and re-layouts  4.03 us (3%)
    pallas_call x1, Pallas kernels, opm(): pl.pallas_call(opm_kernel, in_specs=[vm] * 6 + [ANY], out_specs=[vm] * 3,...  44.8 us
    pallas_call x1, Pallas kernels, fwd(): pl.pallas_call(fwd_kernel, grid=(4,), in_specs=[whole((64, 32, F))] * 2 +...  41.1 us
    pallas_call x1, Pallas kernels, bwd(): pl.pallas_call(bwd_kernel, grid=(4,), in_specs=[COLS, whole((8, 4, 64, F)...  33.8 us
    transpose x1, local copies, waits for them, and re-layouts, by_row(): return a.reshape(32, 64, F).transpose(1, 0, 2)  4.03 us

profile of v8, /device:TPU:0, one launch (start us, length us, event | category | flops | bytes accessed | tf_op | source)
XLA Modules:
  0.0 124.4 jit_solution(10723982166164220561)
XLA Ops:
  0.6 41.1 %attention_forward.1 = (bf16[8,4,64,256]{3,2,1,0:T(8,128)(2,1)}, bf16[4,8,512,512]{3,2,1,0:T(8,128)(2,1)}, f32[4,256,512]{2,1,0:T(8,128)}, f32[4,256,512]{2,1,0:...) custom-call(bf16[64,32,256]{2,1,0:T(8,128)(2,1)} %x_in.1, ...), custom_call_target="tpu_custom_call" | custom-call | tf_op jit(solution)/shard_map/attention_forward/pallas_call | solution.py:400
  41.8 44.8 %outer_product.1 = (bf16[4,32,512]{2,1,0:T(8,128)(2,1)}, bf16[4,32,512]{2,1,0:T(8,128)(2,1)}, bf16[8,4,64,256]{3,2,1,0:T(8,128)(2,1)}) custom-call(bf16[128,512]{1,0:T(8,128)(2,1)} %bitcast.15, bf16[128,512]{1,0:T(8,128)(2,1)} %bitcast.16, bf16[2048,128]{1,0:T(8,128)(2,1)} %bitcast.14, f32[8,256]{1,0:T(8,128)} %get-tuple-element.25.rc, ...), custom_call_target="tpu_custom_call" | custom-call | tf_op jit(solution)/shard_map/outer_product/pallas_call | solution.py:620
  86.6 33.8 %attention_backward.1 = (bf16[8,4,64,256]{3,2,1,0:T(8,128)(2,1)}, bf16[8,4,64,256]{3,2,1,0:T(8,128)(2,1)}) custom-call(bf16[8,4,64,256]{3,2,1,0:T(8,128)(2,1)} %get-tuple-element.21.x_ref, bf16[8,4,64,256]{3,2,1,0:T(8,128)(2,1)} %get-tuple-element.28.up_ref, bf16[4,256,512]{2,1,0:T(8,128)(2,1)} %get-tuple-element.29.at_ref, ...), custom_call_target="tpu_custom_call" | custom-call | tf_op jit(solution)/shard_map/attention_backward/pallas_call | solution.py:422
  120.4 4.0 %copy_bitcast_fusion = (bf16[64,32,256]{2,1,0:T(8,128)(2,1)}, bf16[64,32,256]{2,1,0:T(8,128)(2,1)}) fusion(bf16[32,64,256]{2,1,0:T(8,128)(2,1)} %bitcast.13, bf16[32,64,256]{2,1,0:T(8,128)(2,1)} %bitcast.12), kind=kLoop, calls=%fused_computation | loop fusion | bytes 4194304 | tf_op jit(solution)/shard_map/transpose | solution.py:635

commit v9 on v8

--- a/solution.py
+++ b/solution.py
@@ -71,9 +71,9 @@
 
 
 def fwd_kernel(x_in, u_in, pair_in, present, wq, wk, wv, wg, we, wl, wr,
-               x_ref, p_out, o_ref, g_ref, a_ref, l_ref, r_ref, q_ref, v_ref, kt_ref, ut_out, pd_out, rc_ref, live_out,
+               x_ref, p_out, o_ref, g_ref, a_ref, l_ref, r_ref, q_ref, v_ref, kt_ref, up_out, ut_out, pd_out, rc_ref, live_out,
                wt, bias_s, st_s, p_buf, live_in, hx, ux, px, xbuf, lbuf, livet, jbuf, mine,
-               xs, xr, ps, pr, ls, lr, js, jr, own, p_sem):
+               xs, xr, us, ur, ps, pr, ls, lr, js, jr, own, p_sem):
     k = pl.program_id(0)
     d = lax.axis_index("dep")
     r = lax.axis_index("res")
@@ -87,6 +87,9 @@
     def x_copy(c, n):
         return remote(hx.at[dep_at(n), c], xbuf.at[c, d], xs.at[c, n], xr.at[c, n], dep_at(n), r)
 
+    def up_copy(c, n):
+        return remote(ux.at[dep_at(n), c], up_out.at[d, c], us.at[c, n], ur.at[c, n], dep_at(n), r)
+
     def pd_copy(n):
         return remote(px.at[:, dep_at(n)], pd_out.at[d], ps.at[n], pr.at[n], dep_at(n), r)
 
@@ -96,8 +99,9 @@
     def row_copy(n):
         return remote(mine, jbuf.at[r], js.at[n], jr.at[n], d, res_at(n))
 
+    own_up = pltpu.make_async_copy(ux.at[d, pl.ds(0, 2)], up_out.at[d], own.at[0])
     own_pd = pltpu.make_async_copy(px.at[:, d], pd_out.at[d], own.at[1])
-    later_up = pltpu.make_async_copy(ux, ut_out, own.at[2])
+    later_up = pltpu.make_async_copy(ux.at[:, pl.ds(2, 2)], ut_out, own.at[2])
 
     half = lax.rem(k, 2)
 
@@ -149,8 +153,14 @@
     def _():
         for n in range(1, 8):
             pd_copy(n).start()
+        own_up.start()
         own_pd.start()
         later_up.start()
+
+    @pl.when(k == 2)
+    def _():
+        for n in range(1, 8):
+            up_copy(1, n).start()
 
     @pl.when(k == 3)
     def _():
@@ -204,9 +214,17 @@
             for n in range(1, 8):
                 x_copy(c, n).start()
 
+    def push_up(at, c):
+        @pl.when(k == at)
+        def _():
+            for n in range(1, 8):
+                up_copy(c, n).start()
+
     for h in range(H):
         if h == 2:
             push_x(0, 2)
+        if h == 4:
+            push_up(1, 0)
         if h == 5:
             push_x(0, 3)
         b = h % 2
@@ -243,6 +261,9 @@
     def _():
         for n in range(1, 8):
             pd_copy(n).wait_recv()
+            for c in range(2):
+                up_copy(c, n).wait_recv()
+        own_up.wait()
         own_pd.wait()
         later_up.wait()
         for h in range(H):
@@ -251,13 +272,15 @@
         for n in range(1, 8):
             live_copy(n).wait_send()
             pd_copy(n).wait_send()
+            for c in range(2):
+                up_copy(c, n).wait_send()
             for c in range(1, 4):
                 x_copy(c, n).wait_send()
         for n in range(1, 16):
             row_copy(n).wait_send()
 
 
-def bwd_kernel(x_ref, up_ref, at_ref, lg_ref, rg_ref, p_in, o_ref, g_ref, q_ref, v_ref, kt_ref, wq, wk, wv, wg, we, wl, wr,
+def bwd_kernel(x_ref, ua_ref, ub_ref, at_ref, lg_ref, rg_ref, p_in, o_ref, g_ref, q_ref, v_ref, kt_ref, wq, wk, wv, wg, we, wl, wr,
                out_g, out_i, p_buf, ds_s, acc_q, acc_v, acc_t, dt_s, sbuf, ss, rs, own, p_sem):
     k = pl.program_id(0)
     d = lax.axis_index("dep")
@@ -296,7 +319,7 @@
             dy = mm(wlt, lg_ref[c]) + mm(wrt, rg_ref[c])
             m1 = jnp.mean(dy, 0, keepdims=True)
             m2 = jnp.mean(dy * yhat, 0, keepdims=True)
-            upt = up_ref[:, c].reshape(N, F).T.astype(f32)
+            upt = (ua_ref if c < 2 else ub_ref)[:, c % 2].reshape(N, F).T.astype(f32)
             dt_s[c] = (yinv * (dy - m1 - yhat * m2) + upt).astype(bf16)
             ship(1, c, dt_s[c])
 
@@ -402,27 +425,27 @@
         grid=(4,),
         in_specs=[whole((64, 32, F))] * 2 + [whole((32, 64, CZ)), whole((CW, 64))] + [whole((F, F))] * 5 + [whole((CW, F))] * 2,
         out_specs=[COLS, ANY, percol((F, N)), percol((F, N)), percol((F, N)), percol((CW, N)),
-                   percol((CW, N)), percol((N, F)), percol((N, F)), percol((F, N)), ANY, ANY, whole((8, 256)), whole((8, N))],
+                   percol((CW, N)), percol((N, F)), percol((N, F)), percol((F, N)), ANY, ANY, ANY, whole((8, 256)), whole((8, N))],
         out_shape=[sd((8, 4, 64, F), bf16), sd((4, H, N, N), bf16), sd((4, F, N), f32), sd((4, F, N), f32),
                    sd((4, F, N), bf16), sd((4, CW, N), bf16), sd((4, CW, N), bf16),
-                   sd((4, N, F), bf16), sd((4, N, F), bf16), sd((4, F, N), bf16), sd((8, 4, 64, F), bf16), sd((8, 2, 4, CW, CZ), bf16), sd((8, 256), f32), sd((8, N), f32)],
+                   sd((4, N, F), bf16), sd((4, N, F), bf16), sd((4, F, N), bf16), sd((8, 2, 64, F), bf16), sd((8, 2, 64, F), bf16), sd((8, 2, 4, CW, CZ), bf16), sd((8, 256), f32), sd((8, N), f32)],
         scratch_shapes=[V((4, F, F), bf16), V((N, 128), bf16), V((2, N, N), f32), V((2, H, N, N), bf16), V((64, 128), bf16), V((8, 4, 64, F), bf16), V((8, 4, 64, F), bf16), V((2, 8, 4, CW, CZ), bf16), V((4, 8, 64, F), bf16),
                         V((8, 64, 128), bf16), V((128, N), f32), V((16, 8, N), f32), V((8, N), f32),
-                        dma((4, 8)), dma((4, 8))] + [dma((8,))] * 4 + [dma((16,))] * 2 + [dma((8,)), dma((2, 8))],
+                        dma((4, 8)), dma((4, 8)), dma((4, 8)), dma((4, 8))] + [dma((8,))] * 4 + [dma((16,))] * 2 + [dma((8,)), dma((2, 8))],
         compiler_params=pltpu.CompilerParams(vmem_limit_bytes=60 * 1024 * 1024, collective_id=2, has_side_effects=True,
                                              dimension_semantics=("arbitrary",)),
         name="attention_forward",
     )(msa, upstream, pair, live, wq, wk, wv, wg, we, wl, wr)
 
 
-def bwd(x, up, at, lg, rg, p, o, g, q, v, kt, wq, wk, wv, wg, we, wl, wr):
+def bwd(x, ua, ub, at, lg, rg, p, o, g, q, v, kt, wq, wk, wv, wg, we, wl, wr):
     sd = jax.ShapeDtypeStruct
     V = pltpu.VMEM
     dma = pltpu.SemaphoreType.DMA
     return pl.pallas_call(
         bwd_kernel,
         grid=(4,),
-        in_specs=[COLS, whole((8, 4, 64, F)), whole((4, F, N)), whole((4, CW, N)), whole((4, CW, N)), ANY, percol((F, N)),
+        in_specs=[COLS, whole((8, 2, 64, F)), whole((8, 2, 64, F)), whole((4, F, N)), whole((4, CW, N)), whole((4, CW, N)), ANY, percol((F, N)),
                   percol((F, N)), percol((N, F)), percol((N, F)), percol((F, N))] + [whole((F, F))] * 5 + [whole((CW, F))] * 2,
         out_specs=[ANY, ANY],
         out_shape=[sd((8, 4, 64, F), bf16)] * 2,
@@ -431,7 +454,7 @@
         compiler_params=pltpu.CompilerParams(vmem_limit_bytes=60 * 1024 * 1024, collective_id=3, has_side_effects=True,
                                              dimension_semantics=("arbitrary",)),
         name="attention_backward",
-    )(x, up, at, lg, rg, p, o, g, q, v, kt, wq, wk, wv, wg, we, wl, wr)
+    )(x, ua, ub, at, lg, rg, p, o, g, q, v, kt, wq, wk, wv, wg, we, wl, wr)
 
 
 def opm_kernel(lt, rt, pd, rc, wo, live, ux, lo, ro, up,
@@ -518,11 +541,6 @@
                 right_copy(i).start()
             across(0).start()
 
-        @pl.when(n == 6)
-        def _():
-            for i in range(1, 8):
-                up_copy(i).start()
-
         @pl.when(n == 5)
         def _():
             for i in range(1, 4):
@@ -533,6 +551,8 @@
     lax.fori_loop(0, 8, outer_step, 0)
     for n in range(1, 7):
         left_copy(n).wait_recv()
+    for n in range(1, 8):
+        up_copy(n).start()
     for n in range(4, 7):
         right_copy(n).wait_recv()
         across(n).start()
@@ -621,7 +641,7 @@
         opm_kernel,
         in_specs=[vm] * 6 + [ANY],
         out_specs=[vm] * 3,
-        out_shape=[sd((4, CW, N), bf16)] * 2 + [sd((8, 4, 64, F), bf16)],
+        out_shape=[sd((4, CW, N), bf16)] * 2 + [sd((8, 2, 64, F), bf16)],
         scratch_shapes=[V((1024, 1024), bf16), V((2048, 1024), bf16), V((1024, 2048), bf16),
                         V((8, *chunk), bf16), V((16, *chunk), bf16)] + [V((8, *chunk), bf16)] * 6
         + [V((8, 256, N), f32)] + [V(chunk, f32)] * 2 + [dma] * 14 + [pltpu.SemaphoreType.DMA],
@@ -634,10 +654,10 @@
     def by_row(a):
         return a.reshape(32, 64, F).transpose(1, 0, 2)
 
-    x, p, o, g, at, lt, rt, q, v, kt, ut, pd, recip, livet = fwd(
+    x, p, o, g, at, lt, rt, q, v, kt, ua, ut, pd, recip, livet = fwd(
         msa, upstream, pair, present.T, wq, wk, wv, wg, we, wl.T, wr.T)
-    lg, rg, up = opm(lt.reshape(4 * CW, N), rt.reshape(4 * CW, N), pd.reshape(-1, CZ), recip, wo, livet, ut)
-    grad, inter = bwd(x, up, at, lg, rg, p, o, g, q, v, kt, wq, wk, wv, wg, we, wl.T, wr.T)
+    lg, rg, ub = opm(lt.reshape(4 * CW, N), rt.reshape(4 * CW, N), pd.reshape(-1, CZ), recip, wo, livet, ut)
+    grad, inter = bwd(x, ua, ub, at, lg, rg, p, o, g, q, v, kt, wq, wk, wv, wg, we, wl.T, wr.T)
     return by_row(grad), by_row(inter)
 
 

time: 126 us -> 121 us (0.960)
  Pallas kernels: 120 us -> 116 us
    pallas_call x1, Pallas kernels: 44.8 us -> 40.6 us  [opm(): pl.pallas_call(opm_kernel, in_specs=[vm] * 6 + [ANY], out_specs=[vm] * 3,...]
    pallas_call x1, Pallas kernels: 41.1 us -> 42.5 us  [fwd(): pl.pallas_call(fwd_kernel, grid=(4,), in_specs=[whole((64, 32, F))] * 2 +...]
where the time goes in v9:
time: 121 us; the launch traced here: 120 us
  Pallas kernels  116 us (96%)
  local copies, waits for them, and re-layouts  4.03 us (3%)
    pallas_call x1, Pallas kernels, fwd(): pl.pallas_call(fwd_kernel, grid=(4,), in_specs=[whole((64, 32, F))] * 2 +...  42.5 us
    pallas_call x1, Pallas kernels, opm(): pl.pallas_call(opm_kernel, in_specs=[vm] * 6 + [ANY], out_specs=[vm] * 3,...  40.6 us
    pallas_call x1, Pallas kernels, bwd(): pl.pallas_call(bwd_kernel, grid=(4,), in_specs=[COLS, whole((8, 2, 64, F)...  32.8 us
    transpose x1, local copies, waits for them, and re-layouts, by_row(): return a.reshape(32, 64, F).transpose(1, 0, 2)  4.03 us

profile of v9, /device:TPU:0, one launch (start us, length us, event | category | flops | bytes accessed | tf_op | source)
XLA Modules:
  0.0 120.5 jit_solution(6592303642608433967)
XLA Ops:
  0.6 42.5 %attention_forward.1 = (bf16[8,4,64,256]{3,2,1,0:T(8,128)(2,1)}, bf16[4,8,512,512]{3,2,1,0:T(8,128)(2,1)}, f32[4,256,512]{2,1,0:T(8,128)}, f32[4,256,512]{2,1,0:...) custom-call(bf16[64,32,256]{2,1,0:T(8,128)(2,1)} %x_in.1, ...), custom_call_target="tpu_custom_call" | custom-call | tf_op jit(solution)/shard_map/attention_forward/pallas_call | solution.py:423
  43.1 40.6 %outer_product.1 = (bf16[4,32,512]{2,1,0:T(8,128)(2,1)}, bf16[4,32,512]{2,1,0:T(8,128)(2,1)}, bf16[8,2,64,256]{3,2,1,0:T(8,128)(2,1)}) custom-call(bf16[128,512]{1,0:T(8,128)(2,1)} %bitcast.15, bf16[128,512]{1,0:T(8,128)(2,1)} %bitcast.16, bf16[2048,128]{1,0:T(8,128)(2,1)} %bitcast.14, f32[8,256]{1,0:T(8,128)} %get-tuple-element.27.rc, ...), custom_call_target="tpu_custom_call" | custom-call | tf_op jit(solution)/shard_map/outer_product/pallas_call | solution.py:640
  83.7 32.8 %attention_backward.1 = (bf16[8,4,64,256]{3,2,1,0:T(8,128)(2,1)}, bf16[8,4,64,256]{3,2,1,0:T(8,128)(2,1)}) custom-call(bf16[8,4,64,256]{3,2,1,0:T(8,128)(2,1)} %get-tuple-element.22.x_ref, bf16[8,2,64,256]{3,2,1,0:T(8,128)(2,1)} %get-tuple-element.23.ua_ref, bf16[8,2,64,256]{3,2,1,0:T(8,128)(2,1)} %get-tuple-element.30.ub_ref, ...), custom_call_target="tpu_custom_call" | custom-call | tf_op jit(solution)/shard_map/attention_backward/pallas_call | solution.py:445
  116.5 4.0 %copy_bitcast_fusion = (bf16[64,32,256]{2,1,0:T(8,128)(2,1)}, bf16[64,32,256]{2,1,0:T(8,128)(2,1)}) fusion(bf16[32,64,256]{2,1,0:T(8,128)(2,1)} %bitcast.13, bf16[32,64,256]{2,1,0:T(8,128)(2,1)} %bitcast.12), kind=kLoop, calls=%fused_computation | loop fusion | bytes 4194304 | tf_op jit(solution)/shard_map/transpose | solution.py:655

commit v10 on v9

--- a/solution.py
+++ b/solution.py
@@ -142,15 +142,15 @@
         mine[...] = held
         live_out[...] = held
         jbuf[r] = held
+        for n in range(1, 8):
+            x_copy(0, n).wait_send()
+        for n in range(1, 8):
+            x_copy(1, n).start()
+
+    @pl.when(k == 1)
+    def _():
         for n in range(1, 16):
             row_copy(n).start()
-        for n in range(1, 8):
-            x_copy(0, n).wait_send()
-        for n in range(1, 8):
-            x_copy(1, n).start()
-
-    @pl.when(k == 1)
-    def _():
         for n in range(1, 8):
             pd_copy(n).start()
         own_up.start()
@@ -312,8 +312,9 @@
     def _():
         p_copy(0).start()
         p_copy(1).start()
+        hail([(dep_at(n), r) for n in range(1, 8)])
         wlt, wrt = wl[...].T, wr[...].T
-        greet([(dep_at(n), r) for n in range(1, 8)])
+        gather_all(7)
         for c in range(4):
             yhat, yinv = norm(at_ref[c].astype(f32), 0)
             dy = mm(wlt, lg_ref[c]) + mm(wrt, rg_ref[c])
@@ -572,13 +573,13 @@
 
     mine = pl.ds(pl.multiple_of(128 * core, 128), 128)
     theirs = pl.ds(pl.multiple_of(128 * (1 - core), 128), 128)
-    lall = lbuf[...].reshape(1024, N)
-    for i, (flip, step) in enumerate(order):
-        at = pl.multiple_of(256 * chip_of(flip, step), 256)
-        both[i] = mm(oc1[pl.ds(at, 256), :], lall)
+    def right_mm(i):
+        at = pl.multiple_of(256 * chip_of(*order[i]), 256)
+        both[i] = mm(oc1[pl.ds(at, 256), :], lbuf[...].reshape(1024, N))
         psend[i] = both[i, theirs, :].astype(bf16)
         pass_over(i).start()
-    for i in range(8):
+
+    def right_send(i):
         pass_over(i).wait_recv()
         own = both[i, mine, :] + precv[i].astype(f32)
         if i in (3, 7):
@@ -586,12 +587,10 @@
         else:
             rsend[i] = own.astype(bf16)
             right_part(i).start()
-    for n in range(8):
-        across(n).wait_recv()
-    rall = rbuf[...].reshape(2048, N)
-    for i, (flip, step) in enumerate(order):
-        at = pl.multiple_of(128 * dep_of(flip, step), 128)
-        own = mm(oc2[pl.ds(at, 128), :], rall)
+
+    def left_mm(i):
+        at = pl.multiple_of(128 * dep_of(*order[i]), 128)
+        own = mm(oc2[pl.ds(at, 128), :], rbuf[...].reshape(2048, N))
         if i == 3:
             lkeep[...] = own
         elif i == 7:
@@ -599,6 +598,17 @@
         else:
             lsend[i] = own.astype(bf16)
             left_part(i).start()
+
+    for grp in (range(4), range(4, 8)):
+        for i in grp:
+            right_mm(i)
+        if grp[0] == 0:
+            for n in range(8):
+                across(n).wait_recv()
+        for i in grp:
+            left_mm(i)
+        for i in grp:
+            right_send(i)
     for i in range(3):
         right_part(i).wait_recv()
     rsend[3] = (both[3, mine, :] + jnp.sum(rrecv[0:3].astype(f32), 0)).astype(bf16)

time: 121 us -> 121 us (level)
  no operation moved by 1% of the time
where the time goes in v10:
time: 121 us; the launch traced here: 120 us
  Pallas kernels  116 us (96%)
  local copies, waits for them, and re-layouts  4.03 us (3%)
    pallas_call x1, Pallas kernels, fwd(): pl.pallas_call(fwd_kernel, grid=(4,), in_specs=[whole((64, 32, F))] * 2 +...  43.4 us
    pallas_call x1, Pallas kernels, opm(): pl.pallas_call(opm_kernel, in_specs=[vm] * 6 + [ANY], out_specs=[vm] * 3,...  39.4 us
    pallas_call x1, Pallas kernels, bwd(): pl.pallas_call(bwd_kernel, grid=(4,), in_specs=[COLS, whole((8, 2, 64, F)...  33 us
    transpose x1, local copies, waits for them, and re-layouts, by_row(): return a.reshape(32, 64, F).transpose(1, 0, 2)  4.03 us

profile of v10, /device:TPU:0, one launch (start us, length us, event | category | flops | bytes accessed | tf_op | source)
XLA Modules:
  0.0 120.5 jit_solution(7632266363823599193)
XLA Ops:
  0.6 43.4 %attention_forward.1 = (bf16[8,4,64,256]{3,2,1,0:T(8,128)(2,1)}, bf16[4,8,512,512]{3,2,1,0:T(8,128)(2,1)}, f32[4,256,512]{2,1,0:T(8,128)}, f32[4,256,512]{2,1,0:...) custom-call(bf16[64,32,256]{2,1,0:T(8,128)(2,1)} %x_in.1, ...), custom_call_target="tpu_custom_call" | custom-call | tf_op jit(solution)/shard_map/attention_forward/pallas_call | solution.py:424
  44.0 39.4 %outer_product.1 = (bf16[4,32,512]{2,1,0:T(8,128)(2,1)}, bf16[4,32,512]{2,1,0:T(8,128)(2,1)}, bf16[8,2,64,256]{3,2,1,0:T(8,128)(2,1)}) custom-call(bf16[128,512]{1,0:T(8,128)(2,1)} %bitcast.15, bf16[128,512]{1,0:T(8,128)(2,1)} %bitcast.16, bf16[2048,128]{1,0:T(8,128)(2,1)} %bitcast.14, f32[8,256]{1,0:T(8,128)} %get-tuple-element.27.rc, ...), custom_call_target="tpu_custom_call" | custom-call | tf_op jit(solution)/shard_map/outer_product/pallas_call | solution.py:650
  83.4 33.0 %attention_backward.1 = (bf16[8,4,64,256]{3,2,1,0:T(8,128)(2,1)}, bf16[8,4,64,256]{3,2,1,0:T(8,128)(2,1)}) custom-call(bf16[8,4,64,256]{3,2,1,0:T(8,128)(2,1)} %get-tuple-element.22.x_ref, bf16[8,2,64,256]{3,2,1,0:T(8,128)(2,1)} %get-tuple-element.23.ua_ref, bf16[8,2,64,256]{3,2,1,0:T(8,128)(2,1)} %get-tuple-element.30.ub_ref, ...), custom_call_target="tpu_custom_call" | custom-call | tf_op jit(solution)/shard_map/attention_backward/pallas_call | solution.py:446
  116.5 4.0 %copy_bitcast_fusion = (bf16[64,32,256]{2,1,0:T(8,128)(2,1)}, bf16[64,32,256]{2,1,0:T(8,128)(2,1)}) fusion(bf16[32,64,256]{2,1,0:T(8,128)(2,1)} %bitcast.13, bf16[32,64,256]{2,1,0:T(8,128)(2,1)} %bitcast.12), kind=kLoop, calls=%fused_computation | loop fusion | bytes 4194304 | tf_op jit(solution)/shard_map/transpose | solution.py:665

commit v11 on v10

--- a/solution.py
+++ b/solution.py
@@ -72,7 +72,7 @@
 
 def fwd_kernel(x_in, u_in, pair_in, present, wq, wk, wv, wg, we, wl, wr,
                x_ref, p_out, o_ref, g_ref, a_ref, l_ref, r_ref, q_ref, v_ref, kt_ref, up_out, ut_out, pd_out, rc_ref, live_out,
-               wt, bias_s, st_s, p_buf, live_in, hx, ux, px, xbuf, lbuf, livet, jbuf, mine,
+               wt, bias_s, st_s, p_buf, live_in, u_buf, pair_buf, hx, ux, px, xbuf, lbuf, livet, jbuf, mine,
                xs, xr, us, ur, ps, pr, ls, lr, js, jr, own, p_sem):
     k = pl.program_id(0)
     d = lax.axis_index("dep")
@@ -101,6 +101,8 @@
 
     own_up = pltpu.make_async_copy(ux.at[d, pl.ds(0, 2)], up_out.at[d], own.at[0])
     own_pd = pltpu.make_async_copy(px.at[:, d], pd_out.at[d], own.at[1])
+    load_up = pltpu.make_async_copy(u_in, u_buf, own.at[3])
+    load_pd = pltpu.make_async_copy(pair_in, pair_buf, own.at[4])
     later_up = pltpu.make_async_copy(ux.at[:, pl.ds(2, 2)], ut_out, own.at[2])
 
     half = lax.rem(k, 2)
@@ -116,6 +118,8 @@
     @pl.when(k == 0)
     def _():
         hail([(dep_at(n), r) for n in range(1, 8)] + [(d, res_at(n)) for n in range(1, 16)])
+        load_pd.start()
+        load_up.start()
         hx[...] = jnp.transpose(x_in[...], (1, 0, 2)).reshape(hx.shape)
         flat = jnp.concatenate([present[...].astype(f32), jnp.zeros((CW, 64), f32)], axis=1)
         held = jnp.concatenate([flat, jnp.zeros((96, 128), f32)], axis=0).T[:64].astype(bf16)
@@ -130,8 +134,10 @@
             xbuf[c, d] = hx[d, c]
         for n, w in enumerate((wq, wv, wg, we)):
             wt[n] = w[...].T
-        px[...] = jnp.transpose(pair_in[...], (1, 0, 2)).reshape(px.shape)
-        ux[...] = jnp.transpose(u_in[...], (1, 0, 2)).reshape(ux.shape)
+        load_pd.wait()
+        px[...] = jnp.transpose(pair_buf[...], (1, 0, 2)).reshape(px.shape)
+        load_up.wait()
+        ux[...] = jnp.transpose(u_buf[...], (1, 0, 2)).reshape(ux.shape)
         for n in range(1, 8):
             live_copy(n).wait_recv()
         live = lbuf[...].reshape(N, 128).astype(f32)
@@ -280,11 +286,13 @@
             row_copy(n).wait_send()
 
 
-def bwd_kernel(x_ref, ua_ref, ub_ref, at_ref, lg_ref, rg_ref, p_in, o_ref, g_ref, q_ref, v_ref, kt_ref, wq, wk, wv, wg, we, wl, wr,
-               out_g, out_i, p_buf, ds_s, acc_q, acc_v, acc_t, dt_s, sbuf, ss, rs, own, p_sem):
+def bwd_kernel(x_ref, ua_in, ub_in, at_in, lg_ref, rg_ref, p_in, o_ref, g_ref, q_ref, v_ref, kt_ref, wq, wk, wv, wg, we, wl, wr,
+               out_g, out_i, ua_ref, ub_ref, at_ref, p_buf, ds_s, acc_q, acc_v, acc_t, dt_s, sbuf, ss, rs, own, p_sem, in_sem):
     k = pl.program_id(0)
     d = lax.axis_index("dep")
     r = lax.axis_index("res")
+    loads = [pltpu.make_async_copy(a, b, in_sem.at[n]) for n, (a, b) in
+             enumerate(((at_in, at_ref), (ua_in, ua_ref), (ub_in, ub_ref)))]
     outs = (out_g, out_i)
 
     def dep_at(n):
@@ -310,11 +318,15 @@
 
     @pl.when(k == 0)
     def _():
+        hail([(dep_at(n), r) for n in range(1, 8)])
+        for load in loads:
+            load.start()
         p_copy(0).start()
         p_copy(1).start()
-        hail([(dep_at(n), r) for n in range(1, 8)])
         wlt, wrt = wl[...].T, wr[...].T
         gather_all(7)
+        for load in loads:
+            load.wait()
         for c in range(4):
             yhat, yinv = norm(at_ref[c].astype(f32), 0)
             dy = mm(wlt, lg_ref[c]) + mm(wrt, rg_ref[c])
@@ -424,13 +436,13 @@
     return pl.pallas_call(
         fwd_kernel,
         grid=(4,),
-        in_specs=[whole((64, 32, F))] * 2 + [whole((32, 64, CZ)), whole((CW, 64))] + [whole((F, F))] * 5 + [whole((CW, F))] * 2,
+        in_specs=[whole((64, 32, F)), ANY, ANY, whole((CW, 64))] + [whole((F, F))] * 5 + [whole((CW, F))] * 2,
         out_specs=[COLS, ANY, percol((F, N)), percol((F, N)), percol((F, N)), percol((CW, N)),
                    percol((CW, N)), percol((N, F)), percol((N, F)), percol((F, N)), ANY, ANY, ANY, whole((8, 256)), whole((8, N))],
         out_shape=[sd((8, 4, 64, F), bf16), sd((4, H, N, N), bf16), sd((4, F, N), f32), sd((4, F, N), f32),
                    sd((4, F, N), bf16), sd((4, CW, N), bf16), sd((4, CW, N), bf16),
                    sd((4, N, F), bf16), sd((4, N, F), bf16), sd((4, F, N), bf16), sd((8, 2, 64, F), bf16), sd((8, 2, 64, F), bf16), sd((8, 2, 4, CW, CZ), bf16), sd((8, 256), f32), sd((8, N), f32)],
-        scratch_shapes=[V((4, F, F), bf16), V((N, 128), bf16), V((2, N, N), f32), V((2, H, N, N), bf16), V((64, 128), bf16), V((8, 4, 64, F), bf16), V((8, 4, 64, F), bf16), V((2, 8, 4, CW, CZ), bf16), V((4, 8, 64, F), bf16),
+        scratch_shapes=[V((4, F, F), bf16), V((N, 128), bf16), V((2, N, N), f32), V((2, H, N, N), bf16), V((64, 128), bf16), V((64, 32, F), bf16), V((32, 64, CZ), bf16), V((8, 4, 64, F), bf16), V((8, 4, 64, F), bf16), V((2, 8, 4, CW, CZ), bf16), V((4, 8, 64, F), bf16),
                         V((8, 64, 128), bf16), V((128, N), f32), V((16, 8, N), f32), V((8, N), f32),
                         dma((4, 8)), dma((4, 8)), dma((4, 8)), dma((4, 8))] + [dma((8,))] * 4 + [dma((16,))] * 2 + [dma((8,)), dma((2, 8))],
         compiler_params=pltpu.CompilerParams(vmem_limit_bytes=60 * 1024 * 1024, collective_id=2, has_side_effects=True,
@@ -446,12 +458,12 @@
     return pl.pallas_call(
         bwd_kernel,
         grid=(4,),
-        in_specs=[COLS, whole((8, 2, 64, F)), whole((8, 2, 64, F)), whole((4, F, N)), whole((4, CW, N)), whole((4, CW, N)), ANY, percol((F, N)),
+        in_specs=[COLS, ANY, ANY, ANY, whole((4, CW, N)), whole((4, CW, N)), ANY, percol((F, N)),
                   percol((F, N)), percol((N, F)), percol((N, F)), percol((F, N))] + [whole((F, F))] * 5 + [whole((CW, F))] * 2,
         out_specs=[ANY, ANY],
         out_shape=[sd((8, 4, 64, F), bf16)] * 2,
-        scratch_shapes=[V((2, H, N, N), bf16), V((H, N, N), bf16), V((F, N), f32), V((F, N), f32), V((N, F), f32), V((4, F, N), bf16), V((2, 4, 8, 64, F), bf16),
-                        dma((2, 4, 8)), dma((2, 4, 8)), dma((2, 4)), dma((2,))],
+        scratch_shapes=[V((8, 2, 64, F), bf16), V((8, 2, 64, F), bf16), V((4, F, N), bf16), V((2, H, N, N), bf16), V((H, N, N), bf16), V((F, N), f32), V((F, N), f32), V((N, F), f32), V((4, F, N), bf16), V((2, 4, 8, 64, F), bf16),
+                        dma((2, 4, 8)), dma((2, 4, 8)), dma((2, 4)), dma((2,)), dma((3,))],
         compiler_params=pltpu.CompilerParams(vmem_limit_bytes=60 * 1024 * 1024, collective_id=3, has_side_effects=True,
                                              dimension_semantics=("arbitrary",)),
         name="attention_backward",

time: 121 us -> 121 us (level)
  no operation moved by 1% of the time
where the time goes in v11:
time: 121 us
  Pallas kernels  116 us (96%)
  local copies, waits for them, and re-layouts  4.03 us (3%)
    pallas_call x1, Pallas kernels, fwd(): pl.pallas_call(fwd_kernel, grid=(4,), in_specs=[whole((64, 32, F)), ANY,...  43 us
    pallas_call x1, Pallas kernels, opm(): pl.pallas_call(opm_kernel, in_specs=[vm] * 6 + [ANY], out_specs=[vm] * 3,...  39.4 us
    pallas_call x1, Pallas kernels, bwd(): pl.pallas_call(bwd_kernel, grid=(4,), in_specs=[COLS, ANY, ANY, ANY, whol...  33.6 us
    transpose x1, local copies, waits for them, and re-layouts, by_row(): return a.reshape(32, 64, F).transpose(1, 0, 2)  4.03 us

profile of v11, /device:TPU:0, one launch (start us, length us, event | category | flops | bytes accessed | tf_op | source)
XLA Modules:
  0.0 120.7 jit_solution(5958688888544915057)
XLA Ops:
  0.6 43.0 %attention_forward.1 = (bf16[8,4,64,256]{3,2,1,0:T(8,128)(2,1)}, bf16[4,8,512,512]{3,2,1,0:T(8,128)(2,1)}, f32[4,256,512]{2,1,0:T(8,128)}, f32[4,256,512]{2,1,0:...) custom-call(bf16[64,32,256]{2,1,0:T(8,128)(2,1)} %x_in.1, ...), custom_call_target="tpu_custom_call" | custom-call | tf_op jit(solution)/shard_map/attention_forward/pallas_call | solution.py:436
  43.6 39.4 %outer_product.1 = (bf16[4,32,512]{2,1,0:T(8,128)(2,1)}, bf16[4,32,512]{2,1,0:T(8,128)(2,1)}, bf16[8,2,64,256]{3,2,1,0:T(8,128)(2,1)}) custom-call(bf16[128,512]{1,0:T(8,128)(2,1)} %bitcast.15, bf16[128,512]{1,0:T(8,128)(2,1)} %bitcast.16, bf16[2048,128]{1,0:T(8,128)(2,1)} %bitcast.14, f32[8,256]{1,0:T(8,128)} %get-tuple-element.27.rc, ...), custom_call_target="tpu_custom_call" | custom-call | tf_op jit(solution)/shard_map/outer_product/pallas_call | solution.py:662
  83.0 33.6 %attention_backward.1 = (bf16[8,4,64,256]{3,2,1,0:T(8,128)(2,1)}, bf16[8,4,64,256]{3,2,1,0:T(8,128)(2,1)}) custom-call(bf16[8,4,64,256]{3,2,1,0:T(8,128)(2,1)} %get-tuple-element.22.x_ref, bf16[8,2,64,256]{3,2,1,0:T(8,128)(2,1)} %get-tuple-element.23.ua_in, bf16[8,2,64,256]{3,2,1,0:T(8,128)(2,1)} %get-tuple-element.30.ub_in, ...), custom_call_target="tpu_custom_call" | custom-call | tf_op jit(solution)/shard_map/attention_backward/pallas_call | solution.py:458
  116.6 4.0 %copy_bitcast_fusion = (bf16[64,32,256]{2,1,0:T(8,128)(2,1)}, bf16[64,32,256]{2,1,0:T(8,128)(2,1)}) fusion(bf16[32,64,256]{2,1,0:T(8,128)(2,1)} %bitcast.13, bf16[32,64,256]{2,1,0:T(8,128)(2,1)} %bitcast.12), kind=kLoop, calls=%fused_computation | loop fusion | bytes 4194304 | tf_op jit(solution)/shard_map/transpose | solution.py:677
